TPU v7x, 128 devices: a whole 4x4x4 slice. The times are simulated.
128 devices in a mesh: member: 4 (over z_lo, core), space: 32 (over y, z_hi, x).
Axes of the slice: x: 4, y: 4, z: 4 (z_hi: 2, z_lo: 2; z = z_hi * 2 + z_lo), core: 2. Of those that a mesh axis runs over, the one named last changes fastest.
Arguments:
- members: bfloat16 [64, 32, 512, 384], P('member', None, 'space'), may hold values from -6 to 6
- control: float32 [32, 512, 384], P(None, 'space'), may hold values from -6 to 6
- hybrid_weight: float32 [32], replicated, may hold values from 0.2 to 0.6
- member_weights: int32 [64], replicated, may hold values from 1 to 8
- source_device: int32 [512, 1], P('space'), may hold values from 0 to 31, as said below
- source_row: int32 [512], P('space'), may hold values from 0 to 15
- column_source: int32 [512, 768], P('space'), may hold values from 0 to 382, as said below
- column_code: int32 [512, 768], P('space'), may hold values from 0 to 16
Outputs:
- fine_increment: float32 [512, 32, 2, 768], P('space', 'member')
Inputs may be any that keep to these rules, and one draw needn't show every extreme that they name: `source_device`: among the 16 fine blocks of one device no space index is named more than 2 times, and in every draw some device's blocks name some index exactly 2 times. `column_source`: within 2 of (j - 1) // 2 for fine column j, clipped to the range.
All inputs are finite; a program needn't handle non-finite values.
Results may differ from a plain program's by a relative error of at most 0.0022.
Values sent between devices are 32-bit elements; how exact they have to be, the bound alone decides.
No kernel may reach another device: no remote copies, remote signals or barrier semaphores. Data moves between devices by JAX's collectives and lax.ppermute only.
A program may use at most 128 MiB of HBM per device.

v0:
```python
import jax
import jax.numpy as jnp
import numpy as np
from jax import lax
from jax.experimental import pallas as pl
from jax.experimental.pallas import tpu as pltpu
from jax.sharding import PartitionSpec as P

SCALE = 1.0 / 625.0
LANES = 128
PITCH = 24


def passed_along(x, axis, by):
    length = lax.axis_size(axis)
    pairs = [(i, i + by) for i in range(length) if 0 <= i + by < length]
    return lax.ppermute(x, axis, pairs)


def swapped(x, axis, bit):
    length = lax.axis_size(axis)
    return lax.ppermute(x, axis, [(i, i ^ bit) for i in range(length)])


def split_lanes(x):
    return [x[:, i : i + LANES] for i in range(0, x.shape[-1], LANES)]


def joined(parts):
    return jnp.concatenate(parts, axis=-1)


def side_sum(parts, lane):
    ahead = [pltpu.roll(p, 1, 1) for p in parts]
    behind = [pltpu.roll(p, LANES - 1, 1) for p in parts]
    out = []
    for i in range(len(parts)):
        left = jnp.where(lane == 0, ahead[i - 1] if i else 0.0, ahead[i])
        right = jnp.where(
            lane == LANES - 1, behind[i + 1] if i + 1 < len(parts) else 0.0, behind[i]
        )
        out.append(left + right)
    return out


def plus(a, b):
    return [p + q for p, q in zip(a, b)]


def times(a, b):
    return [p * q for p, q in zip(a, b)]


def scaled(factor, a):
    return [factor * p for p in a]


def widen(parts, lane):
    return plus(parts, side_sum(parts, lane))


def edges_kernel(members_ref, control_ref, top_ref, bottom_ref, scratch, top_out, bottom_out, sems):
    step = pl.program_id(0)
    steps = pl.num_programs(0)
    group = members_ref.shape[0]
    chans, rows = members_ref.shape[1:3]
    parts = scratch.shape[0]

    def copies(first, count, index):
        return [
            pltpu.make_async_copy(
                stage.at[pl.ds(first, count)], ref.at[pl.ds(first, count)], sems.at[side, index]
            )
            for side, (stage, ref) in enumerate(((top_out, top_ref), (bottom_out, bottom_ref)))
        ]

    def rows_out(wide, index):
        for part in range(parts):
            lanes = slice(part * LANES, (part + 1) * LANES)
            for chan in range(chans):
                scratch[part, chan * PITCH : chan * PITCH + rows] = wide[chan, :, lanes]
            for slot in range(2):
                for which, stage in ((slot, top_out), (rows - 2 + slot, bottom_out)):
                    stage[index, slot, :, lanes] = scratch[
                        part, pl.ds(which, chans, stride=PITCH), :
                    ]

    for one in range(group):
        rows_out(members_ref[one].astype(jnp.float32), step * group + one)
    for copy in copies(step * group, group, step):
        copy.start()

    @pl.when(step == steps - 1)
    def _():
        count = top_ref.shape[0] - 1
        rows_out(control_ref[...], count)
        for copy in copies(count, 1, count // group):
            copy.start()
        for index in range(count // group):
            for copy in copies(index * group, group, index):
                copy.wait()
        for copy in copies(count, 1, count // group):
            copy.wait()


def edge_rows(members, control, group):
    count, chans, rows, width = members.shape
    shape = (count + 1, 2, chans, width)
    out = jax.ShapeDtypeStruct(shape, jnp.float32)
    return pl.pallas_call(
        edges_kernel,
        grid=(count // group,),
        in_specs=[
            pl.BlockSpec((group, chans, rows, width), lambda i: (i, 0, 0, 0)),
            pl.BlockSpec((chans, rows, width), lambda i: (0, 0, 0)),
        ],
        out_specs=[pl.BlockSpec(memory_space=pl.ANY)] * 2,
        out_shape=[out, out],
        scratch_shapes=[
            pltpu.VMEM((width // LANES, chans * PITCH, LANES), jnp.float32),
            pltpu.VMEM(shape, jnp.float32),
            pltpu.VMEM(shape, jnp.float32),
            pltpu.SemaphoreType.DMA((2, count // group + 1)),
        ],
        name="edge_rows",
    )(members, control)


def column_operators(width):
    q = np.eye(width) + np.eye(width, k=1) + np.eye(width, k=-1)
    q2 = q @ q
    q3 = q2 @ q
    eye = np.eye(width)
    return q2 @ q2 + 12 * q2 + 6 * eye, 4 * q3 + 12 * q, 6 * q2 + 4 * eye, 4 * q


def windowed(operator):
    first = operator[:256, :256]
    second = operator[128:, 128:].copy()
    second[:128, :128] = 0.0
    return first, second


def stacked(operators):
    first, second = zip(*[windowed(op) for op in operators])
    return np.stack([np.concatenate(first), np.concatenate(second)]).astype(jnp.bfloat16)


def own_kernel(
    place_ref, share_ref, members_ref, control_ref, blend_ref, operator_ref,
    keep_ref, give_ref, near_ref, control_near_ref,
    total, still, field, first, second, mixed, scratch,
):
    step = pl.program_id(0)
    chans, rows, width = members_ref.shape[1:]
    parts = width // LANES
    count = pl.num_programs(0) - 2

    def lanes(part):
        return slice(part * LANES, (part + 1) * LANES)

    @pl.when(step == 0)
    def _():
        field[...] = jnp.zeros(field.shape, jnp.float32)

    @pl.when(step < count)
    def _():
        def fill(chan, carry):
            for part in range(parts):
                state = members_ref[0, chan, :, lanes(part)].astype(jnp.float32)
                field[part, chan, 8 : 8 + rows] = state * control_ref[chan, :, lanes(part)]
                scratch[part, pl.ds(pl.multiple_of(chan * PITCH, 8), rows), :] = state
            return carry

        lax.fori_loop(0, chans, fill, 0, unroll=4)
        for place, row in enumerate((0, 1, 2, 3, rows - 4, rows - 3, rows - 2, rows - 1)):
            for part in range(parts):
                near_ref[0, place, :, lanes(part)] = scratch[
                    part, pl.ds(row, chans, stride=PITCH), :
                ].astype(jnp.bfloat16)

    @pl.when(step >= count)
    def _():
        def fill(chan, carry):
            for part in range(parts):
                block = control_ref[chan, :, lanes(part)]
                rough = block.astype(jnp.bfloat16).astype(jnp.float32)
                field[part, chan, 8 : 8 + rows] = jnp.where(step == count, rough, block - rough)
                scratch[part, pl.ds(pl.multiple_of(chan * PITCH, 8), rows), :] = block
            return carry

        lax.fori_loop(0, chans, fill, 0, unroll=4)

    @pl.when(step == count)
    def _():
        for place, row in enumerate((0, 1, 2, 3, rows - 4, rows - 3, rows - 2, rows - 1)):
            for part in range(parts):
                control_near_ref[place, :, lanes(part)] = scratch[
                    part, pl.ds(row, chans, stride=PITCH), :
                ]

    @pl.when(place_ref[1] == 0)
    def _():
        def image(chan, carry):
            for part in range(parts):
                for row in range(3):
                    field[part, chan, 6 - row : 7 - row] = -field[part, chan, 8 + row : 9 + row]
            return carry

        lax.fori_loop(0, chans, image, 0, unroll=4)

    @pl.when(place_ref[1] == 2)
    def _():
        def image(chan, carry):
            for part in range(parts):
                for row in range(3):
                    field[part, chan, 9 + rows + row : 10 + rows + row] = -field[
                        part, chan, 7 + rows - row : 8 + rows - row
                    ]
            return carry

        lax.fori_loop(0, chans, image, 0, unroll=4)

    def at_distance(part, chan, distance):
        if distance == 0:
            return field[part, chan, 8 : 8 + rows]
        return (
            field[part, chan, 8 - distance : 8 - distance + rows]
            + field[part, chan, 8 + distance : 8 + distance + rows]
        )

    def gather(chan, carry):
        at = pl.ds(pl.multiple_of(chan * rows, rows), rows)
        for distance in range(4):
            base = distance * 2 * LANES
            for part in range(parts):
                value = at_distance(part, chan, distance).astype(jnp.bfloat16)
                if part < 2:
                    first[at, base + part * LANES : base + (part + 1) * LANES] = value
                if part > 0:
                    second[at, base + (part - 1) * LANES : base + part * LANES] = value
        return carry

    lax.fori_loop(0, chans, gather, 0, unroll=4)
    mixed[0] = jnp.dot(first[...], operator_ref[0], preferred_element_type=jnp.float32)
    mixed[1] = jnp.dot(second[...], operator_ref[1], preferred_element_type=jnp.float32)

    def localized(chan):
        at = pl.ds(pl.multiple_of(chan * rows, rows), rows)
        low = [mixed[0, at, lanes(0)], mixed[0, at, lanes(1)]]
        high = [mixed[1, at, lanes(0)], mixed[1, at, lanes(1)]]
        found = [low[0], low[1] + high[0], high[1]]
        return [value + at_distance(part, chan, 4) for part, value in enumerate(found)]

    @pl.when(step < count)
    def _():
        share = share_ref[jnp.minimum(step, count - 1)]

        def one_chan(chan, carry):
            value = localized(chan)
            for part in range(parts):
                state = members_ref[0, chan, :, lanes(part)].astype(jnp.float32)
                term = (share * state) * value[part]
                before = jnp.where(step == 0, 0.0, total[chan, :, lanes(part)])
                total[chan, :, lanes(part)] = before + term
            return carry

        lax.fori_loop(0, chans, one_chan, 0, unroll=4)

    @pl.when(step == count)
    def _():
        def one_chan(chan, carry):
            value = localized(chan)
            for part in range(parts):
                still[chan, :, lanes(part)] = value[part]
            return carry

        lax.fori_loop(0, chans, one_chan, 0, unroll=4)

    @pl.when(step == count + 1)
    def _():
        def one_group(group, carry):
            slot = jnp.bitwise_xor(group, place_ref[0])
            blends = blend_ref[pl.ds(pl.multiple_of(group * 8, 8), 8), :]
            for inner in range(8):
                chan = group * 8 + inner
                blend = jnp.broadcast_to(blends[inner : inner + 1], (rows, LANES))
                value = localized(chan)
                for part in range(parts):
                    whole = value[part] + still[chan, :, lanes(part)]
                    total[chan, :, lanes(part)] = SCALE * (
                        (1.0 - blend) * total[chan, :, lanes(part)] + (0.25 * blend) * whole
                    )
            done = total[pl.ds(pl.multiple_of(group * 8, 8), 8)]

            @pl.when(jnp.bitwise_and(slot, 1) == 0)
            def _():
                keep_ref[slot // 2] = done

            @pl.when(jnp.bitwise_and(slot, 1) == 1)
            def _():
                give_ref[slot // 2] = done

            return carry

        lax.fori_loop(0, chans // 8, one_group, 0)


def own_part(place, share, members, control, blend):
    count, chans, rows, width = members.shape
    parts = width // LANES
    operators = jnp.asarray(stacked(column_operators(width)))
    half = (chans // 16, 8, rows, width)
    return pl.pallas_call(
        own_kernel,
        grid_spec=pltpu.PrefetchScalarGridSpec(
            num_scalar_prefetch=2,
            grid=(count + 2,),
            in_specs=[
                pl.BlockSpec(
                    (1, chans, rows, width),
                    lambda i, place, share: (jnp.minimum(i, count - 1), 0, 0, 0),
                ),
                pl.BlockSpec((chans, rows, width), lambda i, place, share: (0, 0, 0)),
                pl.BlockSpec((chans, LANES), lambda i, place, share: (0, 0)),
                pl.BlockSpec(operators.shape, lambda i, place, share: (0, 0, 0)),
            ],
            out_specs=[
                pl.BlockSpec(half, lambda i, place, share: (0, 0, 0, 0)),
                pl.BlockSpec(half, lambda i, place, share: (0, 0, 0, 0)),
                pl.BlockSpec(
                    (1, 8, chans, width),
                    lambda i, place, share: (jnp.minimum(i, count - 1), 0, 0, 0),
                ),
                pl.BlockSpec((8, chans, width), lambda i, place, share: (0, 0, 0)),
            ],
            scratch_shapes=[
                pltpu.VMEM((chans, rows, width), jnp.float32),
                pltpu.VMEM((chans, rows, width), jnp.float32),
                pltpu.VMEM((parts, chans, rows + 16, LANES), jnp.float32),
                pltpu.VMEM((chans * rows, operators.shape[1]), jnp.bfloat16),
                pltpu.VMEM((chans * rows, operators.shape[1]), jnp.bfloat16),
                pltpu.VMEM((2, chans * rows, 2 * LANES), jnp.float32),
                pltpu.VMEM((parts, chans * PITCH, LANES), jnp.float32),
            ],
        ),
        out_shape=[
            jax.ShapeDtypeStruct(half, jnp.float32),
            jax.ShapeDtypeStruct(half, jnp.float32),
            jax.ShapeDtypeStruct((count, 8, chans, width), jnp.bfloat16),
            jax.ShapeDtypeStruct((8, chans, width), jnp.float32),
        ],
        name="own_part",
    )(place, share, members, control, blend, operators)


def cross_kernel(
    place_ref, share_ref, low_ref, low_control_ref, high_ref, high_control_ref,
    near_ref, control_ref, blend_ref, pair_ref, single_ref,
    keep_ref, give_ref, sums, first, second, third, fourth, mixed, alone,
):
    step = pl.program_id(0)
    group = near_ref.shape[0]
    chans, width = near_ref.shape[2:]
    parts = width // LANES
    lane = lax.broadcasted_iota(jnp.int32, (8, LANES), 1)
    final = step == pl.num_programs(0) - 1
    span = group * chans
    sides = (
        (low_ref, low_control_ref, (1, 0), (0, 1, 2, 3)),
        (high_ref, high_control_ref, (0, 1), (7, 6, 5, 4)),
    )

    def lanes(part, base=0):
        return slice(base + part * LANES, base + (part + 1) * LANES)

    for side, (halo, halo_control, order, own) in enumerate(sides):
        for one in range(group):
            share = share_ref[step * group + one]
            at = slice(side * span + one * chans, side * span + (one + 1) * chans)
            below = slice(2 * span + at.start, 2 * span + at.stop)
            for part in range(parts):
                y1, y2 = [
                    (
                        halo[one, slot, :, lanes(part)]
                        * (share * halo_control[0, slot, :, lanes(part)])
                    ).astype(jnp.bfloat16)
                    for slot in order
                ]
                y3 = (
                    near_ref[one, own[2], :, lanes(part)].astype(jnp.float32)
                    * (share * control_ref[own[2], :, lanes(part)])
                ).astype(jnp.bfloat16)
                if part < 2:
                    first[at, lanes(part)] = y1
                    first[at, lanes(part, 2 * LANES)] = y2
                    third[at, lanes(part)] = y1
                    third[below, lanes(part)] = y3
                if part > 0:
                    second[at, lanes(part - 1)] = y1
                    second[at, lanes(part - 1, 2 * LANES)] = y2
                    fourth[at, lanes(part - 1)] = y1
                    fourth[below, lanes(part - 1)] = y3
    mixed[0] = jnp.dot(first[...], pair_ref[0], preferred_element_type=jnp.float32)
    mixed[1] = jnp.dot(second[...], pair_ref[1], preferred_element_type=jnp.float32)
    alone[0] = jnp.dot(third[...], single_ref[0], preferred_element_type=jnp.float32)
    alone[1] = jnp.dot(fourth[...], single_ref[1], preferred_element_type=jnp.float32)

    def piece(ref, at, part, base):
        if part == 0:
            return ref[0, at, lanes(0, base)]
        if part == parts - 1:
            return ref[1, at, lanes(1, base)]
        return ref[0, at, lanes(1, base)] + ref[1, at, lanes(0, base)]

    def per_chans(eight, carry):
        here = pl.ds(pl.multiple_of(eight * 8, 8), 8)
        for side, (halo, halo_control, order, own) in enumerate(sides):
            for part in range(parts):
                totals = [None] * 6
                c = [
                    halo_control[0, order[0], here, lanes(part)],
                    halo_control[0, order[1], here, lanes(part)],
                    control_ref[own[2], here, lanes(part)],
                    control_ref[own[3], here, lanes(part)],
                ]
                for one in range(group):
                    share = share_ref[step * group + one]
                    start = side * span + one * chans + eight * 8
                    at = pl.ds(pl.multiple_of(start, 8), 8)
                    below = pl.ds(pl.multiple_of(2 * span + start, 8), 8)
                    b1 = halo[one, order[0], here, lanes(part)]
                    b2 = halo[one, order[1], here, lanes(part)]
                    a = [
                        near_ref[one, row, here, lanes(part)].astype(jnp.float32) for row in own
                    ]
                    y = [x * (share * k) for x, k in zip((b1, b2, a[2], a[3]), c)]
                    terms = (
                        a[0] * piece(mixed, at, part, 0),
                        a[1] * piece(mixed, at, part, 2 * LANES),
                        a[2] * (piece(alone, at, part, 0) + y[1]),
                        a[3] * y[0],
                        b1 * (piece(alone, below, part, 0) + y[3]),
                        b2 * y[2],
                    )
                    totals = [t if s is None else s + t for s, t in zip(totals, terms)]
                for i, value in enumerate(totals):
                    place = side * 6 + i
                    before = jnp.where(step == 0, 0.0, sums[place, here, lanes(part)])
                    sums[place, here, lanes(part)] = before + value
        return carry

    lax.fori_loop(0, chans // 8, per_chans, 0)

    def exact(y1, y2, y3, y4):
        wide = scaled(4.0, widen(y1, lane))
        inner = plus(widen(plus(wide, scaled(6.0, y2)), lane), scaled(12.0, y1))
        top = plus(widen(inner, lane), scaled(4.0, y2))
        next_row = plus(
            widen(plus(scaled(1.5, wide), scaled(4.0, y2)), lane), scaled(4.0, y1)
        )
        return top, next_row, plus(wide, y2), y1, plus(scaled(4.0, widen(y3, lane)), y4), y3

    @pl.when(final)
    def _():
        def finish(eight, carry):
            at = pl.ds(pl.multiple_of(eight * 8, 8), 8)
            slot = jnp.bitwise_xor(eight, place_ref[0])
            blend = blend_ref[at, :]
            for side, (halo, halo_control, order, own) in enumerate(sides):
                found = exact(
                    split_lanes(halo_control[0, order[0], at, :]),
                    split_lanes(halo_control[0, order[1], at, :]),
                    split_lanes(control_ref[own[2], at, :]),
                    split_lanes(control_ref[own[3], at, :]),
                )
                for i, value in enumerate(found):
                    place = side * 6 + i
                    for part in range(parts):
                        sums[place, at, lanes(part)] = SCALE * (
                            (1.0 - blend) * sums[place, at, lanes(part)]
                            + (0.25 * blend) * value[part]
                        )

            @pl.when(jnp.bitwise_and(slot, 1) == 0)
            def _():
                keep_ref[slot // 2] = sums[:, at, :]

            @pl.when(jnp.bitwise_and(slot, 1) == 1)
            def _():
                give_ref[slot // 2] = sums[:, at, :]

            return carry

        lax.fori_loop(0, chans // 8, finish, 0, unroll=2)


def cross_part(place, share, low, high, near, control_near, blend, group):
    count, rows, chans, width = near.shape
    halo = pl.BlockSpec((group, 2, chans, width), lambda i: (i, 0, 0, 0))
    halo_control = pl.BlockSpec((1, 2, chans, width), lambda i: (count, 0, 0, 0))
    half = (chans // 16, 12, 8, width)
    _, p1, p2, p3 = column_operators(width)
    left, right = stacked([p1, p2]), stacked([p2, p3])
    pair = jnp.asarray(np.concatenate([left, right], axis=2))
    single = jnp.asarray(stacked([p3]))
    span = 2 * group * chans
    return pl.pallas_call(
        cross_kernel,
        grid=(count // group,),
        in_specs=[
            pl.BlockSpec(memory_space=pltpu.SMEM),
            pl.BlockSpec(memory_space=pltpu.SMEM),
            halo,
            halo_control,
            halo,
            halo_control,
            pl.BlockSpec((group, rows, chans, width), lambda i: (i, 0, 0, 0)),
            pl.BlockSpec((rows, chans, width), lambda i: (0, 0, 0)),
            pl.BlockSpec((chans, LANES), lambda i: (0, 0)),
            pl.BlockSpec(pair.shape, lambda i: (0, 0, 0)),
            pl.BlockSpec(single.shape, lambda i: (0, 0, 0)),
        ],
        out_specs=[pl.BlockSpec(half, lambda i: (0, 0, 0, 0))] * 2,
        out_shape=[jax.ShapeDtypeStruct(half, jnp.float32)] * 2,
        scratch_shapes=[
            pltpu.VMEM((12, chans, width), jnp.float32),
            pltpu.VMEM((span, 4 * LANES), jnp.bfloat16),
            pltpu.VMEM((span, 4 * LANES), jnp.bfloat16),
            pltpu.VMEM((2 * span, 2 * LANES), jnp.bfloat16),
            pltpu.VMEM((2 * span, 2 * LANES), jnp.bfloat16),
            pltpu.VMEM((2, span, 4 * LANES), jnp.float32),
            pltpu.VMEM((2, 2 * span, 2 * LANES), jnp.float32),
        ],
        name="cross_part",
    )(place, share, low, low, high, high, near, control_near, blend, pair, single)


def sent_kernel(own_ref, got_ref, last_ref, cross_ref, cross_got_ref, cross_last_ref, up_ref, down_ref, turned):
    chans, rows, width = last_ref.shape
    whole = own_ref[0] + got_ref[0] + last_ref[...]
    for part in range(width // LANES):
        lanes = slice(part * LANES, (part + 1) * LANES)
        for chan in range(chans):
            turned[chan * PITCH : chan * PITCH + 8] = whole[chan, :8, lanes]
        first = turned[pl.ds(0, chans, stride=PITCH), :]

        def crossed(i):
            return cross_ref[0, i, :, lanes] + cross_got_ref[0, i, :, lanes] + cross_last_ref[i, :, lanes]

        for i in range(2):
            up_ref[i, :, lanes] = crossed(4 + i)
            down_ref[i, :, lanes] = crossed(10 + i)
        up_ref[2, :, lanes] = first + crossed(0)


def sent_rows(own, got, last, cross, cross_got, cross_last):
    chans, rows, width = last.shape
    one = lambda x: pl.BlockSpec((1,) + x.shape[1:], lambda i: (0, 0, 0, 0))
    vmem = pl.BlockSpec(memory_space=pltpu.VMEM)
    return pl.pallas_call(
        sent_kernel,
        grid=(1,),
        in_specs=[one(own), one(got), vmem, one(cross), one(cross_got), vmem],
        out_specs=[vmem, vmem],
        out_shape=[
            jax.ShapeDtypeStruct((3, chans, width), jnp.float32),
            jax.ShapeDtypeStruct((2, chans, width), jnp.float32),
        ],
        scratch_shapes=[pltpu.VMEM((chans * PITCH, LANES), jnp.float32)],
        name="sent_rows",
    )(own, got, last, cross, cross_got, cross_last)


def answer_kernel(
    place_ref, asked_ref, own_ref, got_ref, last_ref, cross_ref, cross_got_ref, cross_last_ref,
    below_ref, above_ref, out_ref, turned, pairs,
):
    chans, rows, width = last_ref.shape
    parts = width // LANES
    capacity = out_ref.shape[0] // asked_ref.shape[0]
    keep_high = (place_ref[2] != 0).astype(jnp.float32)
    whole = own_ref[0] + got_ref[0] + last_ref[...]
    for part in range(parts):
        for chan in range(chans):
            turned[part, chan * PITCH : chan * PITCH + rows] = whole[
                chan, :, part * LANES : (part + 1) * LANES
            ]

    def crossed(i, lanes):
        return cross_ref[0, i, :, lanes] + cross_got_ref[0, i, :, lanes] + cross_last_ref[i, :, lanes]

    for part in range(parts):
        lanes = slice(part * LANES, (part + 1) * LANES)
        for row in range(rows + 1):
            if row < rows:
                value = turned[part, pl.ds(row, chans, stride=PITCH), :]
            else:
                value = keep_high * (above_ref[2, :, lanes] + crossed(10, lanes))
            if row < 4:
                value += crossed(row, lanes)
            if rows - 4 <= row < rows:
                value += crossed(6 + rows - 1 - row, lanes)
            if row < 2:
                value += below_ref[row, :, lanes]
            if rows - 2 <= row < rows:
                value += above_ref[rows - 1 - row, :, lanes]
            if row < rows:
                pairs[part, pl.ds(row * 2 * chans, chans, stride=2), :] = value
            if row > 0:
                pairs[part, pl.ds((row - 1) * 2 * chans + 1, chans, stride=2), :] = value

    def one(device, carry):
        for slot in range(capacity):
            row = asked_ref[device, 0, slot]
            at = pl.ds(pl.multiple_of(row * (2 * chans), 2 * chans), 2 * chans)
            for part in range(parts):
                out_ref[device * capacity + slot, :, part * LANES : (part + 1) * LANES] = pairs[
                    part, at, :
                ]
        return carry

    lax.fori_loop(0, asked_ref.shape[0], one, 0, unroll=4)


def answers(place, asked, capacity, own, got, last, cross, cross_got, cross_last, below, above):
    chans, rows, width = last.shape
    slots = asked.shape[0] * capacity
    smem = pl.BlockSpec(memory_space=pltpu.SMEM)
    vmem = pl.BlockSpec(memory_space=pltpu.VMEM)
    one = lambda x: pl.BlockSpec((1,) + x.shape[1:], lambda i: (0, 0, 0, 0))
    return pl.pallas_call(
        answer_kernel,
        grid=(1,),
        in_specs=[smem, smem, one(own), one(got), vmem, one(cross), one(cross_got), vmem, vmem, vmem],
        out_specs=vmem,
        out_shape=jax.ShapeDtypeStruct((slots, 2 * chans, width), jnp.float32),
        scratch_shapes=[
            pltpu.VMEM((width // LANES, chans * PITCH, LANES), jnp.float32),
            pltpu.VMEM((width // LANES, rows * 2 * chans, LANES), jnp.float32),
        ],
        name="answers",
    )(place, asked, own, got, last, cross, cross_got, cross_last, below, above)


def fine_kernel(slot_ref, arrived_ref, index_ref, weight_ref, out_ref):
    blocks = index_ref.shape[0]
    pairs, width = arrived_ref.shape[1:]
    fine = index_ref.shape[2]
    half = LANES // 2
    quarter = half // 2
    lane = lax.broadcasted_iota(jnp.int32, (8, LANES), 1)
    even = lax.broadcasted_iota(jnp.int32, (8, LANES), 0) % 2 == 0

    def one(block, carry):
        slot = slot_ref[block]
        windows = []
        for group in range(pairs // 8):
            parts = []
            for part in split_lanes(arrived_ref[slot, pl.ds(group * 8, 8), :]):
                other = jnp.where(even, pltpu.roll(part, 7, 0), pltpu.roll(part, 1, 0))
                parts.append(0.75 * part + 0.25 * other)
            turned = {
                shift: [pltpu.roll(p, shift, 1) for p in parts]
                for shift in (quarter, LANES - quarter)
            }
            found = []
            for chunk in range(fine // LANES):
                part, ahead = divmod(chunk * half - quarter, LANES)
                rolled = turned[LANES - ahead]
                if part < 0:
                    found.append(rolled[part + 1])
                elif part + 1 == len(parts):
                    found.append(rolled[part])
                else:
                    found.append(
                        jnp.where(lane < LANES - ahead, rolled[part], rolled[part + 1])
                    )
            windows.append(found)
        for chunk in range(fine // LANES):
            lanes = slice(chunk * LANES, (chunk + 1) * LANES)
            index = index_ref[block, :, lanes]
            weight = weight_ref[block, :, lanes]
            for group in range(pairs // 8):
                near = windows[group][chunk]
                left = jnp.take_along_axis(near, index, axis=1)
                right = jnp.take_along_axis(near, index + 1, axis=1)
                value = (1.0 - weight) * left + weight * right
                out_ref[block, group * 4 : (group + 1) * 4, :, lanes] = value.reshape(4, 2, LANES)
        return carry

    lax.fori_loop(0, blocks, one, 0, unroll=4)


def fine_part(slot, arrived, index, weight):
    blocks, _, fine = index.shape
    chans = arrived.shape[1] // 2
    smem = pl.BlockSpec(memory_space=pltpu.SMEM)
    vmem = pl.BlockSpec(memory_space=pltpu.VMEM)
    return pl.pallas_call(
        fine_kernel,
        in_specs=[smem, vmem, vmem, vmem],
        out_specs=vmem,
        out_shape=jax.ShapeDtypeStruct((blocks, chans, 2, fine), jnp.float32),
        name="fine_part",
    )(slot, arrived, index, weight)


def column_kernel(source_ref, code_ref, index_ref, weight_ref):
    blocks, fine = source_ref.shape
    column = lax.broadcasted_iota(jnp.int32, (1, fine), 1)
    first = (column // LANES) * (LANES // 2) - LANES // 4
    for block in range(blocks):
        shape = index_ref.shape[1:]
        index_ref[block] = jnp.broadcast_to(source_ref[block : block + 1] - first, shape)
        weight_ref[block] = jnp.broadcast_to(
            code_ref[block : block + 1].astype(jnp.float32) * (1.0 / 16.0), shape
        )


def columns(source, code):
    blocks, fine = source.shape
    return pl.pallas_call(
        column_kernel,
        out_shape=[
            jax.ShapeDtypeStruct((blocks, 8, fine), jnp.int32),
            jax.ShapeDtypeStruct((blocks, 8, fine), jnp.float32),
        ],
        name="columns",
    )(source, code)


def per_device(
    members,
    control,
    hybrid_weight,
    member_weights,
    source_device,
    source_row,
    column_source,
    column_code,
):
    member_count, chans, row_count, width = members.shape
    spaces = lax.axis_size("space")
    space_index = lax.axis_index("space")
    member_slot = lax.axis_index("member")

    top, bottom = edge_rows(members, control, 4)
    high = passed_along(top, "space", -1)
    low = passed_along(bottom, "space", 1)

    place = jnp.stack(
        [
            member_slot,
            jnp.where(space_index == 0, 0, jnp.where(space_index == spaces - 1, 2, 1)),
            (space_index < spaces - 1).astype(jnp.int32),
        ]
    ).astype(jnp.int32)
    weight_codes = member_weights.astype(jnp.float32)
    share = lax.dynamic_slice_in_dim(
        weight_codes, member_slot * member_count, member_count
    ) / jnp.sum(weight_codes)
    blend = jnp.broadcast_to(hybrid_weight[:, None], (chans, LANES))
    source_index = source_device[:, 0]
    capacity = max(2, 2 * row_count // spaces)
    chosen = (source_index[:, None] == jnp.arange(spaces, dtype=jnp.int32)[None, :]).astype(
        jnp.int32
    )
    earlier = jnp.cumsum(chosen, axis=0) - chosen
    rank_within = jnp.sum(earlier * chosen, axis=1)
    slot_index = source_index * capacity + rank_within
    spread = slot_index[None, :] - capacity * jnp.arange(spaces, dtype=jnp.int32)[:, None]
    lane = jnp.arange(LANES, dtype=jnp.int32)
    taken = (spread[:, None, :] == lane[None, :, None]) & (lane < capacity)[None, :, None]
    request = jnp.sum(jnp.where(taken, source_row[None, None, :], 0), axis=2)[:, None, :]
    index, weight = columns(column_source, column_code)

    own_keep, own_give, near, control_near = own_part(place, share, members, control, blend)
    own_give, request = lax.optimization_barrier((own_give, request))
    own_got = swapped(own_give, "member", 1)
    own_last = swapped(own_keep[1] + own_got[1], "member", 2)
    asked = lax.all_to_all(request, "space", split_axis=0, concat_axis=0, tiled=True)
    near, asked, own_last, index, weight, slot_index = lax.optimization_barrier(
        (near, asked, own_last, index, weight, slot_index)
    )

    keep, give = cross_part(place, share, low, high, near, control_near, blend, 4)
    got = swapped(give, "member", 1)
    last = swapped(keep[1] + got[1], "member", 2)
    up, down = sent_rows(own_keep, own_got, own_last, keep, got, last)
    above = passed_along(up, "space", -1)
    below = passed_along(down, "space", 1)

    outgoing = answers(
        place, asked, capacity, own_keep, own_got, own_last, keep, got, last, below, above
    )
    pair_rows = outgoing.shape[1]
    arrived = lax.all_to_all(
        outgoing.reshape(spaces, capacity * pair_rows, width),
        "space",
        split_axis=0,
        concat_axis=0,
        tiled=True,
    ).reshape(spaces * capacity, pair_rows, width)
    return fine_part(slot_index, arrived, index, weight)


def solution(mesh):
    placed = (
        P("member", None, "space", None),
        P(None, "space", None),
        P(),
        P(),
        P("space", None),
        P("space"),
        P("space", None),
        P("space", None),
    )
    return jax.shard_map(
        per_device,
        mesh=mesh,
        in_specs=placed,
        out_specs=P("space", "member", None, None),
        check_vma=False,
    )
```

profile of v0, /device:TPU:0, one launch (start us, length us, event | category | flops | bytes accessed | tf_op | source)
XLA Modules:
  0.0 147.7 jit_solution(17162231689223192242)
XLA Ops:
  0.0 0.0 copy-start.13
  0.0 0.0 copy-start.9
  0.0 0.0 copy-start.12
  0.0 5.8 %edge_rows.1 = (f32[17,2,32,384]{3,2,1,0:T(8,128)}, f32[17,2,32,384]{3,2,1,0:T(8,128)}) custom-call(bf16[16,32,16,384]{3,2,1,0:T(8,128)(2,1)} %members_ref.3, f32[32,16,384]{2,1,0:T(8,128)} %control_ref.3), custom_call_target="tpu_custom_call" | custom-call | tf_op jit(solution)/shard_map/edge_rows/pallas_call | solution.py:110
  5.8 3.6 %collective-permute-start.2 = (f32[17,2,32,384]{3,2,1,0:T(8,128)}, f32[17,2,32,384]{3,2,1,0:T(8,128)S(1)}, u32[]{:S(2)}, u32[]{:S(2)}) collective-permute-start(f32[17,2,32,384]{3,2,1,0:T(8,128)} %get-tuple-element.35), channel_id=1, source_target_pairs={{0,1},{1,2},{2,3},{3,4},{4,5},{5,6},{6,7},{7,8},{8,9},{9,10},{10,1... | collective-permute-start | bytes 5013512 | tf_op jit(solution)/shard_map/ppermute | solution.py:17
  9.4 1.3 collective-permute-start.3
  10.7 0.0 copy-done.13
  10.7 0.6 convert_reduce_fusion
  11.4 0.0 copy-done.9
  11.4 0.1 fusion.3
  11.4 0.6 pad_add_fusion.place_ref
  12.1 1.3 dynamic-slice_divide_fusion.share_ref
  13.4 0.0 copy-done.12
  13.4 0.7 broadcast_in_dim.12.blend_ref
  14.1 0.0 copy-start.11
  14.1 34.9 %own_part.1 = (f32[2,8,16,384]{3,2,1,0:T(8,128)}, f32[2,8,16,384]{3,2,1,0:T(8,128)}, bf16[16,8,32,384]{3,2,1,0:T(8,128)(2,1)}, f32[8,32,384]{2,1,0:T(8,128)}) custom-call(s32[3]{0:T(128)} %pad_add_fusion.place_ref, f32[16]{0:T(128)} %dynamic-slice_divide_fusion.share_ref, bf16[16,32,16,384]{3,2,1,0:T(8,128)(2,1)} %members_ref.3, f32[32,16,384]{2,1,0:T(8,128)} %control_ref.3, ...), custom_call_target="tpu_custom_call" | custom-call | tf_op jit(solution)/shard_map/own_part/pallas_call | solution.py:314
  49.0 0.2 select_reduce_fusion.1
  49.2 0.0 copy-start.10
  49.2 0.1 broadcast_subtract_fusion
  49.3 0.0 copy-done.11
  49.3 0.8 select_reduce_fusion
  50.1 0.0 copy-done.10
  50.1 0.0 collective-permute-start
  50.1 1.9 %collective-permute-done.got_ref = f32[2,8,16,384]{3,2,1,0:T(8,128)S(1)} collective-permute-done((f32[2,8,16,384]{3,2,1,0:T(8,128)}, f32[2,8,16,384]{3,2,1,0:T(8,128)S(1)}, u32[]{:S(2)}, u32[]{:S(2)}) %collective-permute-start) | collective-permute-done | bytes 393248 | tf_op jit(solution)/shard_map/ppermute | solution.py:22
  52.0 0.0 copy-start.2
  52.0 0.7 copy-done.2
  52.8 1.6 %fusion.1 = f32[8,16,384]{2,1,0:T(8,128)} fusion(f32[2,8,16,384]{3,2,1,0:T(8,128)S(1)} %collective-permute-done.got_ref, f32[2,8,16,384]{3,2,1,0:T(8,128)} %get-tuple-element.28.own_ref), kind=kLoop, calls=%fused_computation.4 | loop fusion | flops 49152 | bytes 589824 | tf_op jit(solution)/shard_map/add | solution.py:781
  54.4 1.9 %collective-permute-start.1 = (f32[8,16,384]{2,1,0:T(8,128)}, f32[8,16,384]{2,1,0:T(8,128)S(1)}, u32[]{:S(2)}, u32[]{:S(2)}) collective-permute-start(f32[8,16,384]{2,1,0:T(8,128)} %fusion.1), channel_id=1, source_target_pairs={{0,64},{32,96},{64,0},{96,32},{1,65},{33,97},{65,1},{97,33},{2,66}... | collective-permute-start | bytes 589832 | tf_op jit(solution)/shard_map/ppermute | solution.py:22
  56.3 11.0 %all-to-all-start = ((s32[32,1,128]{2,1,0:T(1,128)}), s32[32,1,128]{2,1,0:T(1,128)S(1)}, u32[]{:S(2)}, u32[]{:S(2)}) async-start(s32[32,1,128]{2,1,0:T(1,128)} %bitcast.14), calls=%async_computation | async-start | bytes 32768 | tf_op jit(solution)/shard_map/all_to_all | solution.py:782
  67.4 1.8 %columns.1 = (s32[16,8,768]{2,1,0:T(8,128)}, f32[16,8,768]{2,1,0:T(8,128)}) custom-call(s32[16,768]{1,0:T(8,128)} %source_ref.1, s32[16,768]{1,0:T(8,128)} %code_ref.1), custom_call_target="tpu_custom_call" | custom-call | tf_op jit(solution)/shard_map/columns/pallas_call | solution.py:723
  69.2 8.0 %all-to-all-done.asked_ref = s32[32,1,128]{2,1,0:T(1,128)S(1)} async-done(((s32[32,1,128]{2,1,0:T(1,128)}), s32[32,1,128]{2,1,0:T(1,128)S(1)}, u32[]{:S(2)}, u32[]{:S(2)}) %all-to-all-start) | async-done | bytes 16416 | tf_op jit(solution)/shard_map/all_to_all | solution.py:782
  77.2 0.0 copy-start.6
  77.2 0.0 collective-permute-done.1.last_ref
  77.2 0.0 copy-start.4
  77.2 0.0 collective-permute-done.2.low_ref.low_control_ref
  77.2 0.0 copy-start
  77.2 0.0 collective-permute-done.3.high_ref.high_control_ref
  77.2 0.0 copy-start.1
  77.2 1.2 copy-done
  78.5 0.5 copy-done.1
  78.9 8.6 %cross_part.1 = (f32[2,12,8,384]{3,2,1,0:T(8,128)}, f32[2,12,8,384]{3,2,1,0:T(8,128)}) custom-call(s32[3]{0:T(128)} %pad_add_fusion.place_ref, f32[16]{0:T(128)} %dynamic-slice_divide_fusion.share_ref, f32[17,2,32,384]{3,2,1,0:T(8,128)} %copy-done, f32[17,2,32,384]{3,2,1,0:T(8,128)} %copy-done, f32[17,2,32,384]{3,2,1,0:T(8,128)} %copy-done.1, ...), custom_call_target="tpu_custom_call" | custom-call | tf_op jit(solution)/shard_map/cross_part/pallas_call | solution.py:508
  87.5 0.0 copy-done.6
  87.5 0.0 copy-done.4
  87.5 0.1 collective-permute-start.4
  87.6 1.8 %collective-permute-done.4.cross_got_ref = f32[2,12,8,384]{3,2,1,0:T(8,128)S(1)} collective-permute-done((f32[2,12,8,384]{3,2,1,0:T(8,128)}, f32[2,12,8,384]{3,2,1,0:T(8,128)S(1)}, u32[]{:S(2)}, u32[]{:S(2)}) %collective-permute-start.4) | collective-permute-done | bytes 294944 | tf_op jit(solution)/shard_map/ppermute | solution.py:22
  89.4 0.0 copy-start.3
  89.4 1.0 fusion.2
  90.4 0.1 collective-permute-start.5
  90.5 5.9 %collective-permute-done.5.cross_last_ref = f32[12,8,384]{2,1,0:T(8,128)S(1)} collective-permute-done((f32[12,8,384]{2,1,0:T(8,128)S(1)}, f32[12,8,384]{2,1,0:T(8,128)S(1)}, u32[]{:S(2)}, u32[]{:S(2)}) %collective-permute-start.5) | collective-permute-done | bytes 147488 | tf_op jit(solution)/shard_map/ppermute | solution.py:22
  96.4 0.0 copy-done.3
  96.4 0.0 copy-start.5
  96.4 0.6 copy-done.5
  97.1 1.9 %sent_rows.1 = (f32[3,8,384]{2,1,0:T(8,128)}, f32[2,8,384]{2,1,0:T(8,128)}) custom-call(f32[2,8,16,384]{3,2,1,0:T(8,128)} %get-tuple-element.28.own_ref, f32[2,8,16,384]{3,2,1,0:T(8,128)} %copy-done.2, f32[8,16,384]{2,1,0:T(8,128)} %copy-done.4, f32[2,12,8,384]{3,2,1,0:T(8,128)} %get-tuple-element.39.cross_ref, f32[2,12,8,384]{3,2,1,0:T(8,128)} %copy-done.3, ...), custom_call_target="tpu_custom_call" | custom-call | tf_op jit(solution)/shard_map/sent_rows/pallas_call | solution.py:561
  99.0 1.3 collective-permute-start.7
  100.3 4.5 %collective-permute-start.6 = (f32[2,8,384]{2,1,0:T(8,128)}, f32[2,8,384]{2,1,0:T(8,128)S(1)}, u32[]{:S(2)}, u32[]{:S(2)}) collective-permute-start(f32[2,8,384]{2,1,0:T(8,128)} %get-tuple-element.41), channel_id=1, source_target_pairs={{0,1},{1,2},{2,3},{3,4},{4,5},{5,6},{6,7},{7,8},{8,9},{9,10},{10,1... | collective-permute-start | bytes 73736 | tf_op jit(solution)/shard_map/ppermute | solution.py:17
  104.8 1.7 %collective-permute-done.6.below_ref = f32[2,8,384]{2,1,0:T(8,128)S(1)} collective-permute-done((f32[2,8,384]{2,1,0:T(8,128)}, f32[2,8,384]{2,1,0:T(8,128)S(1)}, u32[]{:S(2)}, u32[]{:S(2)}) %collective-permute-start.6) | collective-permute-done | bytes 24608 | tf_op jit(solution)/shard_map/ppermute | solution.py:17
  106.5 0.0 copy-start.8
  106.6 0.0 collective-permute-done.7.above_ref
  106.6 0.6 copy-done.8
  107.2 0.0 copy-start.7
  107.2 0.6 copy-done.7
  107.8 2.7 %answers.1 = f32[64,16,384]{2,1,0:T(8,128)} custom-call(s32[3]{0:T(128)} %pad_add_fusion.place_ref, s32[32,1,128]{2,1,0:T(1,128)} %copy-done.6, f32[2,8,16,384]{3,2,1,0:T(8,128)} %get-tuple-element.28.own_ref, f32[2,8,16,384]{3,2,1,0:T(8,128)} %copy-done.2, f32[8,16,384]{2,1,0:T(8,128)} %copy-done.4, f32[2,12,8,384]{3,2,1,0:T(8,128)} %get-tuple-element.39.cross_ref, ...), custom_call_target="tpu_custom_call" | custom-call | tf_op jit(solution)/shard_map/answers/pallas_call | solution.py:632
  110.5 32.8 %all_to_all.10 = f32[32,32,384]{2,1,0:T(8,128)} all-to-all(f32[32,32,384]{2,1,0:T(8,128)} %bitcast.12), channel_id=1, replica_groups=mesh['member'=4,'space'=32] {'space'}, dimensions={0} | all-to-all | bytes 3145728 | tf_op jit(solution)/shard_map/all_to_all | solution.py:798
  143.3 4.5 %fine_part.1 = f32[16,8,2,768]{3,2,1,0:T(2,128)} custom-call(s32[16]{0:T(128)} %copy-done.10, f32[64,16,384]{2,1,0:T(8,128)} %bitcast.13, s32[16,8,768]{2,1,0:T(8,128)} %get-tuple-element.43.index_ref, f32[16,8,768]{2,1,0:T(8,128)} %get-tuple-element.44.weight_ref), custom_call_target="tpu_custom_call" | custom-call | tf_op jit(solution)/shard_map/fine_part/pallas_call | solution.py:700
  (5 shorter events, 0.1 us)
Async XLA Ops:
  0.0 10.7 %copy-start.13 = (s32[64]{0:T(128)S(1)}, s32[64]{0:T(128)}, u32[]{:S(2)}) copy-start(s32[64]{0:T(128)} %param.14) | copy-start | bytes 772
  0.0 11.4 %copy-start.9 = (s32[16,1]{0,1:T(1,128)S(1)}, s32[16,1]{0,1:T(1,128)}, u32[]{:S(2)}) copy-start(s32[16,1]{0,1:T(1,128)} %param.15) | copy-start | bytes 196
  0.0 13.4 %copy-start.12 = (f32[32]{0:T(128)S(1)}, f32[32]{0:T(128)}, u32[]{:S(2)}) copy-start(f32[32]{0:T(128)} %param.13) | copy-start | bytes 388
  5.8 71.4 %collective-permute-start.2 = (f32[17,2,32,384]{3,2,1,0:T(8,128)}, f32[17,2,32,384]{3,2,1,0:T(8,128)S(1)}, u32[]{:S(2)}, u32[]{:S(2)}) collective-permute-start(f32[17,2,32,384]{3,2,1,0:T(8,128)} %get-tuple-element.35), channel_id=1, source_target_pairs={{0,1},{1,2},{2,3},{3,4},{4,5},{5,6},{6,7},{7,8},{8,9},{9,10},{10,1... | collective-permute-start | bytes 5013512 | tf_op jit(solution)/shard_map/ppermute | solution.py:17
  9.4 67.8 %collective-permute-start.3 = (f32[17,2,32,384]{3,2,1,0:T(8,128)}, f32[17,2,32,384]{3,2,1,0:T(8,128)S(1)}, u32[]{:S(2)}, u32[]{:S(2)}) collective-permute-start(f32[17,2,32,384]{3,2,1,0:T(8,128)} %get-tuple-element.36), channel_id=1, source_target_pairs={{1,0},{2,1},{3,2},{4,3},{5,4},{6,5},{7,6},{8,7},{9,8},{10,9},{11,1... | collective-permute-start | bytes 5013512 | tf_op jit(solution)/shard_map/ppermute | solution.py:17
  14.1 35.2 %copy-start.11 = (s32[16]{0:T(128)S(1)}, s32[16]{0:T(128)}, u32[]{:S(2)}) copy-start(s32[16]{0:T(128)} %param.16) | copy-start | bytes 196
  49.2 0.9 copy-start.10
  50.1 1.9 %collective-permute-start = (f32[2,8,16,384]{3,2,1,0:T(8,128)}, f32[2,8,16,384]{3,2,1,0:T(8,128)S(1)}, u32[]{:S(2)}, u32[]{:S(2)}) collective-permute-start(f32[2,8,16,384]{3,2,1,0:T(8,128)} %get-tuple-element.29), channel_id=1, source_target_pairs={{0,32},{32,0},{64,96},{96,64},{1,33},{33,1},{65,97},{97,65},{2,34}... | collective-permute-start | bytes 1179656 | tf_op jit(solution)/shard_map/ppermute | solution.py:22
  52.0 0.7 copy-start.2
  54.4 22.8 %collective-permute-start.1 = (f32[8,16,384]{2,1,0:T(8,128)}, f32[8,16,384]{2,1,0:T(8,128)S(1)}, u32[]{:S(2)}, u32[]{:S(2)}) collective-permute-start(f32[8,16,384]{2,1,0:T(8,128)} %fusion.1), channel_id=1, source_target_pairs={{0,64},{32,96},{64,0},{96,32},{1,65},{33,97},{65,1},{97,33},{2,66}... | collective-permute-start | bytes 589832 | tf_op jit(solution)/shard_map/ppermute | solution.py:22
  56.3 20.9 %all-to-all-start = ((s32[32,1,128]{2,1,0:T(1,128)}), s32[32,1,128]{2,1,0:T(1,128)S(1)}, u32[]{:S(2)}, u32[]{:S(2)}) async-start(s32[32,1,128]{2,1,0:T(1,128)} %bitcast.14), calls=%async_computation | async-start | bytes 32768 | tf_op jit(solution)/shard_map/all_to_all | solution.py:782
  77.2 10.3 %copy-start.6 = (s32[32,1,128]{2,1,0:T(1,128)}, s32[32,1,128]{2,1,0:T(1,128)S(1)}, u32[]{:S(2)}) copy-start(s32[32,1,128]{2,1,0:T(1,128)S(1)} %all-to-all-done.asked_ref) | copy-start | bytes 49156
  77.2 10.3 %copy-start.4 = (f32[8,16,384]{2,1,0:T(8,128)}, f32[8,16,384]{2,1,0:T(8,128)S(1)}, u32[]{:S(2)}) copy-start(f32[8,16,384]{2,1,0:T(8,128)S(1)} %collective-permute-done.1.last_ref) | copy-start | bytes 589828
  77.2 1.3 copy-start
  77.2 1.7 %copy-start.1 = (f32[17,2,32,384]{3,2,1,0:T(8,128)}, f32[17,2,32,384]{3,2,1,0:T(8,128)S(1)}, u32[]{:S(2)}) copy-start(f32[17,2,32,384]{3,2,1,0:T(8,128)S(1)} %collective-permute-done.3.high_ref.high_control_ref) | copy-start | bytes 5013508
  87.5 1.9 %collective-permute-start.4 = (f32[2,12,8,384]{3,2,1,0:T(8,128)}, f32[2,12,8,384]{3,2,1,0:T(8,128)S(1)}, u32[]{:S(2)}, u32[]{:S(2)}) collective-permute-start(f32[2,12,8,384]{3,2,1,0:T(8,128)} %get-tuple-element.40), channel_id=1, source_target_pairs={{0,32},{32,0},{64,96},{96,64},{1,33},{33,1},{65,97},{97,65},{2,34}... | collective-permute-start | bytes 884744 | tf_op jit(solution)/shard_map/ppermute | solution.py:22
  89.4 7.0 %copy-start.3 = (f32[2,12,8,384]{3,2,1,0:T(8,128)}, f32[2,12,8,384]{3,2,1,0:T(8,128)S(1)}, u32[]{:S(2)}) copy-start(f32[2,12,8,384]{3,2,1,0:T(8,128)S(1)} %collective-permute-done.4.cross_got_ref) | copy-start | bytes 884740
  90.4 6.0 %collective-permute-start.5 = (f32[12,8,384]{2,1,0:T(8,128)S(1)}, f32[12,8,384]{2,1,0:T(8,128)S(1)}, u32[]{:S(2)}, u32[]{:S(2)}) collective-permute-start(f32[12,8,384]{2,1,0:T(8,128)S(1)} %fusion.2), channel_id=1, source_target_pairs={{0,64},{32,96},{64,0},{96,32},{1,65},{33,97},{65,1},{97,33},{2,66}... | collective-permute-start | bytes 442376 | tf_op jit(solution)/shard_map/ppermute | solution.py:22
  96.4 0.6 copy-start.5
  99.0 7.6 %collective-permute-start.7 = (f32[3,8,384]{2,1,0:T(8,128)}, f32[3,8,384]{2,1,0:T(8,128)S(1)}, u32[]{:S(2)}, u32[]{:S(2)}) collective-permute-start(f32[3,8,384]{2,1,0:T(8,128)} %get-tuple-element.42), channel_id=1, source_target_pairs={{1,0},{2,1},{3,2},{4,3},{5,4},{6,5},{7,6},{8,7},{9,8},{10,9},{11,1... | collective-permute-start | bytes 110600 | tf_op jit(solution)/shard_map/ppermute | solution.py:17
  100.3 6.3 %collective-permute-start.6 = (f32[2,8,384]{2,1,0:T(8,128)}, f32[2,8,384]{2,1,0:T(8,128)S(1)}, u32[]{:S(2)}, u32[]{:S(2)}) collective-permute-start(f32[2,8,384]{2,1,0:T(8,128)} %get-tuple-element.41), channel_id=1, source_target_pairs={{0,1},{1,2},{2,3},{3,4},{4,5},{5,6},{6,7},{7,8},{8,9},{9,10},{10,1... | collective-permute-start | bytes 73736 | tf_op jit(solution)/shard_map/ppermute | solution.py:17
  106.5 0.6 copy-start.8
  107.2 0.6 copy-start.7
where the time goes:
time: 148 us
  Pallas kernels  60.2 us (41%)
  blocking collectives  32.8 us (22%)
  starting transfers between devices  23.9 us (16%)
  waiting for transfers between devices  19.3 us (13%)
  other arithmetic  6.39 us (4%)
  local copies, waits for them, and re-layouts  4.99 us (3%)
    pallas_call x1, Pallas kernels, own_part(): pl.pallas_call(own_kernel, grid_spec=pltpu.PrefetchScalarGridSpec(num_sca...  34.9 us
    all_to_all x1, blocking collectives, per_device(): lax.all_to_all(outgoing.reshape(spaces, capacity * pair_rows, width), 'sp...  32.8 us
    all_to_all x1, starting transfers between devices, per_device(): lax.all_to_all(request, 'space', split_axis=0, concat_axis=0, tiled=True)  11 us
    ppermute x4, starting transfers between devices, passed_along(): return lax.ppermute(x, axis, pairs)  10.7 us
    ppermute x4, waiting for transfers between devices, swapped(): return lax.ppermute(x, axis, [(i, i ^ bit) for i in range(length)])  9.59 us
    pallas_call x1, Pallas kernels, cross_part(): pl.pallas_call(cross_kernel, grid=(count // group,), in_specs=[pl.BlockSp...  8.56 us
    all_to_all x1, waiting for transfers between devices, per_device(): lax.all_to_all(request, 'space', split_axis=0, concat_axis=0, tiled=True)  8.03 us
    pallas_call x1, Pallas kernels, edge_rows(): pl.pallas_call(edges_kernel, grid=(count // group,), in_specs=[pl.BlockSp...  5.78 us
  transfers between devices with their start and end apart: 9, of which 5 were waited for; matrix products, arithmetic and copies ran while one was open for 4% of the time, Pallas kernels for 25%

commit v1 on v0

--- a/solution.py
+++ b/solution.py
@@ -149,51 +149,55 @@
 def own_kernel(
     place_ref, share_ref, members_ref, control_ref, blend_ref, operator_ref,
     keep_ref, give_ref, near_ref, control_near_ref,
-    total, still, field, first, second, mixed, scratch,
+    total, scratch, *work,
 ):
     step = pl.program_id(0)
-    chans, rows, width = members_ref.shape[1:]
+    both, chans, rows, width = members_ref.shape
     parts = width // LANES
-    count = pl.num_programs(0) - 2
+    last = pl.num_programs(0) - 1
+    static = step == last
+    fields, firsts, seconds, mixes = [work[i * both : (i + 1) * both] for i in range(4)]
+    ends = (0, 1, 2, 3, rows - 4, rows - 3, rows - 2, rows - 1)
 
     def lanes(part):
         return slice(part * LANES, (part + 1) * LANES)
 
     @pl.when(step == 0)
     def _():
-        field[...] = jnp.zeros(field.shape, jnp.float32)
-
-    @pl.when(step < count)
+        total[...] = jnp.zeros(total.shape, jnp.float32)
+        for field in fields:
+            field[...] = jnp.zeros(field.shape, jnp.float32)
+
+    @pl.when(step < last)
     def _():
-        def fill(chan, carry):
-            for part in range(parts):
-                state = members_ref[0, chan, :, lanes(part)].astype(jnp.float32)
-                field[part, chan, 8 : 8 + rows] = state * control_ref[chan, :, lanes(part)]
-                scratch[part, pl.ds(pl.multiple_of(chan * PITCH, 8), rows), :] = state
-            return carry
-
-        lax.fori_loop(0, chans, fill, 0, unroll=4)
-        for place, row in enumerate((0, 1, 2, 3, rows - 4, rows - 3, rows - 2, rows - 1)):
-            for part in range(parts):
-                near_ref[0, place, :, lanes(part)] = scratch[
-                    part, pl.ds(row, chans, stride=PITCH), :
-                ].astype(jnp.bfloat16)
-
-    @pl.when(step >= count)
+        for which, field in enumerate(fields):
+
+            def fill(chan, carry):
+                for part in range(parts):
+                    state = members_ref[which, chan, :, lanes(part)].astype(jnp.float32)
+                    field[part, chan, 8 : 8 + rows] = state * control_ref[chan, :, lanes(part)]
+                    scratch[part, pl.ds(pl.multiple_of(chan * PITCH, 8), rows), :] = state
+                return carry
+
+            lax.fori_loop(0, chans, fill, 0, unroll=4)
+            for place, row in enumerate(ends):
+                for part in range(parts):
+                    near_ref[which, place, :, lanes(part)] = scratch[
+                        part, pl.ds(row, chans, stride=PITCH), :
+                    ].astype(jnp.bfloat16)
+
+    @pl.when(static)
     def _():
         def fill(chan, carry):
             for part in range(parts):
                 block = control_ref[chan, :, lanes(part)]
-                rough = block.astype(jnp.bfloat16).astype(jnp.float32)
-                field[part, chan, 8 : 8 + rows] = jnp.where(step == count, rough, block - rough)
+                for field in fields:
+                    field[part, chan, 8 : 8 + rows] = block
                 scratch[part, pl.ds(pl.multiple_of(chan * PITCH, 8), rows), :] = block
             return carry
 
         lax.fori_loop(0, chans, fill, 0, unroll=4)
-
-    @pl.when(step == count)
-    def _():
-        for place, row in enumerate((0, 1, 2, 3, rows - 4, rows - 3, rows - 2, rows - 1)):
+        for place, row in enumerate(ends):
             for part in range(parts):
                 control_near_ref[place, :, lanes(part)] = scratch[
                     part, pl.ds(row, chans, stride=PITCH), :
@@ -202,9 +206,12 @@
     @pl.when(place_ref[1] == 0)
     def _():
         def image(chan, carry):
-            for part in range(parts):
-                for row in range(3):
-                    field[part, chan, 6 - row : 7 - row] = -field[part, chan, 8 + row : 9 + row]
+            for field in fields:
+                for part in range(parts):
+                    for row in range(3):
+                        field[part, chan, 6 - row : 7 - row] = -field[
+                            part, chan, 8 + row : 9 + row
+                        ]
             return carry
 
         lax.fori_loop(0, chans, image, 0, unroll=4)
@@ -212,16 +219,17 @@
     @pl.when(place_ref[1] == 2)
     def _():
         def image(chan, carry):
-            for part in range(parts):
-                for row in range(3):
-                    field[part, chan, 9 + rows + row : 10 + rows + row] = -field[
-                        part, chan, 7 + rows - row : 8 + rows - row
-                    ]
+            for field in fields:
+                for part in range(parts):
+                    for row in range(3):
+                        field[part, chan, 9 + rows + row : 10 + rows + row] = -field[
+                            part, chan, 7 + rows - row : 8 + rows - row
+                        ]
             return carry
 
         lax.fori_loop(0, chans, image, 0, unroll=4)
 
-    def at_distance(part, chan, distance):
+    def at_distance(field, part, chan, distance):
         if distance == 0:
             return field[part, chan, 8 : 8 + rows]
         return (
@@ -229,69 +237,68 @@
             + field[part, chan, 8 + distance : 8 + distance + rows]
         )
 
-    def gather(chan, carry):
-        at = pl.ds(pl.multiple_of(chan * rows, rows), rows)
+    refine = jnp.where(static, 1.0, 0.0)
+
+    def gather(which, chan):
+        start = chan * rows
+        at = pl.ds(start if isinstance(chan, int) else pl.multiple_of(start, rows), rows)
         for distance in range(4):
             base = distance * 2 * LANES
             for part in range(parts):
-                value = at_distance(part, chan, distance).astype(jnp.bfloat16)
+                value = at_distance(fields[which], part, chan, distance)
+                if which:
+                    value -= refine * value.astype(jnp.bfloat16).astype(jnp.float32)
+                value = value.astype(jnp.bfloat16)
                 if part < 2:
-                    first[at, base + part * LANES : base + (part + 1) * LANES] = value
+                    firsts[which][at, base + part * LANES : base + (part + 1) * LANES] = value
                 if part > 0:
-                    second[at, base + (part - 1) * LANES : base + part * LANES] = value
-        return carry
-
-    lax.fori_loop(0, chans, gather, 0, unroll=4)
-    mixed[0] = jnp.dot(first[...], operator_ref[0], preferred_element_type=jnp.float32)
-    mixed[1] = jnp.dot(second[...], operator_ref[1], preferred_element_type=jnp.float32)
-
-    def localized(chan):
-        at = pl.ds(pl.multiple_of(chan * rows, rows), rows)
+                    seconds[which][at, base + (part - 1) * LANES : base + part * LANES] = value
+
+    def multiply(which):
+        for window, ref in enumerate((firsts[which], seconds[which])):
+            mixes[which][window] = jnp.dot(
+                ref[...], operator_ref[window], preferred_element_type=jnp.float32
+            )
+
+    def collect(which, chan):
+        at = pl.ds(chan * rows, rows)
+        mixed = mixes[which]
         low = [mixed[0, at, lanes(0)], mixed[0, at, lanes(1)]]
         high = [mixed[1, at, lanes(0)], mixed[1, at, lanes(1)]]
         found = [low[0], low[1] + high[0], high[1]]
-        return [value + at_distance(part, chan, 4) for part, value in enumerate(found)]
-
-    @pl.when(step < count)
-    def _():
-        share = share_ref[jnp.minimum(step, count - 1)]
-
-        def one_chan(chan, carry):
-            value = localized(chan)
-            for part in range(parts):
-                state = members_ref[0, chan, :, lanes(part)].astype(jnp.float32)
-                term = (share * state) * value[part]
-                before = jnp.where(step == 0, 0.0, total[chan, :, lanes(part)])
-                total[chan, :, lanes(part)] = before + term
-            return carry
-
-        lax.fori_loop(0, chans, one_chan, 0, unroll=4)
-
-    @pl.when(step == count)
-    def _():
-        def one_chan(chan, carry):
-            value = localized(chan)
-            for part in range(parts):
-                still[chan, :, lanes(part)] = value[part]
-            return carry
-
-        lax.fori_loop(0, chans, one_chan, 0, unroll=4)
-
-    @pl.when(step == count + 1)
+        blend = blend_ref[chan : chan + 1, :]
+        share = share_ref[jnp.minimum(step, last - 1) * both + which]
+        factor = jnp.where(static, 0.25 * blend, share)
+        for part in range(parts):
+            far = at_distance(fields[which], part, chan, 4)
+            value = found[part] + (far if which == 0 else (1.0 - refine) * far)
+            state = members_ref[which, chan, :, lanes(part)].astype(jnp.float32)
+            state = jnp.where(static, 1.0, state)
+            before = total[chan, :, lanes(part)]
+            if which == 0:
+                before = jnp.where(static, 1.0 - blend, 1.0) * before
+            total[chan, :, lanes(part)] = before + (factor * state) * value
+
+    def gather_four(group, carry):
+        for inner in range(4):
+            gather(0, group * 4 + inner)
+        return carry
+
+    lax.fori_loop(0, chans // 4, gather_four, 0)
+    multiply(0)
+    for chan in range(chans):
+        gather(1, chan)
+    multiply(1)
+    for chan in range(chans):
+        collect(0, chan)
+    for chan in range(chans):
+        collect(1, chan)
+
+    @pl.when(static)
     def _():
         def one_group(group, carry):
             slot = jnp.bitwise_xor(group, place_ref[0])
-            blends = blend_ref[pl.ds(pl.multiple_of(group * 8, 8), 8), :]
-            for inner in range(8):
-                chan = group * 8 + inner
-                blend = jnp.broadcast_to(blends[inner : inner + 1], (rows, LANES))
-                value = localized(chan)
-                for part in range(parts):
-                    whole = value[part] + still[chan, :, lanes(part)]
-                    total[chan, :, lanes(part)] = SCALE * (
-                        (1.0 - blend) * total[chan, :, lanes(part)] + (0.25 * blend) * whole
-                    )
-            done = total[pl.ds(pl.multiple_of(group * 8, 8), 8)]
+            done = SCALE * total[pl.ds(pl.multiple_of(group * 8, 8), 8)]
 
             @pl.when(jnp.bitwise_and(slot, 1) == 0)
             def _():
@@ -309,17 +316,20 @@
 def own_part(place, share, members, control, blend):
     count, chans, rows, width = members.shape
     parts = width // LANES
+    both = 2
+    steps = count // both
     operators = jnp.asarray(stacked(column_operators(width)))
+    depth = operators.shape[1]
     half = (chans // 16, 8, rows, width)
     return pl.pallas_call(
         own_kernel,
         grid_spec=pltpu.PrefetchScalarGridSpec(
             num_scalar_prefetch=2,
-            grid=(count + 2,),
+            grid=(steps + 1,),
             in_specs=[
                 pl.BlockSpec(
-                    (1, chans, rows, width),
-                    lambda i, place, share: (jnp.minimum(i, count - 1), 0, 0, 0),
+                    (both, chans, rows, width),
+                    lambda i, place, share: (jnp.minimum(i, steps - 1), 0, 0, 0),
                 ),
                 pl.BlockSpec((chans, rows, width), lambda i, place, share: (0, 0, 0)),
                 pl.BlockSpec((chans, LANES), lambda i, place, share: (0, 0)),
@@ -329,20 +339,18 @@
                 pl.BlockSpec(half, lambda i, place, share: (0, 0, 0, 0)),
                 pl.BlockSpec(half, lambda i, place, share: (0, 0, 0, 0)),
                 pl.BlockSpec(
-                    (1, 8, chans, width),
-                    lambda i, place, share: (jnp.minimum(i, count - 1), 0, 0, 0),
+                    (both, 8, chans, width),
+                    lambda i, place, share: (jnp.minimum(i, steps - 1), 0, 0, 0),
                 ),
                 pl.BlockSpec((8, chans, width), lambda i, place, share: (0, 0, 0)),
             ],
             scratch_shapes=[
                 pltpu.VMEM((chans, rows, width), jnp.float32),
-                pltpu.VMEM((chans, rows, width), jnp.float32),
-                pltpu.VMEM((parts, chans, rows + 16, LANES), jnp.float32),
-                pltpu.VMEM((chans * rows, operators.shape[1]), jnp.bfloat16),
-                pltpu.VMEM((chans * rows, operators.shape[1]), jnp.bfloat16),
-                pltpu.VMEM((2, chans * rows, 2 * LANES), jnp.float32),
                 pltpu.VMEM((parts, chans * PITCH, LANES), jnp.float32),
-            ],
+            ]
+            + [pltpu.VMEM((parts, chans, rows + 16, LANES), jnp.float32)] * both
+            + [pltpu.VMEM((chans * rows, depth), jnp.bfloat16)] * (2 * both)
+            + [pltpu.VMEM((2, chans * rows, 2 * LANES), jnp.float32)] * both,
         ),
         out_shape=[
             jax.ShapeDtypeStruct(half, jnp.float32),
@@ -745,7 +753,21 @@
     space_index = lax.axis_index("space")
     member_slot = lax.axis_index("member")
 
+    source_index = source_device[:, 0]
+    capacity = max(2, 2 * row_count // spaces)
+    chosen = (source_index[:, None] == jnp.arange(spaces, dtype=jnp.int32)[None, :]).astype(
+        jnp.int32
+    )
+    earlier = jnp.cumsum(chosen, axis=0) - chosen
+    rank_within = jnp.sum(earlier * chosen, axis=1)
+    slot_index = source_index * capacity + rank_within
+    spread = slot_index[None, :] - capacity * jnp.arange(spaces, dtype=jnp.int32)[:, None]
+    lane = jnp.arange(LANES, dtype=jnp.int32)
+    taken = (spread[:, None, :] == lane[None, :, None]) & (lane < capacity)[None, :, None]
+    request = jnp.sum(jnp.where(taken, source_row[None, None, :], 0), axis=2)[:, None, :]
+    asked = lax.all_to_all(request, "space", split_axis=0, concat_axis=0, tiled=True)
     top, bottom = edge_rows(members, control, 4)
+    top, bottom, asked = lax.optimization_barrier((top, bottom, asked))
     high = passed_along(top, "space", -1)
     low = passed_along(bottom, "space", 1)
 
@@ -761,27 +783,13 @@
         weight_codes, member_slot * member_count, member_count
     ) / jnp.sum(weight_codes)
     blend = jnp.broadcast_to(hybrid_weight[:, None], (chans, LANES))
-    source_index = source_device[:, 0]
-    capacity = max(2, 2 * row_count // spaces)
-    chosen = (source_index[:, None] == jnp.arange(spaces, dtype=jnp.int32)[None, :]).astype(
-        jnp.int32
-    )
-    earlier = jnp.cumsum(chosen, axis=0) - chosen
-    rank_within = jnp.sum(earlier * chosen, axis=1)
-    slot_index = source_index * capacity + rank_within
-    spread = slot_index[None, :] - capacity * jnp.arange(spaces, dtype=jnp.int32)[:, None]
-    lane = jnp.arange(LANES, dtype=jnp.int32)
-    taken = (spread[:, None, :] == lane[None, :, None]) & (lane < capacity)[None, :, None]
-    request = jnp.sum(jnp.where(taken, source_row[None, None, :], 0), axis=2)[:, None, :]
     index, weight = columns(column_source, column_code)
 
     own_keep, own_give, near, control_near = own_part(place, share, members, control, blend)
-    own_give, request = lax.optimization_barrier((own_give, request))
     own_got = swapped(own_give, "member", 1)
     own_last = swapped(own_keep[1] + own_got[1], "member", 2)
-    asked = lax.all_to_all(request, "space", split_axis=0, concat_axis=0, tiled=True)
-    near, asked, own_last, index, weight, slot_index = lax.optimization_barrier(
-        (near, asked, own_last, index, weight, slot_index)
+    near, own_last, index, weight, slot_index = lax.optimization_barrier(
+        (near, own_last, index, weight, slot_index)
     )
 
     keep, give = cross_part(place, share, low, high, near, control_near, blend, 4)

time: 148 us -> 148 us (level)
  Pallas kernels: 60.2 us -> 55.8 us
  blocking collectives: 32.8 us -> 36.3 us
  other arithmetic: 6.39 us -> 8.92 us
    pallas_call x1, Pallas kernels: 34.9 us -> 30.6 us  [own_part(): pl.pallas_call(own_kernel, grid_spec=pltpu.PrefetchScalarGridSpec(num_sca...]
    all_to_all x1, waiting for transfers between devices: 8.03 us -> 3.98 us  [per_device(): lax.all_to_all(request, 'space', split_axis=0, concat_axis=0, tiled=True)]
    all_to_all x1, blocking collectives: 32.8 us -> 36.3 us  [per_device(): lax.all_to_all(outgoing.reshape(spaces, capacity * pair_rows, width), 'sp...]
    ppermute x4, waiting for transfers between devices: 9.59 us -> 12.9 us  [swapped(): return lax.ppermute(x, axis, [(i, i ^ bit) for i in range(length)])]
    unnamed x28 -> x24, local copies, waits for them, and re-layouts: 4.32 us -> 4.36 us
  transfers between devices with their start and end apart: 9 -> 9, of which waited for: 5 -> 6; matrix products, arithmetic and copies ran while one was open for 4% -> 3% of each run, Pallas kernels for 25% -> 26%
where the time goes in v1:
time: 148 us; the launch traced here: 147 us
  Pallas kernels  55.8 us (38%)
  blocking collectives  36.3 us (25%)
  starting transfers between devices  22.7 us (15%)
  waiting for transfers between devices  18.6 us (13%)
  other arithmetic  8.92 us (6%)
  local copies, waits for them, and re-layouts  5.02 us (3%)
    all_to_all x1, blocking collectives, per_device(): lax.all_to_all(outgoing.reshape(spaces, capacity * pair_rows, width), 'sp...  36.3 us
    pallas_call x1, Pallas kernels, own_part(): pl.pallas_call(own_kernel, grid_spec=pltpu.PrefetchScalarGridSpec(num_sca...  30.6 us
    ppermute x4, waiting for transfers between devices, swapped(): return lax.ppermute(x, axis, [(i, i ^ bit) for i in range(length)])  12.9 us
    all_to_all x1, starting transfers between devices, per_device(): lax.all_to_all(request, 'space', split_axis=0, concat_axis=0, tiled=True)  10.7 us
    ppermute x4, starting transfers between devices, passed_along(): return lax.ppermute(x, axis, pairs)  9.69 us
    pallas_call x1, Pallas kernels, cross_part(): pl.pallas_call(cross_kernel, grid=(count // group,), in_specs=[pl.BlockSp...  8.55 us
    pallas_call x1, Pallas kernels, edge_rows(): pl.pallas_call(edges_kernel, grid=(count // group,), in_specs=[pl.BlockSp...  5.74 us
    pallas_call x1, Pallas kernels, fine_part(): pl.pallas_call(fine_kernel, in_specs=[smem, vmem, vmem, vmem], out_specs=...  4.48 us
  transfers between devices with their start and end apart: 9, of which 6 were waited for; matrix products, arithmetic and copies ran while one was open for 3% of the time, Pallas kernels for 26%

profile of v1, /device:TPU:0, one launch (start us, length us, event | category | flops | bytes accessed | tf_op | source)
XLA Modules:
  0.0 147.5 jit_solution(3625596525035913130)
XLA Ops:
  0.0 0.7 fusion.3
  0.8 0.8 select_reduce_fusion.1
  1.6 0.7 multiply_add_fusion.slot_ref
  2.3 0.0 copy-start.9
  2.3 0.1 broadcast_subtract_fusion
  2.3 1.4 select_reduce_fusion
  3.8 0.0 copy-done.9
  3.8 10.7 %all-to-all-start = ((s32[32,1,128]{2,1,0:T(1,128)}), s32[32,1,128]{2,1,0:T(1,128)S(1)}, u32[]{:S(2)}, u32[]{:S(2)}) async-start(s32[32,1,128]{2,1,0:T(1,128)} %bitcast.5), calls=%async_computation | async-start | bytes 32768 | tf_op jit(solution)/shard_map/all_to_all | solution.py:768
  14.6 0.0 copy-start.11
  14.6 0.0 copy-start.10
  14.6 5.7 %edge_rows.1 = (f32[17,2,32,384]{3,2,1,0:T(8,128)}, f32[17,2,32,384]{3,2,1,0:T(8,128)}) custom-call(bf16[16,32,16,384]{3,2,1,0:T(8,128)(2,1)} %members_ref.3, f32[32,16,384]{2,1,0:T(8,128)} %control_ref.3), custom_call_target="tpu_custom_call" | custom-call | tf_op jit(solution)/shard_map/edge_rows/pallas_call | solution.py:110
  20.3 4.0 %all-to-all-done.asked_ref = s32[32,1,128]{2,1,0:T(1,128)S(1)} async-done(((s32[32,1,128]{2,1,0:T(1,128)}), s32[32,1,128]{2,1,0:T(1,128)S(1)}, u32[]{:S(2)}, u32[]{:S(2)}) %all-to-all-start) | async-done | bytes 16416 | tf_op jit(solution)/shard_map/all_to_all | solution.py:768
  24.3 0.0 copy-start.6
  24.3 2.6 %collective-permute-start.2 = (f32[17,2,32,384]{3,2,1,0:T(8,128)}, f32[17,2,32,384]{3,2,1,0:T(8,128)S(1)}, u32[]{:S(2)}, u32[]{:S(2)}) collective-permute-start(f32[17,2,32,384]{3,2,1,0:T(8,128)} %get-tuple-element.35), channel_id=1, source_target_pairs={{0,1},{1,2},{2,3},{3,4},{4,5},{5,6},{6,7},{7,8},{8,9},{9,10},{10,1... | collective-permute-start | bytes 5013512 | tf_op jit(solution)/shard_map/ppermute | solution.py:17
  26.9 1.3 collective-permute-start.3
  28.2 0.0 copy-done.11
  28.2 0.6 pad_add_fusion.place_ref
  28.8 0.6 convert_reduce_fusion
  29.4 1.2 dynamic-slice_divide_fusion.share_ref
  30.7 0.0 copy-done.10
  30.7 0.7 broadcast_in_dim.16.blend_ref
  31.3 30.6 %own_part.1 = (f32[2,8,16,384]{3,2,1,0:T(8,128)}, f32[2,8,16,384]{3,2,1,0:T(8,128)}, bf16[16,8,32,384]{3,2,1,0:T(8,128)(2,1)}, f32[8,32,384]{2,1,0:T(8,128)}) custom-call(s32[3]{0:T(128)} %pad_add_fusion.place_ref, f32[16]{0:T(128)} %dynamic-slice_divide_fusion.share_ref, bf16[16,32,16,384]{3,2,1,0:T(8,128)(2,1)} %members_ref.3, f32[32,16,384]{2,1,0:T(8,128)} %control_ref.3, ...), custom_call_target="tpu_custom_call" | custom-call | tf_op jit(solution)/shard_map/own_part/pallas_call | solution.py:324
  61.9 0.0 copy-done.6
  62.0 0.0 collective-permute-start
  62.0 1.9 %collective-permute-done.got_ref = f32[2,8,16,384]{3,2,1,0:T(8,128)S(1)} collective-permute-done((f32[2,8,16,384]{3,2,1,0:T(8,128)}, f32[2,8,16,384]{3,2,1,0:T(8,128)S(1)}, u32[]{:S(2)}, u32[]{:S(2)}) %collective-permute-start) | collective-permute-done | bytes 393248 | tf_op jit(solution)/shard_map/ppermute | solution.py:22
  63.9 0.0 copy-start.2
  63.9 0.7 copy-done.2
  64.6 1.7 %fusion.1 = f32[8,16,384]{2,1,0:T(8,128)} fusion(f32[2,8,16,384]{3,2,1,0:T(8,128)S(1)} %collective-permute-done.got_ref, f32[2,8,16,384]{3,2,1,0:T(8,128)} %get-tuple-element.26.own_ref), kind=kLoop, calls=%fused_computation.4 | loop fusion | flops 49152 | bytes 589824 | tf_op jit(solution)/shard_map/add | solution.py:790
  66.3 1.0 collective-permute-start.1
  67.3 1.8 %columns.1 = (s32[16,8,768]{2,1,0:T(8,128)}, f32[16,8,768]{2,1,0:T(8,128)}) custom-call(s32[16,768]{1,0:T(8,128)} %source_ref.1, s32[16,768]{1,0:T(8,128)} %code_ref.1), custom_call_target="tpu_custom_call" | custom-call | tf_op jit(solution)/shard_map/columns/pallas_call | solution.py:731
  69.1 4.4 %collective-permute-done.1.last_ref = f32[8,16,384]{2,1,0:T(8,128)S(1)} collective-permute-done((f32[8,16,384]{2,1,0:T(8,128)}, f32[8,16,384]{2,1,0:T(8,128)S(1)}, u32[]{:S(2)}, u32[]{:S(2)}) %collective-permute-start.1) | collective-permute-done | bytes 196640 | tf_op jit(solution)/shard_map/ppermute | solution.py:22
  73.4 0.0 copy-start.4
  73.4 0.0 collective-permute-done.2.low_ref.low_control_ref
  73.4 0.0 copy-start
  73.5 0.0 collective-permute-done.3.high_ref.high_control_ref
  73.5 0.0 copy-start.1
  73.5 1.2 copy-done
  74.7 0.5 copy-done.1
  75.2 8.5 %cross_part.1 = (f32[2,12,8,384]{3,2,1,0:T(8,128)}, f32[2,12,8,384]{3,2,1,0:T(8,128)}) custom-call(s32[3]{0:T(128)} %pad_add_fusion.place_ref, f32[16]{0:T(128)} %dynamic-slice_divide_fusion.share_ref, f32[17,2,32,384]{3,2,1,0:T(8,128)} %copy-done, f32[17,2,32,384]{3,2,1,0:T(8,128)} %copy-done, f32[17,2,32,384]{3,2,1,0:T(8,128)} %copy-done.1, ...), custom_call_target="tpu_custom_call" | custom-call | tf_op jit(solution)/shard_map/cross_part/pallas_call | solution.py:516
  83.7 0.0 copy-done.4
  83.7 0.1 collective-permute-start.4
  83.8 1.8 %collective-permute-done.4.cross_got_ref = f32[2,12,8,384]{3,2,1,0:T(8,128)S(1)} collective-permute-done((f32[2,12,8,384]{3,2,1,0:T(8,128)}, f32[2,12,8,384]{3,2,1,0:T(8,128)S(1)}, u32[]{:S(2)}, u32[]{:S(2)}) %collective-permute-start.4) | collective-permute-done | bytes 294944 | tf_op jit(solution)/shard_map/ppermute | solution.py:22
  85.6 0.0 copy-start.3
  85.6 1.0 fusion.2
  86.7 1.1 collective-permute-start.5
  87.8 4.9 %collective-permute-done.5.cross_last_ref = f32[12,8,384]{2,1,0:T(8,128)S(1)} collective-permute-done((f32[12,8,384]{2,1,0:T(8,128)S(1)}, f32[12,8,384]{2,1,0:T(8,128)S(1)}, u32[]{:S(2)}, u32[]{:S(2)}) %collective-permute-start.5) | collective-permute-done | bytes 147488 | tf_op jit(solution)/shard_map/ppermute | solution.py:22
  92.6 0.0 copy-done.3
  92.6 0.0 copy-start.5
  92.6 0.7 copy-done.5
  93.3 1.9 %sent_rows.1 = (f32[3,8,384]{2,1,0:T(8,128)}, f32[2,8,384]{2,1,0:T(8,128)}) custom-call(f32[2,8,16,384]{3,2,1,0:T(8,128)} %get-tuple-element.26.own_ref, f32[2,8,16,384]{3,2,1,0:T(8,128)} %copy-done.2, f32[8,16,384]{2,1,0:T(8,128)} %copy-done.4, f32[2,12,8,384]{3,2,1,0:T(8,128)} %get-tuple-element.39.cross_ref, f32[2,12,8,384]{3,2,1,0:T(8,128)} %copy-done.3, ...), custom_call_target="tpu_custom_call" | custom-call | tf_op jit(solution)/shard_map/sent_rows/pallas_call | solution.py:569
  95.2 1.3 collective-permute-start.7
  96.5 4.5 %collective-permute-start.6 = (f32[2,8,384]{2,1,0:T(8,128)}, f32[2,8,384]{2,1,0:T(8,128)S(1)}, u32[]{:S(2)}, u32[]{:S(2)}) collective-permute-start(f32[2,8,384]{2,1,0:T(8,128)} %get-tuple-element.41), channel_id=1, source_target_pairs={{0,1},{1,2},{2,3},{3,4},{4,5},{5,6},{6,7},{7,8},{8,9},{9,10},{10,1... | collective-permute-start | bytes 73736 | tf_op jit(solution)/shard_map/ppermute | solution.py:17
  101.1 1.7 %collective-permute-done.6.below_ref = f32[2,8,384]{2,1,0:T(8,128)S(1)} collective-permute-done((f32[2,8,384]{2,1,0:T(8,128)}, f32[2,8,384]{2,1,0:T(8,128)S(1)}, u32[]{:S(2)}, u32[]{:S(2)}) %collective-permute-start.6) | collective-permute-done | bytes 24608 | tf_op jit(solution)/shard_map/ppermute | solution.py:17
  102.8 0.0 copy-start.8
  102.8 0.0 collective-permute-done.7.above_ref
  102.8 0.6 copy-done.8
  103.4 0.0 copy-start.7
  103.4 0.6 copy-done.7
  104.0 2.7 %answers.1 = f32[64,16,384]{2,1,0:T(8,128)} custom-call(s32[3]{0:T(128)} %pad_add_fusion.place_ref, s32[32,1,128]{2,1,0:T(1,128)} %copy-done.6, f32[2,8,16,384]{3,2,1,0:T(8,128)} %get-tuple-element.26.own_ref, f32[2,8,16,384]{3,2,1,0:T(8,128)} %copy-done.2, f32[8,16,384]{2,1,0:T(8,128)} %copy-done.4, f32[2,12,8,384]{3,2,1,0:T(8,128)} %get-tuple-element.39.cross_ref, ...), custom_call_target="tpu_custom_call" | custom-call | tf_op jit(solution)/shard_map/answers/pallas_call | solution.py:640
  106.7 36.3 %all_to_all.10 = f32[32,32,384]{2,1,0:T(8,128)} all-to-all(f32[32,32,384]{2,1,0:T(8,128)} %bitcast.12), channel_id=1, replica_groups=mesh['member'=4,'space'=32] {'space'}, dimensions={0} | all-to-all | bytes 3145728 | tf_op jit(solution)/shard_map/all_to_all | solution.py:806
  143.0 4.5 %fine_part.1 = f32[16,8,2,768]{3,2,1,0:T(2,128)} custom-call(s32[16]{0:T(128)} %copy-done.9, f32[64,16,384]{2,1,0:T(8,128)} %bitcast.13, s32[16,8,768]{2,1,0:T(8,128)} %get-tuple-element.43.index_ref, f32[16,8,768]{2,1,0:T(8,128)} %get-tuple-element.44.weight_ref), custom_call_target="tpu_custom_call" | custom-call | tf_op jit(solution)/shard_map/fine_part/pallas_call | solution.py:708
  (4 shorter events, 0.0 us)
Async XLA Ops:
  2.3 1.5 %copy-start.9 = (s32[16]{0:T(128)}, s32[16]{0:T(128)S(1)}, u32[]{:S(2)}) copy-start(s32[16]{0:T(128)S(1)} %multiply_add_fusion.slot_ref) | copy-start | bytes 196
  3.8 20.5 %all-to-all-start = ((s32[32,1,128]{2,1,0:T(1,128)}), s32[32,1,128]{2,1,0:T(1,128)S(1)}, u32[]{:S(2)}, u32[]{:S(2)}) async-start(s32[32,1,128]{2,1,0:T(1,128)} %bitcast.5), calls=%async_computation | async-start | bytes 32768 | tf_op jit(solution)/shard_map/all_to_all | solution.py:768
  14.6 13.6 %copy-start.11 = (s32[64]{0:T(128)S(1)}, s32[64]{0:T(128)}, u32[]{:S(2)}) copy-start(s32[64]{0:T(128)} %param.14) | copy-start | bytes 772
  14.6 16.1 %copy-start.10 = (f32[32]{0:T(128)S(1)}, f32[32]{0:T(128)}, u32[]{:S(2)}) copy-start(f32[32]{0:T(128)} %param.13) | copy-start | bytes 388
  24.3 37.6 %copy-start.6 = (s32[32,1,128]{2,1,0:T(1,128)}, s32[32,1,128]{2,1,0:T(1,128)S(1)}, u32[]{:S(2)}) copy-start(s32[32,1,128]{2,1,0:T(1,128)S(1)} %all-to-all-done.asked_ref) | copy-start | bytes 49156
  24.3 49.1 %collective-permute-start.2 = (f32[17,2,32,384]{3,2,1,0:T(8,128)}, f32[17,2,32,384]{3,2,1,0:T(8,128)S(1)}, u32[]{:S(2)}, u32[]{:S(2)}) collective-permute-start(f32[17,2,32,384]{3,2,1,0:T(8,128)} %get-tuple-element.35), channel_id=1, source_target_pairs={{0,1},{1,2},{2,3},{3,4},{4,5},{5,6},{6,7},{7,8},{8,9},{9,10},{10,1... | collective-permute-start | bytes 5013512 | tf_op jit(solution)/shard_map/ppermute | solution.py:17
  26.9 46.6 %collective-permute-start.3 = (f32[17,2,32,384]{3,2,1,0:T(8,128)}, f32[17,2,32,384]{3,2,1,0:T(8,128)S(1)}, u32[]{:S(2)}, u32[]{:S(2)}) collective-permute-start(f32[17,2,32,384]{3,2,1,0:T(8,128)} %get-tuple-element.36), channel_id=1, source_target_pairs={{1,0},{2,1},{3,2},{4,3},{5,4},{6,5},{7,6},{8,7},{9,8},{10,9},{11,1... | collective-permute-start | bytes 5013512 | tf_op jit(solution)/shard_map/ppermute | solution.py:17
  62.0 1.9 %collective-permute-start = (f32[2,8,16,384]{3,2,1,0:T(8,128)}, f32[2,8,16,384]{3,2,1,0:T(8,128)S(1)}, u32[]{:S(2)}, u32[]{:S(2)}) collective-permute-start(f32[2,8,16,384]{3,2,1,0:T(8,128)} %get-tuple-element.27), channel_id=1, source_target_pairs={{0,32},{32,0},{64,96},{96,64},{1,33},{33,1},{65,97},{97,65},{2,34}... | collective-permute-start | bytes 1179656 | tf_op jit(solution)/shard_map/ppermute | solution.py:22
  63.9 0.7 copy-start.2
  66.3 7.2 %collective-permute-start.1 = (f32[8,16,384]{2,1,0:T(8,128)}, f32[8,16,384]{2,1,0:T(8,128)S(1)}, u32[]{:S(2)}, u32[]{:S(2)}) collective-permute-start(f32[8,16,384]{2,1,0:T(8,128)} %fusion.1), channel_id=1, source_target_pairs={{0,64},{32,96},{64,0},{96,32},{1,65},{33,97},{65,1},{97,33},{2,66}... | collective-permute-start | bytes 589832 | tf_op jit(solution)/shard_map/ppermute | solution.py:22
  73.4 10.3 %copy-start.4 = (f32[8,16,384]{2,1,0:T(8,128)}, f32[8,16,384]{2,1,0:T(8,128)S(1)}, u32[]{:S(2)}) copy-start(f32[8,16,384]{2,1,0:T(8,128)S(1)} %collective-permute-done.1.last_ref) | copy-start | bytes 589828
  73.4 1.3 copy-start
  73.5 1.7 %copy-start.1 = (f32[17,2,32,384]{3,2,1,0:T(8,128)}, f32[17,2,32,384]{3,2,1,0:T(8,128)S(1)}, u32[]{:S(2)}) copy-start(f32[17,2,32,384]{3,2,1,0:T(8,128)S(1)} %collective-permute-done.3.high_ref.high_control_ref) | copy-start | bytes 5013508
  83.7 1.9 %collective-permute-start.4 = (f32[2,12,8,384]{3,2,1,0:T(8,128)}, f32[2,12,8,384]{3,2,1,0:T(8,128)S(1)}, u32[]{:S(2)}, u32[]{:S(2)}) collective-permute-start(f32[2,12,8,384]{3,2,1,0:T(8,128)} %get-tuple-element.40), channel_id=1, source_target_pairs={{0,32},{32,0},{64,96},{96,64},{1,33},{33,1},{65,97},{97,65},{2,34}... | collective-permute-start | bytes 884744 | tf_op jit(solution)/shard_map/ppermute | solution.py:22
  85.6 7.0 %copy-start.3 = (f32[2,12,8,384]{3,2,1,0:T(8,128)}, f32[2,12,8,384]{3,2,1,0:T(8,128)S(1)}, u32[]{:S(2)}) copy-start(f32[2,12,8,384]{3,2,1,0:T(8,128)S(1)} %collective-permute-done.4.cross_got_ref) | copy-start | bytes 884740
  86.7 6.0 %collective-permute-start.5 = (f32[12,8,384]{2,1,0:T(8,128)S(1)}, f32[12,8,384]{2,1,0:T(8,128)S(1)}, u32[]{:S(2)}, u32[]{:S(2)}) collective-permute-start(f32[12,8,384]{2,1,0:T(8,128)S(1)} %fusion.2), channel_id=1, source_target_pairs={{0,64},{32,96},{64,0},{96,32},{1,65},{33,97},{65,1},{97,33},{2,66}... | collective-permute-start | bytes 442376 | tf_op jit(solution)/shard_map/ppermute | solution.py:22
  92.6 0.7 copy-start.5
  95.2 7.6 %collective-permute-start.7 = (f32[3,8,384]{2,1,0:T(8,128)}, f32[3,8,384]{2,1,0:T(8,128)S(1)}, u32[]{:S(2)}, u32[]{:S(2)}) collective-permute-start(f32[3,8,384]{2,1,0:T(8,128)} %get-tuple-element.42), channel_id=1, source_target_pairs={{1,0},{2,1},{3,2},{4,3},{5,4},{6,5},{7,6},{8,7},{9,8},{10,9},{11,1... | collective-permute-start | bytes 110600 | tf_op jit(solution)/shard_map/ppermute | solution.py:17
  96.5 6.3 %collective-permute-start.6 = (f32[2,8,384]{2,1,0:T(8,128)}, f32[2,8,384]{2,1,0:T(8,128)S(1)}, u32[]{:S(2)}, u32[]{:S(2)}) collective-permute-start(f32[2,8,384]{2,1,0:T(8,128)} %get-tuple-element.41), channel_id=1, source_target_pairs={{0,1},{1,2},{2,3},{3,4},{4,5},{5,6},{6,7},{7,8},{8,9},{9,10},{10,1... | collective-permute-start | bytes 73736 | tf_op jit(solution)/shard_map/ppermute | solution.py:17
  102.8 0.6 copy-start.8
  103.4 0.6 copy-start.7

commit v2 on v1

--- a/solution.py
+++ b/solution.py
@@ -24,10 +24,6 @@
 
 def split_lanes(x):
     return [x[:, i : i + LANES] for i in range(0, x.shape[-1], LANES)]
-
-
-def joined(parts):
-    return jnp.concatenate(parts, axis=-1)
 
 
 def side_sum(parts, lane):
@@ -45,10 +41,6 @@
 
 def plus(a, b):
     return [p + q for p, q in zip(a, b)]
-
-
-def times(a, b):
-    return [p * q for p, q in zip(a, b)]
 
 
 def scaled(factor, a):
@@ -545,7 +537,7 @@
 
 
 def sent_kernel(own_ref, got_ref, last_ref, cross_ref, cross_got_ref, cross_last_ref, up_ref, down_ref, turned):
-    chans, rows, width = last_ref.shape
+    chans, _, width = last_ref.shape
     whole = own_ref[0] + got_ref[0] + last_ref[...]
     for part in range(width // LANES):
         lanes = slice(part * LANES, (part + 1) * LANES)
@@ -563,7 +555,7 @@
 
 
 def sent_rows(own, got, last, cross, cross_got, cross_last):
-    chans, rows, width = last.shape
+    chans, _, width = last.shape
     one = lambda x: pl.BlockSpec((1,) + x.shape[1:], lambda i: (0, 0, 0, 0))
     vmem = pl.BlockSpec(memory_space=pltpu.VMEM)
     return pl.pallas_call(
@@ -653,7 +645,7 @@
 
 def fine_kernel(slot_ref, arrived_ref, index_ref, weight_ref, out_ref):
     blocks = index_ref.shape[0]
-    pairs, width = arrived_ref.shape[1:]
+    pairs, _ = arrived_ref.shape[1:]
     fine = index_ref.shape[2]
     half = LANES // 2
     quarter = half // 2
@@ -753,6 +745,22 @@
     space_index = lax.axis_index("space")
     member_slot = lax.axis_index("member")
 
+    top, bottom = edge_rows(members, control, 4)
+    high = passed_along(top, "space", -1)
+    low = passed_along(bottom, "space", 1)
+
+    place = jnp.stack(
+        [
+            member_slot,
+            jnp.where(space_index == 0, 0, jnp.where(space_index == spaces - 1, 2, 1)),
+            (space_index < spaces - 1).astype(jnp.int32),
+        ]
+    ).astype(jnp.int32)
+    weight_codes = member_weights.astype(jnp.float32)
+    share = lax.dynamic_slice_in_dim(
+        weight_codes, member_slot * member_count, member_count
+    ) / jnp.sum(weight_codes)
+    blend = jnp.broadcast_to(hybrid_weight[:, None], (chans, LANES))
     source_index = source_device[:, 0]
     capacity = max(2, 2 * row_count // spaces)
     chosen = (source_index[:, None] == jnp.arange(spaces, dtype=jnp.int32)[None, :]).astype(
@@ -765,32 +773,14 @@
     lane = jnp.arange(LANES, dtype=jnp.int32)
     taken = (spread[:, None, :] == lane[None, :, None]) & (lane < capacity)[None, :, None]
     request = jnp.sum(jnp.where(taken, source_row[None, None, :], 0), axis=2)[:, None, :]
+    index, weight = columns(column_source, column_code)
+
+    own_keep, own_give, near, control_near = own_part(place, share, members, control, blend)
+    own_give, request = lax.optimization_barrier((own_give, request))
     asked = lax.all_to_all(request, "space", split_axis=0, concat_axis=0, tiled=True)
-    top, bottom = edge_rows(members, control, 4)
-    top, bottom, asked = lax.optimization_barrier((top, bottom, asked))
-    high = passed_along(top, "space", -1)
-    low = passed_along(bottom, "space", 1)
-
-    place = jnp.stack(
-        [
-            member_slot,
-            jnp.where(space_index == 0, 0, jnp.where(space_index == spaces - 1, 2, 1)),
-            (space_index < spaces - 1).astype(jnp.int32),
-        ]
-    ).astype(jnp.int32)
-    weight_codes = member_weights.astype(jnp.float32)
-    share = lax.dynamic_slice_in_dim(
-        weight_codes, member_slot * member_count, member_count
-    ) / jnp.sum(weight_codes)
-    blend = jnp.broadcast_to(hybrid_weight[:, None], (chans, LANES))
-    index, weight = columns(column_source, column_code)
-
-    own_keep, own_give, near, control_near = own_part(place, share, members, control, blend)
     own_got = swapped(own_give, "member", 1)
     own_last = swapped(own_keep[1] + own_got[1], "member", 2)
-    near, own_last, index, weight, slot_index = lax.optimization_barrier(
-        (near, own_last, index, weight, slot_index)
-    )
+    near, index, weight, slot_index = lax.optimization_barrier((near, index, weight, slot_index))
 
     keep, give = cross_part(place, share, low, high, near, control_near, blend, 4)
     got = swapped(give, "member", 1)
@@ -824,6 +814,7 @@
         P("space", None),
         P("space", None),
     )
+
     return jax.shard_map(
         per_device,
         mesh=mesh,

time: 148 us -> 144 us (0.973)
  blocking collectives: 36.3 us -> 55.8 us
  waiting for transfers between devices: 18.6 us -> 9.27 us
  starting transfers between devices: 22.7 us -> 13.6 us
  other arithmetic: 8.92 us -> 5.14 us
    all_to_all x0 -> x1, blocking collectives: none -> 28.3 us  [per_device(): lax.all_to_all(request, 'space', split_axis=0, concat_axis=0, tiled=True)]
    all_to_all x1 -> x0, starting transfers between devices: 10.7 us -> none  [per_device(): lax.all_to_all(request, 'space', split_axis=0, concat_axis=0, tiled=True)]
    all_to_all x1, blocking collectives: 36.3 us -> 27.5 us  [per_device(): lax.all_to_all(outgoing.reshape(spaces, capacity * pair_rows, width), 'sp...]
    ppermute x4, waiting for transfers between devices: 12.9 us -> 6.96 us  [swapped(): return lax.ppermute(x, axis, [(i, i ^ bit) for i in range(length)])]
    all_to_all x1 -> x0, waiting for transfers between devices: 3.98 us -> none  [per_device(): lax.all_to_all(request, 'space', split_axis=0, concat_axis=0, tiled=True)]
  transfers between devices with their start and end apart: 9 -> 8, of which waited for: 6 -> 3; matrix products, arithmetic and copies ran while one was open for 3% -> 4% of each run, Pallas kernels for 26% -> 29%
where the time goes in v2:
time: 144 us
  Pallas kernels  56.1 us (39%)
  blocking collectives  55.8 us (39%)
  starting transfers between devices  13.6 us (9%)
  waiting for transfers between devices  9.27 us (6%)
  other arithmetic  5.14 us (4%)
  local copies, waits for them, and re-layouts  3.76 us (3%)
    pallas_call x1, Pallas kernels, own_part(): pl.pallas_call(own_kernel, grid_spec=pltpu.PrefetchScalarGridSpec(num_sca...  30.8 us
    all_to_all x1, blocking collectives, per_device(): lax.all_to_all(request, 'space', split_axis=0, concat_axis=0, tiled=True)  28.3 us
    all_to_all x1, blocking collectives, per_device(): lax.all_to_all(outgoing.reshape(spaces, capacity * pair_rows, width), 'sp...  27.5 us
    ppermute x4, starting transfers between devices, passed_along(): return lax.ppermute(x, axis, pairs)  10.7 us
    pallas_call x1, Pallas kernels, cross_part(): pl.pallas_call(cross_kernel, grid=(count // group,), in_specs=[pl.BlockSp...  8.57 us
    ppermute x4, waiting for transfers between devices, swapped(): return lax.ppermute(x, axis, [(i, i ^ bit) for i in range(length)])  6.96 us
    pallas_call x1, Pallas kernels, edge_rows(): pl.pallas_call(edges_kernel, grid=(count // group,), in_specs=[pl.BlockSp...  5.77 us
    pallas_call x1, Pallas kernels, fine_part(): pl.pallas_call(fine_kernel, in_specs=[smem, vmem, vmem, vmem], out_specs=...  4.48 us
  transfers between devices with their start and end apart: 8, of which 3 were waited for; matrix products, arithmetic and copies ran while one was open for 4% of the time, Pallas kernels for 29%

profile of v2, /device:TPU:0, one launch (start us, length us, event | category | flops | bytes accessed | tf_op | source)
XLA Modules:
  0.0 143.8 jit_solution(17356616677525179262)
XLA Ops:
  0.0 0.0 copy-start.7
  0.0 0.0 copy-start.11
  0.0 0.0 copy-start.10
  0.0 5.8 %edge_rows.1 = (f32[17,2,32,384]{3,2,1,0:T(8,128)}, f32[17,2,32,384]{3,2,1,0:T(8,128)}) custom-call(bf16[16,32,16,384]{3,2,1,0:T(8,128)(2,1)} %members_ref.3, f32[32,16,384]{2,1,0:T(8,128)} %control_ref.3), custom_call_target="tpu_custom_call" | custom-call | tf_op jit(solution)/shard_map/edge_rows/pallas_call | solution.py:102
  5.8 3.6 %collective-permute-start.2 = (f32[17,2,32,384]{3,2,1,0:T(8,128)}, f32[17,2,32,384]{3,2,1,0:T(8,128)S(1)}, u32[]{:S(2)}, u32[]{:S(2)}) collective-permute-start(f32[17,2,32,384]{3,2,1,0:T(8,128)} %get-tuple-element.31), channel_id=1, source_target_pairs={{0,1},{1,2},{2,3},{3,4},{4,5},{5,6},{6,7},{7,8},{8,9},{9,10},{10,1... | collective-permute-start | bytes 5013512 | tf_op jit(solution)/shard_map/ppermute | solution.py:17
  9.4 1.3 collective-permute-start.3
  10.7 0.0 copy-done.7
  10.7 0.1 fusion.3
  10.8 0.0 copy-done.11
  10.8 0.7 pad_add_fusion.place_ref
  11.5 0.6 convert_reduce_fusion
  12.1 1.2 dynamic-slice_divide_fusion.share_ref
  13.3 0.0 copy-done.10
  13.3 0.7 broadcast_in_dim.12.blend_ref
  14.0 0.0 copy-start.9
  14.0 30.8 %own_part.1 = (f32[2,8,16,384]{3,2,1,0:T(8,128)}, f32[2,8,16,384]{3,2,1,0:T(8,128)}, bf16[16,8,32,384]{3,2,1,0:T(8,128)(2,1)}, f32[8,32,384]{2,1,0:T(8,128)}) custom-call(s32[3]{0:T(128)} %pad_add_fusion.place_ref, f32[16]{0:T(128)} %dynamic-slice_divide_fusion.share_ref, bf16[16,32,16,384]{3,2,1,0:T(8,128)(2,1)} %members_ref.3, f32[32,16,384]{2,1,0:T(8,128)} %control_ref.3, ...), custom_call_target="tpu_custom_call" | custom-call | tf_op jit(solution)/shard_map/own_part/pallas_call | solution.py:316
  44.8 0.2 select_reduce_fusion.1
  45.0 0.0 copy-start.8
  45.0 0.1 broadcast_subtract_fusion
  45.1 0.0 copy-done.9
  45.1 0.2 select_reduce_fusion
  45.3 0.1 collective-permute-start
  45.4 1.8 %columns.1 = (s32[16,8,768]{2,1,0:T(8,128)}, f32[16,8,768]{2,1,0:T(8,128)}) custom-call(s32[16,768]{1,0:T(8,128)} %source_ref.1, s32[16,768]{1,0:T(8,128)} %code_ref.1), custom_call_target="tpu_custom_call" | custom-call | tf_op jit(solution)/shard_map/columns/pallas_call | solution.py:723
  47.2 0.0 collective-permute-done.2.low_ref.low_control_ref
  47.2 0.0 copy-start
  47.2 2.3 %collective-permute-done.3.high_ref.high_control_ref = f32[17,2,32,384]{3,2,1,0:T(8,128)S(1)} collective-permute-done((f32[17,2,32,384]{3,2,1,0:T(8,128)}, f32[17,2,32,384]{3,2,1,0:T(8,128)S(1)}, u32[]{:S(2)}, u32[]{:S(2)}) %collective-permute-start.3) | collective-permute-done | bytes 1671200 | tf_op jit(solution)/shard_map/ppermute | solution.py:17
  49.5 0.0 copy-start.1
  49.5 0.0 copy-done
  49.5 1.2 copy-done.1
  50.7 8.6 %cross_part.1 = (f32[2,12,8,384]{3,2,1,0:T(8,128)}, f32[2,12,8,384]{3,2,1,0:T(8,128)}) custom-call(s32[3]{0:T(128)} %pad_add_fusion.place_ref, f32[16]{0:T(128)} %dynamic-slice_divide_fusion.share_ref, f32[17,2,32,384]{3,2,1,0:T(8,128)} %copy-done, f32[17,2,32,384]{3,2,1,0:T(8,128)} %copy-done, f32[17,2,32,384]{3,2,1,0:T(8,128)} %copy-done.1, ...), custom_call_target="tpu_custom_call" | custom-call | tf_op jit(solution)/shard_map/cross_part/pallas_call | solution.py:508
  59.2 0.0 copy-done.8
  59.2 0.1 collective-permute-start.4
  59.3 0.0 collective-permute-done.got_ref
  59.3 1.0 fusion.1
  60.4 2.0 %collective-permute-start.1 = (f32[8,16,384]{2,1,0:T(8,128)S(1)}, f32[8,16,384]{2,1,0:T(8,128)S(1)}, u32[]{:S(2)}, u32[]{:S(2)}) collective-permute-start(f32[8,16,384]{2,1,0:T(8,128)S(1)} %fusion.1), channel_id=1, source_target_pairs={{0,64},{32,96},{64,0},{96,32},{1,65},{33,97},{65,1},{97,33},{2,66}... | collective-permute-start | bytes 589832 | tf_op jit(solution)/shard_map/ppermute | solution.py:22
  62.4 0.0 collective-permute-done.4.cross_got_ref
  62.4 0.0 copy-start.2
  62.4 1.0 fusion.2
  63.4 0.7 collective-permute-start.5
  64.1 4.1 %collective-permute-done.1.last_ref = f32[8,16,384]{2,1,0:T(8,128)S(1)} collective-permute-done((f32[8,16,384]{2,1,0:T(8,128)S(1)}, f32[8,16,384]{2,1,0:T(8,128)S(1)}, u32[]{:S(2)}, u32[]{:S(2)}) %collective-permute-start.1) | collective-permute-done | bytes 196640 | tf_op jit(solution)/shard_map/ppermute | solution.py:22
  68.2 0.0 copy-start.3
  68.2 2.8 %collective-permute-done.5.cross_last_ref = f32[12,8,384]{2,1,0:T(8,128)S(1)} collective-permute-done((f32[12,8,384]{2,1,0:T(8,128)S(1)}, f32[12,8,384]{2,1,0:T(8,128)S(1)}, u32[]{:S(2)}, u32[]{:S(2)}) %collective-permute-start.5) | collective-permute-done | bytes 147488 | tf_op jit(solution)/shard_map/ppermute | solution.py:22
  71.1 0.0 copy-done.2
  71.1 0.0 copy-done.3
  71.1 0.0 copy-start.4
  71.1 0.7 copy-done.4
  71.8 1.9 %sent_rows.1 = (f32[3,8,384]{2,1,0:T(8,128)}, f32[2,8,384]{2,1,0:T(8,128)}) custom-call(f32[2,8,16,384]{3,2,1,0:T(8,128)} %get-tuple-element.29.own_ref, f32[2,8,16,384]{3,2,1,0:T(8,128)} %collective-permute-done.got_ref, f32[8,16,384]{2,1,0:T(8,128)} %copy-done.3, f32[2,12,8,384]{3,2,1,0:T(8,128)} %get-tuple-element.35.cross_ref, ...), custom_call_target="tpu_custom_call" | custom-call | tf_op jit(solution)/shard_map/sent_rows/pallas_call | solution.py:561
  73.7 1.3 collective-permute-start.7
  75.0 4.5 %collective-permute-start.6 = (f32[2,8,384]{2,1,0:T(8,128)}, f32[2,8,384]{2,1,0:T(8,128)S(1)}, u32[]{:S(2)}, u32[]{:S(2)}) collective-permute-start(f32[2,8,384]{2,1,0:T(8,128)} %get-tuple-element.37), channel_id=1, source_target_pairs={{0,1},{1,2},{2,3},{3,4},{4,5},{5,6},{6,7},{7,8},{8,9},{9,10},{10,1... | collective-permute-start | bytes 73736 | tf_op jit(solution)/shard_map/ppermute | solution.py:17
  79.5 28.3 %all_to_all.10.asked_ref = s32[32,1,128]{2,1,0:T(1,128)} all-to-all(s32[32,1,128]{2,1,0:T(1,128)S(1)} %bitcast.14), channel_id=1, replica_groups=mesh['member'=4,'space'=32] {'space'}, dimensions={0} | all-to-all | bytes 32768 | tf_op jit(solution)/shard_map/all_to_all | solution.py:780
  107.8 0.0 collective-permute-done.6.below_ref
  107.8 0.0 copy-start.6
  107.8 0.0 collective-permute-done.7.above_ref
  107.8 0.6 copy-done.6
  108.4 0.0 copy-start.5
  108.4 0.6 copy-done.5
  109.0 2.7 %answers.1 = f32[64,16,384]{2,1,0:T(8,128)} custom-call(s32[3]{0:T(128)} %pad_add_fusion.place_ref, s32[32,1,128]{2,1,0:T(1,128)} %all_to_all.10.asked_ref, f32[2,8,16,384]{3,2,1,0:T(8,128)} %get-tuple-element.29.own_ref, f32[2,8,16,384]{3,2,1,0:T(8,128)} %collective-permute-done.got_ref, f32[8,16,384]{2,1,0:T(8,128)} %copy-done.3, ...), custom_call_target="tpu_custom_call" | custom-call | tf_op jit(solution)/shard_map/answers/pallas_call | solution.py:632
  111.8 27.5 %all_to_all.11 = f32[32,32,384]{2,1,0:T(8,128)} all-to-all(f32[32,32,384]{2,1,0:T(8,128)} %bitcast.12), channel_id=1, replica_groups=mesh['member'=4,'space'=32] {'space'}, dimensions={0} | all-to-all | bytes 3145728 | tf_op jit(solution)/shard_map/all_to_all | solution.py:796
  139.3 4.5 %fine_part.1 = f32[16,8,2,768]{3,2,1,0:T(2,128)} custom-call(s32[16]{0:T(128)} %copy-done.8, f32[64,16,384]{2,1,0:T(8,128)} %bitcast.13, s32[16,8,768]{2,1,0:T(8,128)} %get-tuple-element.39.index_ref, f32[16,8,768]{2,1,0:T(8,128)} %get-tuple-element.40.weight_ref), custom_call_target="tpu_custom_call" | custom-call | tf_op jit(solution)/shard_map/fine_part/pallas_call | solution.py:700
  (5 shorter events, 0.1 us)
Async XLA Ops:
  0.0 10.7 %copy-start.7 = (s32[16,1]{0,1:T(1,128)S(1)}, s32[16,1]{0,1:T(1,128)}, u32[]{:S(2)}) copy-start(s32[16,1]{0,1:T(1,128)} %param.15) | copy-start | bytes 196
  0.0 10.8 %copy-start.11 = (s32[64]{0:T(128)S(1)}, s32[64]{0:T(128)}, u32[]{:S(2)}) copy-start(s32[64]{0:T(128)} %param.14) | copy-start | bytes 772
  0.0 13.3 %copy-start.10 = (f32[32]{0:T(128)S(1)}, f32[32]{0:T(128)}, u32[]{:S(2)}) copy-start(f32[32]{0:T(128)} %param.13) | copy-start | bytes 388
  5.8 41.4 %collective-permute-start.2 = (f32[17,2,32,384]{3,2,1,0:T(8,128)}, f32[17,2,32,384]{3,2,1,0:T(8,128)S(1)}, u32[]{:S(2)}, u32[]{:S(2)}) collective-permute-start(f32[17,2,32,384]{3,2,1,0:T(8,128)} %get-tuple-element.31), channel_id=1, source_target_pairs={{0,1},{1,2},{2,3},{3,4},{4,5},{5,6},{6,7},{7,8},{8,9},{9,10},{10,1... | collective-permute-start | bytes 5013512 | tf_op jit(solution)/shard_map/ppermute | solution.py:17
  9.4 40.1 %collective-permute-start.3 = (f32[17,2,32,384]{3,2,1,0:T(8,128)}, f32[17,2,32,384]{3,2,1,0:T(8,128)S(1)}, u32[]{:S(2)}, u32[]{:S(2)}) collective-permute-start(f32[17,2,32,384]{3,2,1,0:T(8,128)} %get-tuple-element.32), channel_id=1, source_target_pairs={{1,0},{2,1},{3,2},{4,3},{5,4},{6,5},{7,6},{8,7},{9,8},{10,9},{11,1... | collective-permute-start | bytes 5013512 | tf_op jit(solution)/shard_map/ppermute | solution.py:17
  14.0 31.1 %copy-start.9 = (s32[16]{0:T(128)S(1)}, s32[16]{0:T(128)}, u32[]{:S(2)}) copy-start(s32[16]{0:T(128)} %param.16) | copy-start | bytes 196
  45.0 14.2 %copy-start.8 = (s32[16]{0:T(128)}, s32[16]{0:T(128)S(1)}, u32[]{:S(2)}) copy-start(s32[16]{0:T(128)S(1)} %multiply_add_fusion.slot_ref) | copy-start | bytes 196
  45.3 14.1 %collective-permute-start = (f32[2,8,16,384]{3,2,1,0:T(8,128)}, f32[2,8,16,384]{3,2,1,0:T(8,128)}, u32[]{:S(2)}, u32[]{:S(2)}) collective-permute-start(f32[2,8,16,384]{3,2,1,0:T(8,128)} %get-tuple-element.30), channel_id=1, source_target_pairs={{0,32},{32,0},{64,96},{96,64},{1,33},{33,1},{65,97},{97,65},{2,34}... | collective-permute-start | bytes 1179656 | tf_op jit(solution)/shard_map/ppermute | solution.py:22
  47.2 2.3 %copy-start = (f32[17,2,32,384]{3,2,1,0:T(8,128)}, f32[17,2,32,384]{3,2,1,0:T(8,128)S(1)}, u32[]{:S(2)}) copy-start(f32[17,2,32,384]{3,2,1,0:T(8,128)S(1)} %collective-permute-done.2.low_ref.low_control_ref) | copy-start | bytes 5013508
  49.5 1.2 copy-start.1
  59.2 3.1 %collective-permute-start.4 = (f32[2,12,8,384]{3,2,1,0:T(8,128)}, f32[2,12,8,384]{3,2,1,0:T(8,128)S(1)}, u32[]{:S(2)}, u32[]{:S(2)}) collective-permute-start(f32[2,12,8,384]{3,2,1,0:T(8,128)} %get-tuple-element.36), channel_id=1, source_target_pairs={{0,32},{32,0},{64,96},{96,64},{1,33},{33,1},{65,97},{97,65},{2,34}... | collective-permute-start | bytes 884744 | tf_op jit(solution)/shard_map/ppermute | solution.py:22
  60.4 7.9 %collective-permute-start.1 = (f32[8,16,384]{2,1,0:T(8,128)S(1)}, f32[8,16,384]{2,1,0:T(8,128)S(1)}, u32[]{:S(2)}, u32[]{:S(2)}) collective-permute-start(f32[8,16,384]{2,1,0:T(8,128)S(1)} %fusion.1), channel_id=1, source_target_pairs={{0,64},{32,96},{64,0},{96,32},{1,65},{33,97},{65,1},{97,33},{2,66}... | collective-permute-start | bytes 589832 | tf_op jit(solution)/shard_map/ppermute | solution.py:22
  62.4 8.7 %copy-start.2 = (f32[2,12,8,384]{3,2,1,0:T(8,128)}, f32[2,12,8,384]{3,2,1,0:T(8,128)S(1)}, u32[]{:S(2)}) copy-start(f32[2,12,8,384]{3,2,1,0:T(8,128)S(1)} %collective-permute-done.4.cross_got_ref) | copy-start | bytes 884740
  63.4 7.7 %collective-permute-start.5 = (f32[12,8,384]{2,1,0:T(8,128)S(1)}, f32[12,8,384]{2,1,0:T(8,128)S(1)}, u32[]{:S(2)}, u32[]{:S(2)}) collective-permute-start(f32[12,8,384]{2,1,0:T(8,128)S(1)} %fusion.2), channel_id=1, source_target_pairs={{0,64},{32,96},{64,0},{96,32},{1,65},{33,97},{65,1},{97,33},{2,66}... | collective-permute-start | bytes 442376 | tf_op jit(solution)/shard_map/ppermute | solution.py:22
  68.2 2.9 %copy-start.3 = (f32[8,16,384]{2,1,0:T(8,128)}, f32[8,16,384]{2,1,0:T(8,128)S(1)}, u32[]{:S(2)}) copy-start(f32[8,16,384]{2,1,0:T(8,128)S(1)} %collective-permute-done.1.last_ref) | copy-start | bytes 589828
  71.1 0.7 copy-start.4
  73.7 34.1 %collective-permute-start.7 = (f32[3,8,384]{2,1,0:T(8,128)}, f32[3,8,384]{2,1,0:T(8,128)S(1)}, u32[]{:S(2)}, u32[]{:S(2)}) collective-permute-start(f32[3,8,384]{2,1,0:T(8,128)} %get-tuple-element.38), channel_id=1, source_target_pairs={{1,0},{2,1},{3,2},{4,3},{5,4},{6,5},{7,6},{8,7},{9,8},{10,9},{11,1... | collective-permute-start | bytes 110600 | tf_op jit(solution)/shard_map/ppermute | solution.py:17
  75.0 32.8 %collective-permute-start.6 = (f32[2,8,384]{2,1,0:T(8,128)}, f32[2,8,384]{2,1,0:T(8,128)S(1)}, u32[]{:S(2)}, u32[]{:S(2)}) collective-permute-start(f32[2,8,384]{2,1,0:T(8,128)} %get-tuple-element.37), channel_id=1, source_target_pairs={{0,1},{1,2},{2,3},{3,4},{4,5},{5,6},{6,7},{7,8},{8,9},{9,10},{10,1... | collective-permute-start | bytes 73736 | tf_op jit(solution)/shard_map/ppermute | solution.py:17
  107.8 0.6 copy-start.6
  108.4 0.6 copy-start.5

commit v3 on v2

--- a/solution.py
+++ b/solution.py
@@ -11,9 +11,11 @@
 PITCH = 24
 
 
-def passed_along(x, axis, by):
+def paired(x, axis, first):
     length = lax.axis_size(axis)
-    pairs = [(i, i + by) for i in range(length) if 0 <= i + by < length]
+    pairs = []
+    for low in range(first, length - 1, 2):
+        pairs += [(low, low + 1), (low + 1, low)]
     return lax.ppermute(x, axis, pairs)
 
 
@@ -51,19 +53,20 @@
     return plus(parts, side_sum(parts, lane))
 
 
-def edges_kernel(members_ref, control_ref, top_ref, bottom_ref, scratch, top_out, bottom_out, sems):
+def edges_kernel(place_ref, members_ref, control_ref, a_ref, b_ref, scratch, stage, sems):
     step = pl.program_id(0)
     steps = pl.num_programs(0)
     group = members_ref.shape[0]
     chans, rows = members_ref.shape[1:3]
     parts = scratch.shape[0]
+    odd = place_ref[3]
 
     def copies(first, count, index):
         return [
             pltpu.make_async_copy(
-                stage.at[pl.ds(first, count)], ref.at[pl.ds(first, count)], sems.at[side, index]
+                stage.at[side, pl.ds(first, count)], ref.at[pl.ds(first, count)], sems.at[side, index]
             )
-            for side, (stage, ref) in enumerate(((top_out, top_ref), (bottom_out, bottom_ref)))
+            for side, ref in enumerate((a_ref, b_ref))
         ]
 
     def rows_out(wide, index):
@@ -72,8 +75,8 @@
             for chan in range(chans):
                 scratch[part, chan * PITCH : chan * PITCH + rows] = wide[chan, :, lanes]
             for slot in range(2):
-                for which, stage in ((slot, top_out), (rows - 2 + slot, bottom_out)):
-                    stage[index, slot, :, lanes] = scratch[
+                for which, side in ((slot, 1 - odd), (rows - 1 - slot, odd)):
+                    stage[side, index, slot, :, lanes] = scratch[
                         part, pl.ds(which, chans, stride=PITCH), :
                     ]
 
@@ -84,7 +87,7 @@
 
     @pl.when(step == steps - 1)
     def _():
-        count = top_ref.shape[0] - 1
+        count = a_ref.shape[0] - 1
         rows_out(control_ref[...], count)
         for copy in copies(count, 1, count // group):
             copy.start()
@@ -95,7 +98,7 @@
             copy.wait()
 
 
-def edge_rows(members, control, group):
+def edge_rows(place, members, control, group):
     count, chans, rows, width = members.shape
     shape = (count + 1, 2, chans, width)
     out = jax.ShapeDtypeStruct(shape, jnp.float32)
@@ -103,6 +106,7 @@
         edges_kernel,
         grid=(count // group,),
         in_specs=[
+            pl.BlockSpec(memory_space=pltpu.SMEM),
             pl.BlockSpec((group, chans, rows, width), lambda i: (i, 0, 0, 0)),
             pl.BlockSpec((chans, rows, width), lambda i: (0, 0, 0)),
         ],
@@ -110,12 +114,11 @@
         out_shape=[out, out],
         scratch_shapes=[
             pltpu.VMEM((width // LANES, chans * PITCH, LANES), jnp.float32),
-            pltpu.VMEM(shape, jnp.float32),
-            pltpu.VMEM(shape, jnp.float32),
+            pltpu.VMEM((2,) + shape, jnp.float32),
             pltpu.SemaphoreType.DMA((2, count // group + 1)),
         ],
         name="edge_rows",
-    )(members, control)
+    )(place, members, control)
 
 
 def column_operators(width):
@@ -149,7 +152,9 @@
     last = pl.num_programs(0) - 1
     static = step == last
     fields, firsts, seconds, mixes = [work[i * both : (i + 1) * both] for i in range(4)]
-    ends = (0, 1, 2, 3, rows - 4, rows - 3, rows - 2, rows - 1)
+    odd = place_ref[3]
+    ends = [(4 * (1 - odd) + i, i) for i in range(4)]
+    ends += [(4 * odd + i, rows - 1 - i) for i in range(4)]
 
     def lanes(part):
         return slice(part * LANES, (part + 1) * LANES)
@@ -172,7 +177,7 @@
                 return carry
 
             lax.fori_loop(0, chans, fill, 0, unroll=4)
-            for place, row in enumerate(ends):
+            for place, row in ends:
                 for part in range(parts):
                     near_ref[which, place, :, lanes(part)] = scratch[
                         part, pl.ds(row, chans, stride=PITCH), :
@@ -189,7 +194,7 @@
             return carry
 
         lax.fori_loop(0, chans, fill, 0, unroll=4)
-        for place, row in enumerate(ends):
+        for place, row in ends:
             for part in range(parts):
                 control_near_ref[place, :, lanes(part)] = scratch[
                     part, pl.ds(row, chans, stride=PITCH), :
@@ -355,7 +360,7 @@
 
 
 def cross_kernel(
-    place_ref, share_ref, low_ref, low_control_ref, high_ref, high_control_ref,
+    place_ref, share_ref, a_ref, a_control_ref, b_ref, b_control_ref,
     near_ref, control_ref, blend_ref, pair_ref, single_ref,
     keep_ref, give_ref, sums, first, second, third, fourth, mixed, alone,
 ):
@@ -367,8 +372,8 @@
     final = step == pl.num_programs(0) - 1
     span = group * chans
     sides = (
-        (low_ref, low_control_ref, (1, 0), (0, 1, 2, 3)),
-        (high_ref, high_control_ref, (0, 1), (7, 6, 5, 4)),
+        (a_ref, a_control_ref, (0, 1), (0, 1, 2, 3)),
+        (b_ref, b_control_ref, (0, 1), (4, 5, 6, 7)),
     )
 
     def lanes(part, base=0):
@@ -495,7 +500,7 @@
         lax.fori_loop(0, chans // 8, finish, 0, unroll=2)
 
 
-def cross_part(place, share, low, high, near, control_near, blend, group):
+def cross_part(place, share, a, b, near, control_near, blend, group):
     count, rows, chans, width = near.shape
     halo = pl.BlockSpec((group, 2, chans, width), lambda i: (i, 0, 0, 0))
     halo_control = pl.BlockSpec((1, 2, chans, width), lambda i: (count, 0, 0, 0))
@@ -533,10 +538,12 @@
             pltpu.VMEM((2, 2 * span, 2 * LANES), jnp.float32),
         ],
         name="cross_part",
-    )(place, share, low, low, high, high, near, control_near, blend, pair, single)
-
-
-def sent_kernel(own_ref, got_ref, last_ref, cross_ref, cross_got_ref, cross_last_ref, up_ref, down_ref, turned):
+    )(place, share, a, a, b, b, near, control_near, blend, pair, single)
+
+
+def sent_kernel(
+    place_ref, own_ref, got_ref, last_ref, cross_ref, cross_got_ref, cross_last_ref, a_ref, b_ref, turned
+):
     chans, _, width = last_ref.shape
     whole = own_ref[0] + got_ref[0] + last_ref[...]
     for part in range(width // LANES):
@@ -548,38 +555,40 @@
         def crossed(i):
             return cross_ref[0, i, :, lanes] + cross_got_ref[0, i, :, lanes] + cross_last_ref[i, :, lanes]
 
-        for i in range(2):
-            up_ref[i, :, lanes] = crossed(4 + i)
-            down_ref[i, :, lanes] = crossed(10 + i)
-        up_ref[2, :, lanes] = first + crossed(0)
-
-
-def sent_rows(own, got, last, cross, cross_got, cross_last):
+        first += crossed(6 * (1 - place_ref[3]))
+        for side, ref in enumerate((a_ref, b_ref)):
+            for i in range(2):
+                ref[i, :, lanes] = crossed(6 * side + 4 + i)
+            ref[2, :, lanes] = first
+
+
+def sent_rows(place, own, got, last, cross, cross_got, cross_last):
     chans, _, width = last.shape
     one = lambda x: pl.BlockSpec((1,) + x.shape[1:], lambda i: (0, 0, 0, 0))
     vmem = pl.BlockSpec(memory_space=pltpu.VMEM)
     return pl.pallas_call(
         sent_kernel,
         grid=(1,),
-        in_specs=[one(own), one(got), vmem, one(cross), one(cross_got), vmem],
+        in_specs=[
+            pl.BlockSpec(memory_space=pltpu.SMEM),
+            one(own), one(got), vmem, one(cross), one(cross_got), vmem,
+        ],
         out_specs=[vmem, vmem],
-        out_shape=[
-            jax.ShapeDtypeStruct((3, chans, width), jnp.float32),
-            jax.ShapeDtypeStruct((2, chans, width), jnp.float32),
-        ],
+        out_shape=[jax.ShapeDtypeStruct((3, chans, width), jnp.float32)] * 2,
         scratch_shapes=[pltpu.VMEM((chans * PITCH, LANES), jnp.float32)],
         name="sent_rows",
-    )(own, got, last, cross, cross_got, cross_last)
+    )(place, own, got, last, cross, cross_got, cross_last)
 
 
 def answer_kernel(
     place_ref, asked_ref, own_ref, got_ref, last_ref, cross_ref, cross_got_ref, cross_last_ref,
-    below_ref, above_ref, out_ref, turned, pairs,
+    a_ref, b_ref, out_ref, turned, pairs,
 ):
     chans, rows, width = last_ref.shape
     parts = width // LANES
     capacity = out_ref.shape[0] // asked_ref.shape[0]
     keep_high = (place_ref[2] != 0).astype(jnp.float32)
+    odd = place_ref[3]
     whole = own_ref[0] + got_ref[0] + last_ref[...]
     for part in range(parts):
         for chan in range(chans):
@@ -590,21 +599,27 @@
     def crossed(i, lanes):
         return cross_ref[0, i, :, lanes] + cross_got_ref[0, i, :, lanes] + cross_last_ref[i, :, lanes]
 
+    def from_next(i, lanes):
+        return jnp.where(odd == 0, a_ref[i, :, lanes], b_ref[i, :, lanes])
+
+    def from_before(i, lanes):
+        return jnp.where(odd == 0, b_ref[i, :, lanes], a_ref[i, :, lanes])
+
     for part in range(parts):
         lanes = slice(part * LANES, (part + 1) * LANES)
         for row in range(rows + 1):
             if row < rows:
                 value = turned[part, pl.ds(row, chans, stride=PITCH), :]
             else:
-                value = keep_high * (above_ref[2, :, lanes] + crossed(10, lanes))
+                value = keep_high * (from_next(2, lanes) + crossed(6 * odd + 4, lanes))
             if row < 4:
-                value += crossed(row, lanes)
+                value += crossed(6 * (1 - odd) + row, lanes)
             if rows - 4 <= row < rows:
-                value += crossed(6 + rows - 1 - row, lanes)
+                value += crossed(6 * odd + rows - 1 - row, lanes)
             if row < 2:
-                value += below_ref[row, :, lanes]
+                value += from_before(row, lanes)
             if rows - 2 <= row < rows:
-                value += above_ref[rows - 1 - row, :, lanes]
+                value += from_next(rows - 1 - row, lanes)
             if row < rows:
                 pairs[part, pl.ds(row * 2 * chans, chans, stride=2), :] = value
             if row > 0:
@@ -623,7 +638,7 @@
     lax.fori_loop(0, asked_ref.shape[0], one, 0, unroll=4)
 
 
-def answers(place, asked, capacity, own, got, last, cross, cross_got, cross_last, below, above):
+def answers(place, asked, capacity, own, got, last, cross, cross_got, cross_last, a, b):
     chans, rows, width = last.shape
     slots = asked.shape[0] * capacity
     smem = pl.BlockSpec(memory_space=pltpu.SMEM)
@@ -640,7 +655,7 @@
             pltpu.VMEM((width // LANES, rows * 2 * chans, LANES), jnp.float32),
         ],
         name="answers",
-    )(place, asked, own, got, last, cross, cross_got, cross_last, below, above)
+    )(place, asked, own, got, last, cross, cross_got, cross_last, a, b)
 
 
 def fine_kernel(slot_ref, arrived_ref, index_ref, weight_ref, out_ref):
@@ -745,17 +760,18 @@
     space_index = lax.axis_index("space")
     member_slot = lax.axis_index("member")
 
-    top, bottom = edge_rows(members, control, 4)
-    high = passed_along(top, "space", -1)
-    low = passed_along(bottom, "space", 1)
-
     place = jnp.stack(
         [
             member_slot,
             jnp.where(space_index == 0, 0, jnp.where(space_index == spaces - 1, 2, 1)),
             (space_index < spaces - 1).astype(jnp.int32),
+            space_index % 2,
         ]
     ).astype(jnp.int32)
+    to_a, to_b = edge_rows(place, members, control, 4)
+    halo_b = paired(to_b, "space", 1)
+    halo_a = paired(to_a, "space", 0)
+
     weight_codes = member_weights.astype(jnp.float32)
     share = lax.dynamic_slice_in_dim(
         weight_codes, member_slot * member_count, member_count
@@ -782,15 +798,15 @@
     own_last = swapped(own_keep[1] + own_got[1], "member", 2)
     near, index, weight, slot_index = lax.optimization_barrier((near, index, weight, slot_index))
 
-    keep, give = cross_part(place, share, low, high, near, control_near, blend, 4)
+    keep, give = cross_part(place, share, halo_a, halo_b, near, control_near, blend, 4)
     got = swapped(give, "member", 1)
     last = swapped(keep[1] + got[1], "member", 2)
-    up, down = sent_rows(own_keep, own_got, own_last, keep, got, last)
-    above = passed_along(up, "space", -1)
-    below = passed_along(down, "space", 1)
+    back_a, back_b = sent_rows(place, own_keep, own_got, own_last, keep, got, last)
+    back_b = paired(back_b, "space", 1)
+    back_a = paired(back_a, "space", 0)
 
     outgoing = answers(
-        place, asked, capacity, own_keep, own_got, own_last, keep, got, last, below, above
+        place, asked, capacity, own_keep, own_got, own_last, keep, got, last, back_a, back_b
     )
     pair_rows = outgoing.shape[1]
     arrived = lax.all_to_all(

time: 144 us -> 136 us (0.944)
  starting transfers between devices: 13.6 us -> 9.8 us
  blocking collectives: 55.8 us -> 52.9 us
  waiting for transfers between devices: 9.27 us -> 7.08 us
    ppermute x4, starting transfers between devices: 10.7 us -> 6.65 us  [paired(): return lax.ppermute(x, axis, pairs)]
    all_to_all x1, blocking collectives: 28.3 us -> 25.4 us  [per_device(): lax.all_to_all(request, 'space', split_axis=0, concat_axis=0, tiled=True)]
    ppermute x4, waiting for transfers between devices: 2.31 us -> 0.12 us  [paired(): return lax.ppermute(x, axis, pairs)]
  transfers between devices with their start and end apart: 8 -> 8, of which waited for: 3 -> 3; matrix products, arithmetic and copies ran while one was open for 4% -> 4% of each run, Pallas kernels for 29% -> 30%
where the time goes in v3:
time: 136 us; the launch traced here: 135 us
  Pallas kernels  56.1 us (41%)
  blocking collectives  52.9 us (39%)
  starting transfers between devices  9.8 us (7%)
  waiting for transfers between devices  7.08 us (5%)
  other arithmetic  5.14 us (4%)
  local copies, waits for them, and re-layouts  4.26 us (3%)
    pallas_call x1, Pallas kernels, own_part(): pl.pallas_call(own_kernel, grid_spec=pltpu.PrefetchScalarGridSpec(num_sca...  30.8 us
    all_to_all x1, blocking collectives, per_device(): lax.all_to_all(outgoing.reshape(spaces, capacity * pair_rows, width), 'sp...  27.5 us
    all_to_all x1, blocking collectives, per_device(): lax.all_to_all(request, 'space', split_axis=0, concat_axis=0, tiled=True)  25.4 us
    pallas_call x1, Pallas kernels, cross_part(): pl.pallas_call(cross_kernel, grid=(count // group,), in_specs=[pl.BlockSp...  8.56 us
    ppermute x4, waiting for transfers between devices, swapped(): return lax.ppermute(x, axis, [(i, i ^ bit) for i in range(length)])  6.96 us
    ppermute x4, starting transfers between devices, paired(): return lax.ppermute(x, axis, pairs)  6.65 us
    pallas_call x1, Pallas kernels, edge_rows(): pl.pallas_call(edges_kernel, grid=(count // group,), in_specs=[pl.BlockSp...  5.81 us
    pallas_call x1, Pallas kernels, fine_part(): pl.pallas_call(fine_kernel, in_specs=[smem, vmem, vmem, vmem], out_specs=...  4.48 us
  transfers between devices with their start and end apart: 8, of which 3 were waited for; matrix products, arithmetic and copies ran while one was open for 4% of the time, Pallas kernels for 30%

profile of v3, /device:TPU:0, one launch (start us, length us, event | category | flops | bytes accessed | tf_op | source)
XLA Modules:
  0.0 135.4 jit_solution(11669555757548803082)
XLA Ops:
  0.0 0.7 pad_add_fusion.place_ref
  0.7 0.0 copy-start.11
  0.7 0.0 copy-start.7
  0.7 0.0 copy-start.10
  0.7 5.8 %edge_rows.1 = (f32[17,2,32,384]{3,2,1,0:T(8,128)}, f32[17,2,32,384]{3,2,1,0:T(8,128)}) custom-call(s32[4]{0:T(128)} %pad_add_fusion.place_ref, bf16[16,32,16,384]{3,2,1,0:T(8,128)(2,1)} %members_ref.3, f32[32,16,384]{2,1,0:T(8,128)} %control_ref.3), custom_call_target="tpu_custom_call" | custom-call | tf_op jit(solution)/shard_map/edge_rows/pallas_call | solution.py:105
  6.5 1.7 %collective-permute-start.2 = (f32[17,2,32,384]{3,2,1,0:T(8,128)}, f32[17,2,32,384]{3,2,1,0:T(8,128)S(1)}, u32[]{:S(2)}, u32[]{:S(2)}) collective-permute-start(f32[17,2,32,384]{3,2,1,0:T(8,128)} %get-tuple-element.31), channel_id=1, source_target_pairs={{0,1},{1,0},{2,3},{3,2},{4,5},{5,4},{6,7},{7,6},{8,9},{9,8},{10,11... | collective-permute-start | bytes 5013512 | tf_op jit(solution)/shard_map/ppermute | solution.py:19
  8.2 0.8 collective-permute-start.3
  8.9 0.0 copy-done.11
  9.0 0.0 copy-done.7
  9.0 0.1 fusion.3
  9.1 0.6 convert_reduce_fusion
  9.7 1.2 dynamic-slice_divide_fusion.share_ref
  10.9 0.0 copy-done.10
  10.9 0.7 broadcast_in_dim.12.blend_ref
  11.6 0.0 copy-start.9
  11.6 30.8 %own_part.1 = (f32[2,8,16,384]{3,2,1,0:T(8,128)}, f32[2,8,16,384]{3,2,1,0:T(8,128)}, bf16[16,8,32,384]{3,2,1,0:T(8,128)(2,1)}, f32[8,32,384]{2,1,0:T(8,128)}) custom-call(s32[4]{0:T(128)} %pad_add_fusion.place_ref, f32[16]{0:T(128)} %dynamic-slice_divide_fusion.share_ref, bf16[16,32,16,384]{3,2,1,0:T(8,128)(2,1)} %members_ref.3, f32[32,16,384]{2,1,0:T(8,128)} %control_ref.3, ...), custom_call_target="tpu_custom_call" | custom-call | tf_op jit(solution)/shard_map/own_part/pallas_call | solution.py:321
  42.4 0.2 select_reduce_fusion.1
  42.6 0.0 copy-start.8
  42.6 0.1 broadcast_subtract_fusion
  42.7 0.0 copy-done.9
  42.7 0.2 select_reduce_fusion
  42.9 0.1 collective-permute-start
  43.0 1.8 %columns.1 = (s32[16,8,768]{2,1,0:T(8,128)}, f32[16,8,768]{2,1,0:T(8,128)}) custom-call(s32[16,768]{1,0:T(8,128)} %source_ref.1, s32[16,768]{1,0:T(8,128)} %code_ref.1), custom_call_target="tpu_custom_call" | custom-call | tf_op jit(solution)/shard_map/columns/pallas_call | solution.py:738
  44.8 0.1 collective-permute-done.2.a_ref.a_control_ref
  44.9 0.0 copy-start
  44.9 0.0 collective-permute-done.3.b_ref.b_control_ref
  44.9 0.0 copy-start.1
  44.9 1.2 copy-done
  46.1 0.5 copy-done.1
  46.6 8.6 %cross_part.1 = (f32[2,12,8,384]{3,2,1,0:T(8,128)}, f32[2,12,8,384]{3,2,1,0:T(8,128)}) custom-call(s32[4]{0:T(128)} %pad_add_fusion.place_ref, f32[16]{0:T(128)} %dynamic-slice_divide_fusion.share_ref, f32[17,2,32,384]{3,2,1,0:T(8,128)} %copy-done, f32[17,2,32,384]{3,2,1,0:T(8,128)} %copy-done, f32[17,2,32,384]{3,2,1,0:T(8,128)} %copy-done.1, ...), custom_call_target="tpu_custom_call" | custom-call | tf_op jit(solution)/shard_map/cross_part/pallas_call | solution.py:513
  55.1 0.0 copy-done.8
  55.1 0.4 collective-permute-start.4
  55.6 0.0 collective-permute-done.got_ref
  55.6 1.0 fusion.1
  56.6 2.0 %collective-permute-start.1 = (f32[8,16,384]{2,1,0:T(8,128)S(1)}, f32[8,16,384]{2,1,0:T(8,128)S(1)}, u32[]{:S(2)}, u32[]{:S(2)}) collective-permute-start(f32[8,16,384]{2,1,0:T(8,128)S(1)} %fusion.1), channel_id=1, source_target_pairs={{0,64},{32,96},{64,0},{96,32},{1,65},{33,97},{65,1},{97,33},{2,66}... | collective-permute-start | bytes 589832 | tf_op jit(solution)/shard_map/ppermute | solution.py:24
  58.7 0.0 collective-permute-done.4.cross_got_ref
  58.7 0.0 copy-start.2
  58.7 1.0 fusion.2
  59.7 0.6 collective-permute-start.5
  60.3 4.2 %collective-permute-done.1.last_ref = f32[8,16,384]{2,1,0:T(8,128)S(1)} collective-permute-done((f32[8,16,384]{2,1,0:T(8,128)S(1)}, f32[8,16,384]{2,1,0:T(8,128)S(1)}, u32[]{:S(2)}, u32[]{:S(2)}) %collective-permute-start.1) | collective-permute-done | bytes 196640 | tf_op jit(solution)/shard_map/ppermute | solution.py:24
  64.5 0.0 copy-start.3
  64.5 2.8 %collective-permute-done.5.cross_last_ref = f32[12,8,384]{2,1,0:T(8,128)S(1)} collective-permute-done((f32[12,8,384]{2,1,0:T(8,128)S(1)}, f32[12,8,384]{2,1,0:T(8,128)S(1)}, u32[]{:S(2)}, u32[]{:S(2)}) %collective-permute-start.5) | collective-permute-done | bytes 147488 | tf_op jit(solution)/shard_map/ppermute | solution.py:24
  67.3 0.0 copy-done.2
  67.3 0.0 copy-done.3
  67.3 0.0 copy-start.4
  67.3 0.7 copy-done.4
  67.9 1.9 %sent_rows.1 = (f32[3,8,384]{2,1,0:T(8,128)}, f32[3,8,384]{2,1,0:T(8,128)}) custom-call(s32[4]{0:T(128)} %pad_add_fusion.place_ref, f32[2,8,16,384]{3,2,1,0:T(8,128)} %get-tuple-element.29.own_ref, f32[2,8,16,384]{3,2,1,0:T(8,128)} %collective-permute-done.got_ref, f32[8,16,384]{2,1,0:T(8,128)} %copy-done.3, f32[2,12,8,384]{3,2,1,0:T(8,128)} %get-tuple-element.35.cross_ref, ...), custom_call_target="tpu_custom_call" | custom-call | tf_op jit(solution)/shard_map/sent_rows/pallas_call | solution.py:569
  69.9 3.6 %collective-permute-start.6 = (f32[3,8,384]{2,1,0:T(8,128)}, f32[3,8,384]{2,1,0:T(8,128)S(1)}, u32[]{:S(2)}, u32[]{:S(2)}) collective-permute-start(f32[3,8,384]{2,1,0:T(8,128)} %get-tuple-element.37), channel_id=1, source_target_pairs={{0,1},{1,0},{2,3},{3,2},{4,5},{5,4},{6,7},{7,6},{8,9},{9,8},{10,11... | collective-permute-start | bytes 110600 | tf_op jit(solution)/shard_map/ppermute | solution.py:19
  73.4 0.7 collective-permute-start.7
  74.1 25.4 %all_to_all.10.asked_ref = s32[32,1,128]{2,1,0:T(1,128)} all-to-all(s32[32,1,128]{2,1,0:T(1,128)S(1)} %bitcast.15), channel_id=1, replica_groups=mesh['member'=4,'space'=32] {'space'}, dimensions={0} | all-to-all | bytes 32768 | tf_op jit(solution)/shard_map/all_to_all | solution.py:796
  99.5 0.0 collective-permute-done.6.a_ref
  99.5 0.0 copy-start.5
  99.5 0.0 collective-permute-done.7.b_ref
  99.5 0.6 copy-done.5
  100.1 0.0 copy-start.6
  100.1 0.6 copy-done.6
  100.7 2.7 %answers.1 = f32[64,16,384]{2,1,0:T(8,128)} custom-call(s32[4]{0:T(128)} %pad_add_fusion.place_ref, s32[32,1,128]{2,1,0:T(1,128)} %all_to_all.10.asked_ref, f32[2,8,16,384]{3,2,1,0:T(8,128)} %get-tuple-element.29.own_ref, f32[2,8,16,384]{3,2,1,0:T(8,128)} %collective-permute-done.got_ref, f32[8,16,384]{2,1,0:T(8,128)} %copy-done.3, ...), custom_call_target="tpu_custom_call" | custom-call | tf_op jit(solution)/shard_map/answers/pallas_call | solution.py:647
  103.4 27.5 %all_to_all.11 = f32[32,32,384]{2,1,0:T(8,128)} all-to-all(f32[32,32,384]{2,1,0:T(8,128)} %bitcast.13), channel_id=1, replica_groups=mesh['member'=4,'space'=32] {'space'}, dimensions={0} | all-to-all | bytes 3145728 | tf_op jit(solution)/shard_map/all_to_all | solution.py:812
  130.9 4.5 %fine_part.1 = f32[16,8,2,768]{3,2,1,0:T(2,128)} custom-call(s32[16]{0:T(128)} %copy-done.8, f32[64,16,384]{2,1,0:T(8,128)} %bitcast.14, s32[16,8,768]{2,1,0:T(8,128)} %get-tuple-element.39.index_ref, f32[16,8,768]{2,1,0:T(8,128)} %get-tuple-element.40.weight_ref), custom_call_target="tpu_custom_call" | custom-call | tf_op jit(solution)/shard_map/fine_part/pallas_call | solution.py:715
  (5 shorter events, 0.1 us)
Async XLA Ops:
  0.7 8.3 %copy-start.11 = (s32[64]{0:T(128)S(1)}, s32[64]{0:T(128)}, u32[]{:S(2)}) copy-start(s32[64]{0:T(128)} %param.14) | copy-start | bytes 772
  0.7 8.3 %copy-start.7 = (s32[16,1]{0,1:T(1,128)S(1)}, s32[16,1]{0,1:T(1,128)}, u32[]{:S(2)}) copy-start(s32[16,1]{0,1:T(1,128)} %param.15) | copy-start | bytes 196
  0.7 10.3 %copy-start.10 = (f32[32]{0:T(128)S(1)}, f32[32]{0:T(128)}, u32[]{:S(2)}) copy-start(f32[32]{0:T(128)} %param.13) | copy-start | bytes 388
  6.5 38.4 %collective-permute-start.2 = (f32[17,2,32,384]{3,2,1,0:T(8,128)}, f32[17,2,32,384]{3,2,1,0:T(8,128)S(1)}, u32[]{:S(2)}, u32[]{:S(2)}) collective-permute-start(f32[17,2,32,384]{3,2,1,0:T(8,128)} %get-tuple-element.31), channel_id=1, source_target_pairs={{0,1},{1,0},{2,3},{3,2},{4,5},{5,4},{6,7},{7,6},{8,9},{9,8},{10,11... | collective-permute-start | bytes 5013512 | tf_op jit(solution)/shard_map/ppermute | solution.py:19
  8.2 36.7 %collective-permute-start.3 = (f32[17,2,32,384]{3,2,1,0:T(8,128)}, f32[17,2,32,384]{3,2,1,0:T(8,128)S(1)}, u32[]{:S(2)}, u32[]{:S(2)}) collective-permute-start(f32[17,2,32,384]{3,2,1,0:T(8,128)} %get-tuple-element.32), channel_id=1, source_target_pairs={{1,2},{2,1},{3,4},{4,3},{5,6},{6,5},{7,8},{8,7},{9,10},{10,9},{11,... | collective-permute-start | bytes 5013512 | tf_op jit(solution)/shard_map/ppermute | solution.py:19
  11.6 31.1 %copy-start.9 = (s32[16]{0:T(128)S(1)}, s32[16]{0:T(128)}, u32[]{:S(2)}) copy-start(s32[16]{0:T(128)} %param.16) | copy-start | bytes 196
  42.6 12.6 %copy-start.8 = (s32[16]{0:T(128)}, s32[16]{0:T(128)S(1)}, u32[]{:S(2)}) copy-start(s32[16]{0:T(128)S(1)} %multiply_add_fusion.slot_ref) | copy-start | bytes 196
  42.9 12.7 %collective-permute-start = (f32[2,8,16,384]{3,2,1,0:T(8,128)}, f32[2,8,16,384]{3,2,1,0:T(8,128)}, u32[]{:S(2)}, u32[]{:S(2)}) collective-permute-start(f32[2,8,16,384]{3,2,1,0:T(8,128)} %get-tuple-element.30), channel_id=1, source_target_pairs={{0,32},{32,0},{64,96},{96,64},{1,33},{33,1},{65,97},{97,65},{2,34}... | collective-permute-start | bytes 1179656 | tf_op jit(solution)/shard_map/ppermute | solution.py:24
  44.9 1.2 copy-start
  44.9 1.7 %copy-start.1 = (f32[17,2,32,384]{3,2,1,0:T(8,128)}, f32[17,2,32,384]{3,2,1,0:T(8,128)S(1)}, u32[]{:S(2)}) copy-start(f32[17,2,32,384]{3,2,1,0:T(8,128)S(1)} %collective-permute-done.3.b_ref.b_control_ref) | copy-start | bytes 5013508
  55.1 3.5 %collective-permute-start.4 = (f32[2,12,8,384]{3,2,1,0:T(8,128)}, f32[2,12,8,384]{3,2,1,0:T(8,128)S(1)}, u32[]{:S(2)}, u32[]{:S(2)}) collective-permute-start(f32[2,12,8,384]{3,2,1,0:T(8,128)} %get-tuple-element.36), channel_id=1, source_target_pairs={{0,32},{32,0},{64,96},{96,64},{1,33},{33,1},{65,97},{97,65},{2,34}... | collective-permute-start | bytes 884744 | tf_op jit(solution)/shard_map/ppermute | solution.py:24
  56.6 7.9 %collective-permute-start.1 = (f32[8,16,384]{2,1,0:T(8,128)S(1)}, f32[8,16,384]{2,1,0:T(8,128)S(1)}, u32[]{:S(2)}, u32[]{:S(2)}) collective-permute-start(f32[8,16,384]{2,1,0:T(8,128)S(1)} %fusion.1), channel_id=1, source_target_pairs={{0,64},{32,96},{64,0},{96,32},{1,65},{33,97},{65,1},{97,33},{2,66}... | collective-permute-start | bytes 589832 | tf_op jit(solution)/shard_map/ppermute | solution.py:24
  58.7 8.6 %copy-start.2 = (f32[2,12,8,384]{3,2,1,0:T(8,128)}, f32[2,12,8,384]{3,2,1,0:T(8,128)S(1)}, u32[]{:S(2)}) copy-start(f32[2,12,8,384]{3,2,1,0:T(8,128)S(1)} %collective-permute-done.4.cross_got_ref) | copy-start | bytes 884740
  59.7 7.6 %collective-permute-start.5 = (f32[12,8,384]{2,1,0:T(8,128)S(1)}, f32[12,8,384]{2,1,0:T(8,128)S(1)}, u32[]{:S(2)}, u32[]{:S(2)}) collective-permute-start(f32[12,8,384]{2,1,0:T(8,128)S(1)} %fusion.2), channel_id=1, source_target_pairs={{0,64},{32,96},{64,0},{96,32},{1,65},{33,97},{65,1},{97,33},{2,66}... | collective-permute-start | bytes 442376 | tf_op jit(solution)/shard_map/ppermute | solution.py:24
  64.5 2.8 %copy-start.3 = (f32[8,16,384]{2,1,0:T(8,128)}, f32[8,16,384]{2,1,0:T(8,128)S(1)}, u32[]{:S(2)}) copy-start(f32[8,16,384]{2,1,0:T(8,128)S(1)} %collective-permute-done.1.last_ref) | copy-start | bytes 589828
  67.3 0.7 copy-start.4
  69.9 29.6 %collective-permute-start.6 = (f32[3,8,384]{2,1,0:T(8,128)}, f32[3,8,384]{2,1,0:T(8,128)S(1)}, u32[]{:S(2)}, u32[]{:S(2)}) collective-permute-start(f32[3,8,384]{2,1,0:T(8,128)} %get-tuple-element.37), channel_id=1, source_target_pairs={{0,1},{1,0},{2,3},{3,2},{4,5},{5,4},{6,7},{7,6},{8,9},{9,8},{10,11... | collective-permute-start | bytes 110600 | tf_op jit(solution)/shard_map/ppermute | solution.py:19
  73.4 26.0 %collective-permute-start.7 = (f32[3,8,384]{2,1,0:T(8,128)}, f32[3,8,384]{2,1,0:T(8,128)S(1)}, u32[]{:S(2)}, u32[]{:S(2)}) collective-permute-start(f32[3,8,384]{2,1,0:T(8,128)} %get-tuple-element.38), channel_id=1, source_target_pairs={{1,2},{2,1},{3,4},{4,3},{5,6},{6,5},{7,8},{8,7},{9,10},{10,9},{11,... | collective-permute-start | bytes 110600 | tf_op jit(solution)/shard_map/ppermute | solution.py:19
  99.5 0.6 copy-start.5
  100.1 0.6 copy-start.6

commit v4 on v3

--- a/solution.py
+++ b/solution.py
@@ -9,6 +9,7 @@
 SCALE = 1.0 / 625.0
 LANES = 128
 PITCH = 24
+LIMIT = 67043328
 
 
 def paired(x, axis, first):
@@ -39,6 +40,13 @@
         )
         out.append(left + right)
     return out
+
+
+def inverse_total(weights_ref, rows):
+    total = weights_ref[0]
+    for i in range(1, weights_ref.shape[0]):
+        total += weights_ref[i]
+    return 1.0 / jnp.full((rows, LANES), total.astype(jnp.float32))
 
 
 def plus(a, b):
@@ -251,6 +259,8 @@
                 if part > 0:
                     seconds[which][at, base + (part - 1) * LANES : base + part * LANES] = value
 
+    inverse = inverse_total(share_ref, 1)
+
     def multiply(which):
         for window, ref in enumerate((firsts[which], seconds[which])):
             mixes[which][window] = jnp.dot(
@@ -264,7 +274,8 @@
         high = [mixed[1, at, lanes(0)], mixed[1, at, lanes(1)]]
         found = [low[0], low[1] + high[0], high[1]]
         blend = blend_ref[chan : chan + 1, :]
-        share = share_ref[jnp.minimum(step, last - 1) * both + which]
+        member = jnp.minimum(step, last - 1) * both + which
+        share = share_ref[place_ref[0] * (last * both) + member].astype(jnp.float32)
         factor = jnp.where(static, 0.25 * blend, share)
         for part in range(parts):
             far = at_distance(fields[which], part, chan, 4)
@@ -273,7 +284,7 @@
             state = jnp.where(static, 1.0, state)
             before = total[chan, :, lanes(part)]
             if which == 0:
-                before = jnp.where(static, 1.0 - blend, 1.0) * before
+                before = jnp.where(static, (1.0 - blend) * inverse, 1.0) * before
             total[chan, :, lanes(part)] = before + (factor * state) * value
 
     def gather_four(group, carry):
@@ -355,6 +366,7 @@
             jax.ShapeDtypeStruct((count, 8, chans, width), jnp.bfloat16),
             jax.ShapeDtypeStruct((8, chans, width), jnp.float32),
         ],
+        compiler_params=pltpu.CompilerParams(vmem_limit_bytes=LIMIT),
         name="own_part",
     )(place, share, members, control, blend, operators)
 
@@ -371,6 +383,7 @@
     lane = lax.broadcasted_iota(jnp.int32, (8, LANES), 1)
     final = step == pl.num_programs(0) - 1
     span = group * chans
+    first_member = (place_ref[0] * pl.num_programs(0) + step) * group
     sides = (
         (a_ref, a_control_ref, (0, 1), (0, 1, 2, 3)),
         (b_ref, b_control_ref, (0, 1), (4, 5, 6, 7)),
@@ -381,7 +394,7 @@
 
     for side, (halo, halo_control, order, own) in enumerate(sides):
         for one in range(group):
-            share = share_ref[step * group + one]
+            share = share_ref[first_member + one].astype(jnp.float32)
             at = slice(side * span + one * chans, side * span + (one + 1) * chans)
             below = slice(2 * span + at.start, 2 * span + at.stop)
             for part in range(parts):
@@ -430,7 +443,7 @@
                     control_ref[own[3], here, lanes(part)],
                 ]
                 for one in range(group):
-                    share = share_ref[step * group + one]
+                    share = share_ref[first_member + one].astype(jnp.float32)
                     start = side * span + one * chans + eight * 8
                     at = pl.ds(pl.multiple_of(start, 8), 8)
                     below = pl.ds(pl.multiple_of(2 * span + start, 8), 8)
@@ -468,6 +481,8 @@
 
     @pl.when(final)
     def _():
+        inverse = inverse_total(share_ref, 8)
+
         def finish(eight, carry):
             at = pl.ds(pl.multiple_of(eight * 8, 8), 8)
             slot = jnp.bitwise_xor(eight, place_ref[0])
@@ -483,7 +498,7 @@
                     place = side * 6 + i
                     for part in range(parts):
                         sums[place, at, lanes(part)] = SCALE * (
-                            (1.0 - blend) * sums[place, at, lanes(part)]
+                            ((1.0 - blend) * inverse) * sums[place, at, lanes(part)]
                             + (0.25 * blend) * value[part]
                         )
 
@@ -668,7 +683,7 @@
     even = lax.broadcasted_iota(jnp.int32, (8, LANES), 0) % 2 == 0
 
     def one(block, carry):
-        slot = slot_ref[block]
+        slot = slot_ref[pl.program_id(0) * blocks + block]
         windows = []
         for group in range(pairs // 8):
             parts = []
@@ -707,16 +722,20 @@
     lax.fori_loop(0, blocks, one, 0, unroll=4)
 
 
-def fine_part(slot, arrived, index, weight):
-    blocks, _, fine = index.shape
-    chans = arrived.shape[1] // 2
-    smem = pl.BlockSpec(memory_space=pltpu.SMEM)
-    vmem = pl.BlockSpec(memory_space=pltpu.VMEM)
+def fine_part(slot, arrived, index, weight, group):
+    blocks, lines, fine = index.shape
+    slots, pairs, width = arrived.shape
     return pl.pallas_call(
         fine_kernel,
-        in_specs=[smem, vmem, vmem, vmem],
-        out_specs=vmem,
-        out_shape=jax.ShapeDtypeStruct((blocks, chans, 2, fine), jnp.float32),
+        grid=(blocks // group,),
+        in_specs=[
+            pl.BlockSpec(memory_space=pltpu.SMEM),
+            pl.BlockSpec((slots, pairs, width), lambda i: (0, 0, 0)),
+            pl.BlockSpec((group, lines, fine), lambda i: (i, 0, 0)),
+            pl.BlockSpec((group, lines, fine), lambda i: (i, 0, 0)),
+        ],
+        out_specs=pl.BlockSpec((group, pairs // 2, 2, fine), lambda i: (i, 0, 0, 0)),
+        out_shape=jax.ShapeDtypeStruct((blocks, pairs // 2, 2, fine), jnp.float32),
         name="fine_part",
     )(slot, arrived, index, weight)
 
@@ -755,7 +774,7 @@
     column_source,
     column_code,
 ):
-    member_count, chans, row_count, width = members.shape
+    _, chans, row_count, width = members.shape
     spaces = lax.axis_size("space")
     space_index = lax.axis_index("space")
     member_slot = lax.axis_index("member")
@@ -772,10 +791,6 @@
     halo_b = paired(to_b, "space", 1)
     halo_a = paired(to_a, "space", 0)
 
-    weight_codes = member_weights.astype(jnp.float32)
-    share = lax.dynamic_slice_in_dim(
-        weight_codes, member_slot * member_count, member_count
-    ) / jnp.sum(weight_codes)
     blend = jnp.broadcast_to(hybrid_weight[:, None], (chans, LANES))
     source_index = source_device[:, 0]
     capacity = max(2, 2 * row_count // spaces)
@@ -791,14 +806,16 @@
     request = jnp.sum(jnp.where(taken, source_row[None, None, :], 0), axis=2)[:, None, :]
     index, weight = columns(column_source, column_code)
 
-    own_keep, own_give, near, control_near = own_part(place, share, members, control, blend)
+    own_keep, own_give, near, control_near = own_part(
+        place, member_weights, members, control, blend
+    )
     own_give, request = lax.optimization_barrier((own_give, request))
     asked = lax.all_to_all(request, "space", split_axis=0, concat_axis=0, tiled=True)
     own_got = swapped(own_give, "member", 1)
     own_last = swapped(own_keep[1] + own_got[1], "member", 2)
     near, index, weight, slot_index = lax.optimization_barrier((near, index, weight, slot_index))
 
-    keep, give = cross_part(place, share, halo_a, halo_b, near, control_near, blend, 4)
+    keep, give = cross_part(place, member_weights, halo_a, halo_b, near, control_near, blend, 4)
     got = swapped(give, "member", 1)
     last = swapped(keep[1] + got[1], "member", 2)
     back_a, back_b = sent_rows(place, own_keep, own_got, own_last, keep, got, last)
@@ -816,7 +833,7 @@
         concat_axis=0,
         tiled=True,
     ).reshape(spaces * capacity, pair_rows, width)
-    return fine_part(slot_index, arrived, index, weight)
+    return fine_part(slot_index, arrived, index, weight, 4)
 
 
 def solution(mesh):

time: 136 us -> 134 us (0.985)
  local copies, waits for them, and re-layouts: 4.26 us -> 2.56 us
    unnamed x24 -> x20, local copies, waits for them, and re-layouts: 3.59 us -> 1.88 us
  transfers between devices with their start and end apart: 8 -> 8, of which waited for: 3 -> 2; matrix products, arithmetic and copies ran while one was open for 4% -> 4% of each run, Pallas kernels for 30% -> 31%
where the time goes in v4:
time: 134 us
  Pallas kernels  56.9 us (42%)
  blocking collectives  52.9 us (39%)
  starting transfers between devices  10.6 us (8%)
  waiting for transfers between devices  5.86 us (4%)
  other arithmetic  4.85 us (4%)
  local copies, waits for them, and re-layouts  2.56 us (2%)
    pallas_call x1, Pallas kernels, own_part(): pl.pallas_call(own_kernel, grid_spec=pltpu.PrefetchScalarGridSpec(num_sca...  31.1 us
    all_to_all x1, blocking collectives, per_device(): lax.all_to_all(outgoing.reshape(spaces, capacity * pair_rows, width), 'sp...  27.5 us
    all_to_all x1, blocking collectives, per_device(): lax.all_to_all(request, 'space', split_axis=0, concat_axis=0, tiled=True)  25.4 us
    pallas_call x1, Pallas kernels, cross_part(): pl.pallas_call(cross_kernel, grid=(count // group,), in_specs=[pl.BlockSp...  8.65 us
    ppermute x4, starting transfers between devices, paired(): return lax.ppermute(x, axis, pairs)  6.53 us
    ppermute x4, waiting for transfers between devices, swapped(): return lax.ppermute(x, axis, [(i, i ^ bit) for i in range(length)])  5.84 us
    pallas_call x1, Pallas kernels, edge_rows(): pl.pallas_call(edges_kernel, grid=(count // group,), in_specs=[pl.BlockSp...  5.83 us
    pallas_call x1, Pallas kernels, fine_part(): pl.pallas_call(fine_kernel, grid=(blocks // group,), in_specs=[pl.BlockSp...  4.87 us
  transfers between devices with their start and end apart: 8, of which 2 were waited for; matrix products, arithmetic and copies ran while one was open for 4% of the time, Pallas kernels for 31%

profile of v4, /device:TPU:0, one launch (start us, length us, event | category | flops | bytes accessed | tf_op | source)
XLA Modules:
  0.0 133.8 jit_solution(3190254520513517438)
XLA Ops:
  0.0 0.6 pad_add_fusion.place_ref
  0.6 0.0 copy-start.7
  0.6 0.0 copy-start.9
  0.6 5.8 %edge_rows.1 = (f32[17,2,32,384]{3,2,1,0:T(8,128)}, f32[17,2,32,384]{3,2,1,0:T(8,128)}) custom-call(s32[4]{0:T(128)} %pad_add_fusion.place_ref, bf16[16,32,16,384]{3,2,1,0:T(8,128)(2,1)} %members_ref.3, f32[32,16,384]{2,1,0:T(8,128)} %control_ref.3), custom_call_target="tpu_custom_call" | custom-call | tf_op jit(solution)/shard_map/edge_rows/pallas_call | solution.py:113
  6.5 1.7 %collective-permute-start.2 = (f32[17,2,32,384]{3,2,1,0:T(8,128)}, f32[17,2,32,384]{3,2,1,0:T(8,128)}, u32[]{:S(2)}, u32[]{:S(2)}) collective-permute-start(f32[17,2,32,384]{3,2,1,0:T(8,128)} %get-tuple-element.31), channel_id=1, source_target_pairs={{0,1},{1,0},{2,3},{3,2},{4,5},{5,4},{6,7},{7,6},{8,9},{9,8},{10,11... | collective-permute-start | bytes 5013512 | tf_op jit(solution)/shard_map/ppermute | solution.py:20
  8.2 1.9 %collective-permute-start.3 = (f32[17,2,32,384]{3,2,1,0:T(8,128)}, f32[17,2,32,384]{3,2,1,0:T(8,128)}, u32[]{:S(2)}, u32[]{:S(2)}) collective-permute-start(f32[17,2,32,384]{3,2,1,0:T(8,128)} %get-tuple-element.32), channel_id=1, source_target_pairs={{1,2},{2,1},{3,4},{4,3},{5,6},{6,5},{7,8},{8,7},{9,10},{10,9},{11,... | collective-permute-start | bytes 5013512 | tf_op jit(solution)/shard_map/ppermute | solution.py:20
  10.1 0.0 copy-done.7
  10.1 0.1 fusion.3
  10.1 0.6 reduce_window_sum.11
  10.8 0.0 copy-done.9
  10.8 0.7 broadcast_in_dim.12.blend_ref
  11.4 31.1 %own_part.1 = (f32[2,8,16,384]{3,2,1,0:T(8,128)}, f32[2,8,16,384]{3,2,1,0:T(8,128)}, bf16[16,8,32,384]{3,2,1,0:T(8,128)(2,1)}, f32[8,32,384]{2,1,0:T(8,128)}) custom-call(s32[4]{0:T(128)} %pad_add_fusion.place_ref, s32[64]{0:T(128)} %share_ref.3, bf16[16,32,16,384]{3,2,1,0:T(8,128)(2,1)} %members_ref.3, f32[32,16,384]{2,1,0:T(8,128)} %control_ref.3, ...), custom_call_target="tpu_custom_call" | custom-call | tf_op jit(solution)/shard_map/own_part/pallas_call | solution.py:332
  42.5 0.9 select_reduce_fusion.1
  43.4 0.7 multiply_add_fusion.slot_ref
  44.1 0.0 copy-start.8
  44.1 0.1 broadcast_subtract_fusion
  44.2 0.8 select_reduce_fusion
  45.0 0.1 collective-permute-start
  45.1 1.8 %columns.1 = (s32[16,8,768]{2,1,0:T(8,128)}, f32[16,8,768]{2,1,0:T(8,128)}) custom-call(s32[16,768]{1,0:T(8,128)} %source_ref.1, s32[16,768]{1,0:T(8,128)} %code_ref.1), custom_call_target="tpu_custom_call" | custom-call | tf_op jit(solution)/shard_map/columns/pallas_call | solution.py:757
  46.9 0.0 collective-permute-done.2.a_ref.a_control_ref
  46.9 0.0 collective-permute-done.3.b_ref.b_control_ref
  46.9 0.0 copy-start
  46.9 8.6 %cross_part.1 = (f32[2,12,8,384]{3,2,1,0:T(8,128)}, f32[2,12,8,384]{3,2,1,0:T(8,128)}) custom-call(s32[4]{0:T(128)} %pad_add_fusion.place_ref, s32[64]{0:T(128)} %share_ref.3, f32[17,2,32,384]{3,2,1,0:T(8,128)} %collective-permute-done.2.a_ref.a_control_ref, f32[17,2,32,384]{3,2,1,0:T(8,128)} %collective-permute-done.2.a_ref.a_control_ref, ...), custom_call_target="tpu_custom_call" | custom-call | tf_op jit(solution)/shard_map/cross_part/pallas_call | solution.py:528
  55.6 0.0 copy-done.8
  55.6 0.6 collective-permute-start.4
  56.2 0.0 collective-permute-done.got_ref
  56.2 0.0 copy-start.1
  56.2 0.0 copy-done
  56.2 2.0 %collective-permute-start.1 = (f32[8,16,384]{2,1,0:T(8,128)S(1)}, f32[8,16,384]{2,1,0:T(8,128)S(1)}, u32[]{:S(2)}, u32[]{:S(2)}) collective-permute-start(f32[8,16,384]{2,1,0:T(8,128)S(1)} %fusion.1), channel_id=1, source_target_pairs={{0,64},{32,96},{64,0},{96,32},{1,65},{33,97},{65,1},{97,33},{2,66}... | collective-permute-start | bytes 589832 | tf_op jit(solution)/shard_map/ppermute | solution.py:25
  58.2 0.0 collective-permute-done.4.cross_got_ref
  58.2 0.0 copy-start.2
  58.2 1.0 fusion.2
  59.2 1.4 %collective-permute-start.5 = (f32[12,8,384]{2,1,0:T(8,128)S(1)}, f32[12,8,384]{2,1,0:T(8,128)S(1)}, u32[]{:S(2)}, u32[]{:S(2)}) collective-permute-start(f32[12,8,384]{2,1,0:T(8,128)S(1)} %fusion.2), channel_id=1, source_target_pairs={{0,64},{32,96},{64,0},{96,32},{1,65},{33,97},{65,1},{97,33},{2,66}... | collective-permute-start | bytes 442376 | tf_op jit(solution)/shard_map/ppermute | solution.py:25
  60.6 3.4 %collective-permute-done.1.last_ref = f32[8,16,384]{2,1,0:T(8,128)S(1)} collective-permute-done((f32[8,16,384]{2,1,0:T(8,128)S(1)}, f32[8,16,384]{2,1,0:T(8,128)S(1)}, u32[]{:S(2)}, u32[]{:S(2)}) %collective-permute-start.1) | collective-permute-done | bytes 196640 | tf_op jit(solution)/shard_map/ppermute | solution.py:25
  64.0 0.0 copy-start.3
  64.1 2.4 %collective-permute-done.5.cross_last_ref = f32[12,8,384]{2,1,0:T(8,128)S(1)} collective-permute-done((f32[12,8,384]{2,1,0:T(8,128)S(1)}, f32[12,8,384]{2,1,0:T(8,128)S(1)}, u32[]{:S(2)}, u32[]{:S(2)}) %collective-permute-start.5) | collective-permute-done | bytes 147488 | tf_op jit(solution)/shard_map/ppermute | solution.py:25
  66.4 0.0 copy-done.1
  66.4 0.0 copy-done.2
  66.5 0.0 copy-done.3
  66.5 0.0 copy-start.4
  66.5 0.6 copy-done.4
  67.1 1.9 %sent_rows.1 = (f32[3,8,384]{2,1,0:T(8,128)}, f32[3,8,384]{2,1,0:T(8,128)}) custom-call(s32[4]{0:T(128)} %pad_add_fusion.place_ref, f32[2,8,16,384]{3,2,1,0:T(8,128)} %get-tuple-element.29.own_ref, f32[2,8,16,384]{3,2,1,0:T(8,128)} %copy-done.1, f32[8,16,384]{2,1,0:T(8,128)} %copy-done.3, f32[2,12,8,384]{3,2,1,0:T(8,128)} %get-tuple-element.35.cross_ref, ...), custom_call_target="tpu_custom_call" | custom-call | tf_op jit(solution)/shard_map/sent_rows/pallas_call | solution.py:584
  69.1 2.3 %collective-permute-start.6 = (f32[3,8,384]{2,1,0:T(8,128)}, f32[3,8,384]{2,1,0:T(8,128)S(1)}, u32[]{:S(2)}, u32[]{:S(2)}) collective-permute-start(f32[3,8,384]{2,1,0:T(8,128)} %get-tuple-element.37), channel_id=1, source_target_pairs={{0,1},{1,0},{2,3},{3,2},{4,5},{5,4},{6,7},{7,6},{8,9},{9,8},{10,11... | collective-permute-start | bytes 110600 | tf_op jit(solution)/shard_map/ppermute | solution.py:20
  71.4 0.7 collective-permute-start.7
  72.0 25.4 %all_to_all.10.asked_ref = s32[32,1,128]{2,1,0:T(1,128)} all-to-all(s32[32,1,128]{2,1,0:T(1,128)S(1)} %bitcast.15), channel_id=1, replica_groups=mesh['member'=4,'space'=32] {'space'}, dimensions={0} | all-to-all | bytes 32768 | tf_op jit(solution)/shard_map/all_to_all | solution.py:813
  97.4 0.0 collective-permute-done.6.a_ref
  97.4 0.0 copy-start.5
  97.4 0.0 collective-permute-done.7.b_ref
  97.4 0.6 copy-done.5
  98.0 0.0 copy-start.6
  98.0 0.6 copy-done.6
  98.7 2.7 %answers.1 = f32[64,16,384]{2,1,0:T(8,128)} custom-call(s32[4]{0:T(128)} %pad_add_fusion.place_ref, s32[32,1,128]{2,1,0:T(1,128)} %all_to_all.10.asked_ref, f32[2,8,16,384]{3,2,1,0:T(8,128)} %get-tuple-element.29.own_ref, f32[2,8,16,384]{3,2,1,0:T(8,128)} %copy-done.1, f32[8,16,384]{2,1,0:T(8,128)} %copy-done.3, ...), custom_call_target="tpu_custom_call" | custom-call | tf_op jit(solution)/shard_map/answers/pallas_call | solution.py:662
  101.4 27.5 %all_to_all.11 = f32[32,32,384]{2,1,0:T(8,128)} all-to-all(f32[32,32,384]{2,1,0:T(8,128)} %bitcast.13), channel_id=1, replica_groups=mesh['member'=4,'space'=32] {'space'}, dimensions={0} | all-to-all | bytes 3145728 | tf_op jit(solution)/shard_map/all_to_all | solution.py:829
  128.9 4.9 %fine_part.1 = f32[16,8,2,768]{3,2,1,0:T(2,128)} custom-call(s32[16]{0:T(128)} %copy-done.8, f32[64,16,384]{2,1,0:T(8,128)} %bitcast.14, s32[16,8,768]{2,1,0:T(8,128)} %get-tuple-element.39.index_ref, f32[16,8,768]{2,1,0:T(8,128)} %get-tuple-element.40.weight_ref), custom_call_target="tpu_custom_call" | custom-call | tf_op jit(solution)/shard_map/fine_part/pallas_call | solution.py:728
  (3 shorter events, 0.0 us)
Async XLA Ops:
  0.6 9.4 %copy-start.7 = (s32[16,1]{0,1:T(1,128)S(1)}, s32[16,1]{0,1:T(1,128)}, u32[]{:S(2)}) copy-start(s32[16,1]{0,1:T(1,128)} %param.15) | copy-start | bytes 196
  0.6 10.1 %copy-start.9 = (f32[32]{0:T(128)S(1)}, f32[32]{0:T(128)}, u32[]{:S(2)}) copy-start(f32[32]{0:T(128)} %param.13) | copy-start | bytes 388
  6.5 40.4 %collective-permute-start.2 = (f32[17,2,32,384]{3,2,1,0:T(8,128)}, f32[17,2,32,384]{3,2,1,0:T(8,128)}, u32[]{:S(2)}, u32[]{:S(2)}) collective-permute-start(f32[17,2,32,384]{3,2,1,0:T(8,128)} %get-tuple-element.31), channel_id=1, source_target_pairs={{0,1},{1,0},{2,3},{3,2},{4,5},{5,4},{6,7},{7,6},{8,9},{9,8},{10,11... | collective-permute-start | bytes 5013512 | tf_op jit(solution)/shard_map/ppermute | solution.py:20
  8.2 38.7 %collective-permute-start.3 = (f32[17,2,32,384]{3,2,1,0:T(8,128)}, f32[17,2,32,384]{3,2,1,0:T(8,128)}, u32[]{:S(2)}, u32[]{:S(2)}) collective-permute-start(f32[17,2,32,384]{3,2,1,0:T(8,128)} %get-tuple-element.32), channel_id=1, source_target_pairs={{1,2},{2,1},{3,4},{4,3},{5,6},{6,5},{7,8},{8,7},{9,10},{10,9},{11,... | collective-permute-start | bytes 5013512 | tf_op jit(solution)/shard_map/ppermute | solution.py:20
  44.1 11.5 %copy-start.8 = (s32[16]{0:T(128)}, s32[16]{0:T(128)S(1)}, u32[]{:S(2)}) copy-start(s32[16]{0:T(128)S(1)} %multiply_add_fusion.slot_ref) | copy-start | bytes 196
  45.0 11.2 %collective-permute-start = (f32[2,8,16,384]{3,2,1,0:T(8,128)}, f32[2,8,16,384]{3,2,1,0:T(8,128)S(1)}, u32[]{:S(2)}, u32[]{:S(2)}) collective-permute-start(f32[2,8,16,384]{3,2,1,0:T(8,128)} %get-tuple-element.30), channel_id=1, source_target_pairs={{0,32},{32,0},{64,96},{96,64},{1,33},{33,1},{65,97},{97,65},{2,34}... | collective-permute-start | bytes 1179656 | tf_op jit(solution)/shard_map/ppermute | solution.py:25
  46.9 9.3 %copy-start = (f32[2,8,16,384]{3,2,1,0:T(8,128)S(1)}, f32[2,8,16,384]{3,2,1,0:T(8,128)}, u32[]{:S(2)}) copy-start(f32[2,8,16,384]{3,2,1,0:T(8,128)} %get-tuple-element.29.own_ref) | copy-start | bytes 1179652
  55.6 2.6 %collective-permute-start.4 = (f32[2,12,8,384]{3,2,1,0:T(8,128)}, f32[2,12,8,384]{3,2,1,0:T(8,128)S(1)}, u32[]{:S(2)}, u32[]{:S(2)}) collective-permute-start(f32[2,12,8,384]{3,2,1,0:T(8,128)} %get-tuple-element.36), channel_id=1, source_target_pairs={{0,32},{32,0},{64,96},{96,64},{1,33},{33,1},{65,97},{97,65},{2,34}... | collective-permute-start | bytes 884744 | tf_op jit(solution)/shard_map/ppermute | solution.py:25
  56.2 10.3 %copy-start.1 = (f32[2,8,16,384]{3,2,1,0:T(8,128)}, f32[2,8,16,384]{3,2,1,0:T(8,128)S(1)}, u32[]{:S(2)}) copy-start(f32[2,8,16,384]{3,2,1,0:T(8,128)S(1)} %collective-permute-done.got_ref) | copy-start | bytes 1179652
  56.2 7.9 %collective-permute-start.1 = (f32[8,16,384]{2,1,0:T(8,128)S(1)}, f32[8,16,384]{2,1,0:T(8,128)S(1)}, u32[]{:S(2)}, u32[]{:S(2)}) collective-permute-start(f32[8,16,384]{2,1,0:T(8,128)S(1)} %fusion.1), channel_id=1, source_target_pairs={{0,64},{32,96},{64,0},{96,32},{1,65},{33,97},{65,1},{97,33},{2,66}... | collective-permute-start | bytes 589832 | tf_op jit(solution)/shard_map/ppermute | solution.py:25
  58.2 8.3 %copy-start.2 = (f32[2,12,8,384]{3,2,1,0:T(8,128)}, f32[2,12,8,384]{3,2,1,0:T(8,128)S(1)}, u32[]{:S(2)}) copy-start(f32[2,12,8,384]{3,2,1,0:T(8,128)S(1)} %collective-permute-done.4.cross_got_ref) | copy-start | bytes 884740
  59.2 7.2 %collective-permute-start.5 = (f32[12,8,384]{2,1,0:T(8,128)S(1)}, f32[12,8,384]{2,1,0:T(8,128)S(1)}, u32[]{:S(2)}, u32[]{:S(2)}) collective-permute-start(f32[12,8,384]{2,1,0:T(8,128)S(1)} %fusion.2), channel_id=1, source_target_pairs={{0,64},{32,96},{64,0},{96,32},{1,65},{33,97},{65,1},{97,33},{2,66}... | collective-permute-start | bytes 442376 | tf_op jit(solution)/shard_map/ppermute | solution.py:25
  64.0 2.4 %copy-start.3 = (f32[8,16,384]{2,1,0:T(8,128)}, f32[8,16,384]{2,1,0:T(8,128)S(1)}, u32[]{:S(2)}) copy-start(f32[8,16,384]{2,1,0:T(8,128)S(1)} %collective-permute-done.1.last_ref) | copy-start | bytes 589828
  66.5 0.7 copy-start.4
  69.1 28.4 %collective-permute-start.6 = (f32[3,8,384]{2,1,0:T(8,128)}, f32[3,8,384]{2,1,0:T(8,128)S(1)}, u32[]{:S(2)}, u32[]{:S(2)}) collective-permute-start(f32[3,8,384]{2,1,0:T(8,128)} %get-tuple-element.37), channel_id=1, source_target_pairs={{0,1},{1,0},{2,3},{3,2},{4,5},{5,4},{6,7},{7,6},{8,9},{9,8},{10,11... | collective-permute-start | bytes 110600 | tf_op jit(solution)/shard_map/ppermute | solution.py:20
  71.4 26.1 %collective-permute-start.7 = (f32[3,8,384]{2,1,0:T(8,128)}, f32[3,8,384]{2,1,0:T(8,128)S(1)}, u32[]{:S(2)}, u32[]{:S(2)}) collective-permute-start(f32[3,8,384]{2,1,0:T(8,128)} %get-tuple-element.38), channel_id=1, source_target_pairs={{1,2},{2,1},{3,4},{4,3},{5,6},{6,5},{7,8},{8,7},{9,10},{10,9},{11,... | collective-permute-start | bytes 110600 | tf_op jit(solution)/shard_map/ppermute | solution.py:20
  97.4 0.6 copy-start.5
  98.0 0.6 copy-start.6

commit v5 on v4

--- a/solution.py
+++ b/solution.py
@@ -1,3 +1,5 @@
+import functools
+
 import jax
 import jax.numpy as jnp
 import numpy as np
@@ -740,6 +742,33 @@
     )(slot, arrived, index, weight)
 
 
+def request_kernel(device_ref, row_ref, slot_ref, request_ref, *, capacity):
+    blocks = device_ref.shape[0]
+    lane = lax.broadcasted_iota(jnp.int32, (1, LANES), 1)
+    request_ref[...] = jnp.zeros(request_ref.shape, jnp.int32)
+    for block in range(blocks):
+        device = device_ref[block]
+        rank = jnp.int32(0)
+        for earlier in range(block):
+            rank += (device_ref[earlier] == device).astype(jnp.int32)
+        slot_ref[block] = device * capacity + rank
+        request_ref[device] = jnp.where(lane == rank, row_ref[block], request_ref[device])
+
+
+def requests(device, row, spaces, capacity):
+    smem = pl.BlockSpec(memory_space=pltpu.SMEM)
+    return pl.pallas_call(
+        functools.partial(request_kernel, capacity=capacity),
+        in_specs=[smem, smem],
+        out_specs=[smem, pl.BlockSpec(memory_space=pltpu.VMEM)],
+        out_shape=[
+            jax.ShapeDtypeStruct(device.shape, jnp.int32),
+            jax.ShapeDtypeStruct((spaces, 1, LANES), jnp.int32),
+        ],
+        name="requests",
+    )(device, row)
+
+
 def column_kernel(source_ref, code_ref, index_ref, weight_ref):
     blocks, fine = source_ref.shape
     column = lax.broadcasted_iota(jnp.int32, (1, fine), 1)
@@ -787,23 +816,14 @@
             space_index % 2,
         ]
     ).astype(jnp.int32)
-    to_a, to_b = edge_rows(place, members, control, 4)
+    to_a, to_b = edge_rows(place, members, control, 2)
     halo_b = paired(to_b, "space", 1)
     halo_a = paired(to_a, "space", 0)
 
     blend = jnp.broadcast_to(hybrid_weight[:, None], (chans, LANES))
     source_index = source_device[:, 0]
     capacity = max(2, 2 * row_count // spaces)
-    chosen = (source_index[:, None] == jnp.arange(spaces, dtype=jnp.int32)[None, :]).astype(
-        jnp.int32
-    )
-    earlier = jnp.cumsum(chosen, axis=0) - chosen
-    rank_within = jnp.sum(earlier * chosen, axis=1)
-    slot_index = source_index * capacity + rank_within
-    spread = slot_index[None, :] - capacity * jnp.arange(spaces, dtype=jnp.int32)[:, None]
-    lane = jnp.arange(LANES, dtype=jnp.int32)
-    taken = (spread[:, None, :] == lane[None, :, None]) & (lane < capacity)[None, :, None]
-    request = jnp.sum(jnp.where(taken, source_row[None, None, :], 0), axis=2)[:, None, :]
+    slot_index, request = requests(source_index, source_row, spaces, capacity)
     index, weight = columns(column_source, column_code)
 
     own_keep, own_give, near, control_near = own_part(
@@ -833,7 +853,7 @@
         concat_axis=0,
         tiled=True,
     ).reshape(spaces * capacity, pair_rows, width)
-    return fine_part(slot_index, arrived, index, weight, 4)
+    return fine_part(slot_index, arrived, index, weight, 16)
 
 
 def solution(mesh):

time: 134 us -> 136 us (1.015)
  other arithmetic: 4.85 us -> 1.67 us
  Pallas kernels: 56.9 us -> 59.8 us
  starting transfers between devices: 10.6 us -> 12.3 us
    pallas_call x1, Pallas kernels: 5.83 us -> 7.63 us  [edge_rows(): pl.pallas_call(edges_kernel, grid=(count // group,), in_specs=[pl.BlockSp...]
    ppermute x4, starting transfers between devices: 6.53 us -> 8.3 us  [paired(): return lax.ppermute(x, axis, pairs)]
    reduce_sum x2 -> x0, other arithmetic: 1.72 us -> none  [the longest x1 0.88 us: per_device(): rank_within = jnp.sum(earlier * chosen, axis=1)]
    pallas_call x0 -> x1, Pallas kernels: none -> 1.43 us  [requests(): pl.pallas_call(functools.partial(request_kernel, capacity=capacity), in_s...]
  transfers between devices with their start and end apart: 8 -> 8, of which waited for: 2 -> 2; matrix products, arithmetic and copies ran while one was open for 4% -> 1% of each run, Pallas kernels for 31% -> 32%
where the time goes in v5:
time: 136 us; the launch traced here: 135 us
  Pallas kernels  59.8 us (44%)
  blocking collectives  52.9 us (39%)
  starting transfers between devices  12.3 us (9%)
  waiting for transfers between devices  5.91 us (4%)
  local copies, waits for them, and re-layouts  2.54 us (2%)
  other arithmetic  1.67 us (1%)
    pallas_call x1, Pallas kernels, own_part(): pl.pallas_call(own_kernel, grid_spec=pltpu.PrefetchScalarGridSpec(num_sca...  31.1 us
    all_to_all x1, blocking collectives, per_device(): lax.all_to_all(outgoing.reshape(spaces, capacity * pair_rows, width), 'sp...  27.5 us
    all_to_all x1, blocking collectives, per_device(): lax.all_to_all(request, 'space', split_axis=0, concat_axis=0, tiled=True)  25.4 us
    pallas_call x1, Pallas kernels, cross_part(): pl.pallas_call(cross_kernel, grid=(count // group,), in_specs=[pl.BlockSp...  8.64 us
    ppermute x4, starting transfers between devices, paired(): return lax.ppermute(x, axis, pairs)  8.3 us
    pallas_call x1, Pallas kernels, edge_rows(): pl.pallas_call(edges_kernel, grid=(count // group,), in_specs=[pl.BlockSp...  7.63 us
    ppermute x4, waiting for transfers between devices, swapped(): return lax.ppermute(x, axis, [(i, i ^ bit) for i in range(length)])  5.9 us
    pallas_call x1, Pallas kernels, fine_part(): pl.pallas_call(fine_kernel, grid=(blocks // group,), in_specs=[pl.BlockSp...  4.48 us
  transfers between devices with their start and end apart: 8, of which 2 were waited for; matrix products, arithmetic and copies ran while one was open for 1% of the time, Pallas kernels for 32%

profile of v5, /device:TPU:0, one launch (start us, length us, event | category | flops | bytes accessed | tf_op | source)
XLA Modules:
  0.0 135.1 jit_solution(12105837312182719192)
XLA Ops:
  0.0 0.6 pad_add_fusion.place_ref
  0.6 0.0 copy-start.8
  0.6 7.6 %edge_rows.1 = (f32[17,2,32,384]{3,2,1,0:T(8,128)}, f32[17,2,32,384]{3,2,1,0:T(8,128)}) custom-call(s32[4]{0:T(128)} %pad_add_fusion.place_ref, bf16[16,32,16,384]{3,2,1,0:T(8,128)(2,1)} %members_ref.3, f32[32,16,384]{2,1,0:T(8,128)} %control_ref.3), custom_call_target="tpu_custom_call" | custom-call | tf_op jit(solution)/shard_map/edge_rows/pallas_call | solution.py:115
  8.3 1.7 %collective-permute-start.2 = (f32[17,2,32,384]{3,2,1,0:T(8,128)}, f32[17,2,32,384]{3,2,1,0:T(8,128)}, u32[]{:S(2)}, u32[]{:S(2)}) collective-permute-start(f32[17,2,32,384]{3,2,1,0:T(8,128)} %get-tuple-element.35), channel_id=1, source_target_pairs={{0,1},{1,0},{2,3},{3,2},{4,5},{5,4},{6,7},{7,6},{8,9},{9,8},{10,11... | collective-permute-start | bytes 5013512 | tf_op jit(solution)/shard_map/ppermute | solution.py:22
  9.9 1.9 %collective-permute-start.3 = (f32[17,2,32,384]{3,2,1,0:T(8,128)}, f32[17,2,32,384]{3,2,1,0:T(8,128)}, u32[]{:S(2)}, u32[]{:S(2)}) collective-permute-start(f32[17,2,32,384]{3,2,1,0:T(8,128)} %get-tuple-element.36), channel_id=1, source_target_pairs={{1,2},{2,1},{3,4},{4,3},{5,6},{6,5},{7,8},{8,7},{9,10},{10,9},{11,... | collective-permute-start | bytes 5013512 | tf_op jit(solution)/shard_map/ppermute | solution.py:22
  11.8 1.4 %requests.1 = (s32[16]{0:T(128)}, s32[32,1,128]{2,1,0:T(1,128)}) custom-call(s32[16]{0:T(128)} %bitcast.13, s32[16]{0:T(128)} %row_ref.1), custom_call_target="tpu_custom_call" | custom-call | tf_op jit(solution)/shard_map/requests/pallas_call | solution.py:760
  13.3 0.0 copy-done.8
  13.3 0.7 broadcast_in_dim.2.blend_ref
  14.0 31.1 %own_part.1 = (f32[2,8,16,384]{3,2,1,0:T(8,128)}, f32[2,8,16,384]{3,2,1,0:T(8,128)}, bf16[16,8,32,384]{3,2,1,0:T(8,128)(2,1)}, f32[8,32,384]{2,1,0:T(8,128)}) custom-call(s32[4]{0:T(128)} %pad_add_fusion.place_ref, s32[64]{0:T(128)} %share_ref.3, bf16[16,32,16,384]{3,2,1,0:T(8,128)(2,1)} %members_ref.3, f32[32,16,384]{2,1,0:T(8,128)} %control_ref.3, ...), custom_call_target="tpu_custom_call" | custom-call | tf_op jit(solution)/shard_map/own_part/pallas_call | solution.py:334
  45.1 0.0 collective-permute-start
  45.1 1.8 %columns.1 = (s32[16,8,768]{2,1,0:T(8,128)}, f32[16,8,768]{2,1,0:T(8,128)}) custom-call(s32[16,768]{1,0:T(8,128)} %source_ref.1, s32[16,768]{1,0:T(8,128)} %code_ref.1), custom_call_target="tpu_custom_call" | custom-call | tf_op jit(solution)/shard_map/columns/pallas_call | solution.py:786
  46.9 0.0 collective-permute-done.2.a_ref.a_control_ref
  46.9 0.0 collective-permute-done.3.b_ref.b_control_ref
  46.9 0.0 copy-start
  46.9 8.6 %cross_part.1 = (f32[2,12,8,384]{3,2,1,0:T(8,128)}, f32[2,12,8,384]{3,2,1,0:T(8,128)}) custom-call(s32[4]{0:T(128)} %pad_add_fusion.place_ref, s32[64]{0:T(128)} %share_ref.3, f32[17,2,32,384]{3,2,1,0:T(8,128)} %collective-permute-done.2.a_ref.a_control_ref, f32[17,2,32,384]{3,2,1,0:T(8,128)} %collective-permute-done.2.a_ref.a_control_ref, ...), custom_call_target="tpu_custom_call" | custom-call | tf_op jit(solution)/shard_map/cross_part/pallas_call | solution.py:530
  55.5 0.0 copy-start.7
  55.5 0.6 collective-permute-start.4
  56.1 0.0 collective-permute-done.got_ref
  56.1 0.0 copy-start.1
  56.1 0.0 copy-done
  56.2 2.0 %collective-permute-start.1 = (f32[8,16,384]{2,1,0:T(8,128)S(1)}, f32[8,16,384]{2,1,0:T(8,128)S(1)}, u32[]{:S(2)}, u32[]{:S(2)}) collective-permute-start(f32[8,16,384]{2,1,0:T(8,128)S(1)} %fusion), channel_id=1, source_target_pairs={{0,64},{32,96},{64,0},{96,32},{1,65},{33,97},{65,1},{97,33},{2,66}... | collective-permute-start | bytes 589832 | tf_op jit(solution)/shard_map/ppermute | solution.py:27
  58.2 0.0 collective-permute-done.4.cross_got_ref
  58.2 0.0 copy-start.2
  58.2 1.0 fusion.1
  59.2 1.4 %collective-permute-start.5 = (f32[12,8,384]{2,1,0:T(8,128)S(1)}, f32[12,8,384]{2,1,0:T(8,128)S(1)}, u32[]{:S(2)}, u32[]{:S(2)}) collective-permute-start(f32[12,8,384]{2,1,0:T(8,128)S(1)} %fusion.1), channel_id=1, source_target_pairs={{0,64},{32,96},{64,0},{96,32},{1,65},{33,97},{65,1},{97,33},{2,66}... | collective-permute-start | bytes 442376 | tf_op jit(solution)/shard_map/ppermute | solution.py:27
  60.6 3.4 %collective-permute-done.1.last_ref = f32[8,16,384]{2,1,0:T(8,128)S(1)} collective-permute-done((f32[8,16,384]{2,1,0:T(8,128)S(1)}, f32[8,16,384]{2,1,0:T(8,128)S(1)}, u32[]{:S(2)}, u32[]{:S(2)}) %collective-permute-start.1) | collective-permute-done | bytes 196640 | tf_op jit(solution)/shard_map/ppermute | solution.py:27
  64.0 0.0 copy-start.3
  64.0 2.5 %collective-permute-done.5.cross_last_ref = f32[12,8,384]{2,1,0:T(8,128)S(1)} collective-permute-done((f32[12,8,384]{2,1,0:T(8,128)S(1)}, f32[12,8,384]{2,1,0:T(8,128)S(1)}, u32[]{:S(2)}, u32[]{:S(2)}) %collective-permute-start.5) | collective-permute-done | bytes 147488 | tf_op jit(solution)/shard_map/ppermute | solution.py:27
  66.5 0.0 copy-done.1
  66.5 0.0 copy-done.2
  66.5 0.0 copy-done.3
  66.5 0.0 copy-start.4
  66.5 0.6 copy-done.4
  67.1 1.9 %sent_rows.1 = (f32[3,8,384]{2,1,0:T(8,128)}, f32[3,8,384]{2,1,0:T(8,128)}) custom-call(s32[4]{0:T(128)} %pad_add_fusion.place_ref, f32[2,8,16,384]{3,2,1,0:T(8,128)} %get-tuple-element.33.own_ref, f32[2,8,16,384]{3,2,1,0:T(8,128)} %copy-done.1, f32[8,16,384]{2,1,0:T(8,128)} %copy-done.3, f32[2,12,8,384]{3,2,1,0:T(8,128)} %get-tuple-element.39.cross_ref, ...), custom_call_target="tpu_custom_call" | custom-call | tf_op jit(solution)/shard_map/sent_rows/pallas_call | solution.py:586
  69.1 4.1 %collective-permute-start.6 = (f32[3,8,384]{2,1,0:T(8,128)}, f32[3,8,384]{2,1,0:T(8,128)S(1)}, u32[]{:S(2)}, u32[]{:S(2)}) collective-permute-start(f32[3,8,384]{2,1,0:T(8,128)} %get-tuple-element.41), channel_id=1, source_target_pairs={{0,1},{1,0},{2,3},{3,2},{4,5},{5,4},{6,7},{7,6},{8,9},{9,8},{10,11... | collective-permute-start | bytes 110600 | tf_op jit(solution)/shard_map/ppermute | solution.py:22
  73.1 0.7 collective-permute-start.7
  73.8 0.0 copy-done.7
  73.8 25.4 %all_to_all.10.asked_ref = s32[32,1,128]{2,1,0:T(1,128)} all-to-all(s32[32,1,128]{2,1,0:T(1,128)S(1)} %copy-done.7), channel_id=1, replica_groups=mesh['member'=4,'space'=32] {'space'}, dimensions={0} | all-to-all | bytes 32768 | tf_op jit(solution)/shard_map/all_to_all | solution.py:833
  99.2 0.0 collective-permute-done.6.a_ref
  99.2 0.0 copy-start.5
  99.2 0.0 collective-permute-done.7.b_ref
  99.2 0.6 copy-done.5
  99.8 0.0 copy-start.6
  99.8 0.6 copy-done.6
  100.4 2.7 %answers.1 = f32[64,16,384]{2,1,0:T(8,128)} custom-call(s32[4]{0:T(128)} %pad_add_fusion.place_ref, s32[32,1,128]{2,1,0:T(1,128)} %all_to_all.10.asked_ref, f32[2,8,16,384]{3,2,1,0:T(8,128)} %get-tuple-element.33.own_ref, f32[2,8,16,384]{3,2,1,0:T(8,128)} %copy-done.1, f32[8,16,384]{2,1,0:T(8,128)} %copy-done.3, ...), custom_call_target="tpu_custom_call" | custom-call | tf_op jit(solution)/shard_map/answers/pallas_call | solution.py:664
  103.1 27.5 %all_to_all.11 = f32[32,32,384]{2,1,0:T(8,128)} all-to-all(f32[32,32,384]{2,1,0:T(8,128)} %bitcast.11), channel_id=1, replica_groups=mesh['member'=4,'space'=32] {'space'}, dimensions={0} | all-to-all | bytes 3145728 | tf_op jit(solution)/shard_map/all_to_all | solution.py:849
  130.6 4.5 %fine_part.1 = f32[16,8,2,768]{3,2,1,0:T(2,128)} custom-call(s32[16]{0:T(128)} %get-tuple-element.29.slot_ref, f32[64,16,384]{2,1,0:T(8,128)} %bitcast.12, s32[16,8,768]{2,1,0:T(8,128)} %get-tuple-element.43.index_ref, f32[16,8,768]{2,1,0:T(8,128)} %get-tuple-element.44.weight_ref), custom_call_target="tpu_custom_call" | custom-call | tf_op jit(solution)/shard_map/fine_part/pallas_call | solution.py:730
  (1 shorter events, 0.0 us)
Async XLA Ops:
  0.6 12.7 %copy-start.8 = (f32[32]{0:T(128)S(1)}, f32[32]{0:T(128)}, u32[]{:S(2)}) copy-start(f32[32]{0:T(128)} %param.13) | copy-start | bytes 388
  8.3 38.6 %collective-permute-start.2 = (f32[17,2,32,384]{3,2,1,0:T(8,128)}, f32[17,2,32,384]{3,2,1,0:T(8,128)}, u32[]{:S(2)}, u32[]{:S(2)}) collective-permute-start(f32[17,2,32,384]{3,2,1,0:T(8,128)} %get-tuple-element.35), channel_id=1, source_target_pairs={{0,1},{1,0},{2,3},{3,2},{4,5},{5,4},{6,7},{7,6},{8,9},{9,8},{10,11... | collective-permute-start | bytes 5013512 | tf_op jit(solution)/shard_map/ppermute | solution.py:22
  9.9 36.9 %collective-permute-start.3 = (f32[17,2,32,384]{3,2,1,0:T(8,128)}, f32[17,2,32,384]{3,2,1,0:T(8,128)}, u32[]{:S(2)}, u32[]{:S(2)}) collective-permute-start(f32[17,2,32,384]{3,2,1,0:T(8,128)} %get-tuple-element.36), channel_id=1, source_target_pairs={{1,2},{2,1},{3,4},{4,3},{5,6},{6,5},{7,8},{8,7},{9,10},{10,9},{11,... | collective-permute-start | bytes 5013512 | tf_op jit(solution)/shard_map/ppermute | solution.py:22
  45.1 11.1 %collective-permute-start = (f32[2,8,16,384]{3,2,1,0:T(8,128)}, f32[2,8,16,384]{3,2,1,0:T(8,128)S(1)}, u32[]{:S(2)}, u32[]{:S(2)}) collective-permute-start(f32[2,8,16,384]{3,2,1,0:T(8,128)} %get-tuple-element.34), channel_id=1, source_target_pairs={{0,32},{32,0},{64,96},{96,64},{1,33},{33,1},{65,97},{97,65},{2,34}... | collective-permute-start | bytes 1179656 | tf_op jit(solution)/shard_map/ppermute | solution.py:27
  46.9 9.2 %copy-start = (f32[2,8,16,384]{3,2,1,0:T(8,128)S(1)}, f32[2,8,16,384]{3,2,1,0:T(8,128)}, u32[]{:S(2)}) copy-start(f32[2,8,16,384]{3,2,1,0:T(8,128)} %get-tuple-element.33.own_ref) | copy-start | bytes 1179652
  55.5 18.3 %copy-start.7 = (s32[32,1,128]{2,1,0:T(1,128)S(1)}, s32[32,1,128]{2,1,0:T(1,128)}, u32[]{:S(2)}) copy-start(s32[32,1,128]{2,1,0:T(1,128)} %get-tuple-element.32) | copy-start | bytes 49156
  55.5 2.6 %collective-permute-start.4 = (f32[2,12,8,384]{3,2,1,0:T(8,128)}, f32[2,12,8,384]{3,2,1,0:T(8,128)S(1)}, u32[]{:S(2)}, u32[]{:S(2)}) collective-permute-start(f32[2,12,8,384]{3,2,1,0:T(8,128)} %get-tuple-element.40), channel_id=1, source_target_pairs={{0,32},{32,0},{64,96},{96,64},{1,33},{33,1},{65,97},{97,65},{2,34}... | collective-permute-start | bytes 884744 | tf_op jit(solution)/shard_map/ppermute | solution.py:27
  56.1 10.3 %copy-start.1 = (f32[2,8,16,384]{3,2,1,0:T(8,128)}, f32[2,8,16,384]{3,2,1,0:T(8,128)S(1)}, u32[]{:S(2)}) copy-start(f32[2,8,16,384]{3,2,1,0:T(8,128)S(1)} %collective-permute-done.got_ref) | copy-start | bytes 1179652
  56.2 7.9 %collective-permute-start.1 = (f32[8,16,384]{2,1,0:T(8,128)S(1)}, f32[8,16,384]{2,1,0:T(8,128)S(1)}, u32[]{:S(2)}, u32[]{:S(2)}) collective-permute-start(f32[8,16,384]{2,1,0:T(8,128)S(1)} %fusion), channel_id=1, source_target_pairs={{0,64},{32,96},{64,0},{96,32},{1,65},{33,97},{65,1},{97,33},{2,66}... | collective-permute-start | bytes 589832 | tf_op jit(solution)/shard_map/ppermute | solution.py:27
  58.2 8.3 %copy-start.2 = (f32[2,12,8,384]{3,2,1,0:T(8,128)}, f32[2,12,8,384]{3,2,1,0:T(8,128)S(1)}, u32[]{:S(2)}) copy-start(f32[2,12,8,384]{3,2,1,0:T(8,128)S(1)} %collective-permute-done.4.cross_got_ref) | copy-start | bytes 884740
  59.2 7.3 %collective-permute-start.5 = (f32[12,8,384]{2,1,0:T(8,128)S(1)}, f32[12,8,384]{2,1,0:T(8,128)S(1)}, u32[]{:S(2)}, u32[]{:S(2)}) collective-permute-start(f32[12,8,384]{2,1,0:T(8,128)S(1)} %fusion.1), channel_id=1, source_target_pairs={{0,64},{32,96},{64,0},{96,32},{1,65},{33,97},{65,1},{97,33},{2,66}... | collective-permute-start | bytes 442376 | tf_op jit(solution)/shard_map/ppermute | solution.py:27
  64.0 2.5 %copy-start.3 = (f32[8,16,384]{2,1,0:T(8,128)}, f32[8,16,384]{2,1,0:T(8,128)S(1)}, u32[]{:S(2)}) copy-start(f32[8,16,384]{2,1,0:T(8,128)S(1)} %collective-permute-done.1.last_ref) | copy-start | bytes 589828
  66.5 0.7 copy-start.4
  69.1 30.1 %collective-permute-start.6 = (f32[3,8,384]{2,1,0:T(8,128)}, f32[3,8,384]{2,1,0:T(8,128)S(1)}, u32[]{:S(2)}, u32[]{:S(2)}) collective-permute-start(f32[3,8,384]{2,1,0:T(8,128)} %get-tuple-element.41), channel_id=1, source_target_pairs={{0,1},{1,0},{2,3},{3,2},{4,5},{5,4},{6,7},{7,6},{8,9},{9,8},{10,11... | collective-permute-start | bytes 110600 | tf_op jit(solution)/shard_map/ppermute | solution.py:22
  73.1 26.1 %collective-permute-start.7 = (f32[3,8,384]{2,1,0:T(8,128)}, f32[3,8,384]{2,1,0:T(8,128)S(1)}, u32[]{:S(2)}, u32[]{:S(2)}) collective-permute-start(f32[3,8,384]{2,1,0:T(8,128)} %get-tuple-element.42), channel_id=1, source_target_pairs={{1,2},{2,1},{3,4},{4,3},{5,6},{6,5},{7,8},{8,7},{9,10},{10,9},{11,... | collective-permute-start | bytes 110600 | tf_op jit(solution)/shard_map/ppermute | solution.py:22
  99.2 0.6 copy-start.5
  99.8 0.6 copy-start.6
